TPU v7x, 32 devices: a whole 2x2x4 slice. The times are simulated.
32 devices in a mesh: local: 4 (over y, x), dp: 8 (over z, core).
Axes of the slice: x: 2, y: 2, z: 4, core: 2. Of those that a mesh axis runs over, the one named last changes fastest.
Arguments:
- gradient: bfloat16 [32, 72, 7168], P(('local', 'dp')), may hold values from -1.1953125 to 1.1953125
- feedback: bfloat16 [32, 72, 7168], P(('local', 'dp')), may hold values from -0.59765625 to 0.59765625
- basis_in: float32 [7168, 32], replicated, may hold values from -6 to 6
Outputs:
- new_feedback: bfloat16 [32, 72, 7168], P(('local', 'dp'))
- new_basis: float32 [7168, 32], replicated
All inputs are finite; a program needn't handle non-finite values.
Results may differ from a plain program's by a relative error of at most 0.001.
Values sent between devices are 32-bit elements; how exact they have to be, the bound alone decides.
No kernel may reach another device: no remote copies, remote signals or barrier semaphores. Data moves between devices by JAX's collectives and lax.ppermute only.
A program may use at most 64 MiB of HBM per device.

v0:
```python
import jax
import jax.numpy as jnp
from jax import lax
from jax.sharding import PartitionSpec as P

epsilon = 1e-06


def orthonormal(matrix):
    highest = lax.Precision.HIGHEST
    count = matrix.shape[1]
    positions = jnp.arange(count, dtype=jnp.int32)

    def sweep(index, working):
        vector = lax.dynamic_slice_in_dim(working, index, 1, 1)[:, 0]
        vector = vector * lax.rsqrt(jnp.sum(vector * vector) + epsilon)
        projections = jnp.dot(vector, working, precision=highest)
        projections = jnp.where(positions > index, projections, jnp.zeros_like(projections))
        working = working - vector[:, None] * projections[None, :]
        return lax.dynamic_update_slice_in_dim(working, vector[:, None], index, 1)

    return lax.fori_loop(0, count, sweep, matrix)


def body(gradient, feedback, basis_in):
    highest = lax.Precision.HIGHEST
    merged = gradient[0].astype(jnp.float32) + feedback[0].astype(jnp.float32)
    workers = lax.axis_size("local") * lax.axis_size("dp")
    left_term = jnp.dot(merged, basis_in, precision=highest)
    left_sum = lax.psum(left_term, ("local", "dp"))
    left_basis = orthonormal(left_sum)
    right_term = jnp.dot(merged.T, left_basis, precision=highest)
    share_rows = lax.psum_scatter(right_term, "local", scatter_dimension=0, tiled=True)
    share_rows = lax.psum(share_rows, "dp")
    new_basis = lax.all_gather(share_rows, "local", axis=0, tiled=True)
    approx = jnp.dot(left_basis, new_basis.T, precision=highest) / workers
    new_feedback = (merged - approx).astype(jnp.bfloat16)
    return (new_feedback[None], new_basis)


def solution(mesh):
    return jax.shard_map(
        body,
        mesh=mesh,
        in_specs=(P(("local", "dp"), None, None), P(("local", "dp"), None, None), P()),
        out_specs=(P(("local", "dp"), None, None), P()),
        check_vma=False,
    )
```

profile of v0, /device:TPU:0, one launch (start us, length us, event | category | flops | bytes accessed | tf_op | source)
XLA Modules:
  0.0 214.8 jit_solution(16565798836019193358)
XLA Ops:
  7.2 1.1 copy-done
  8.3 3.4 %fusion.8 = f32[72,32]{0,1:T(8,128)S(1)} fusion(f32[7168,32]{0,1:T(8,128)S(1)} %copy-done, bf16[1,72,7168]{2,1,0:T(8,128)(2,1)} %param.6, bf16[1,72,7168]{2,1,0:T(8,128)(2,1)} %param.5), kind=kOutput, calls=%fused_computation.13 | convolution fusion | flops 199729152 | bytes 2991104 | tf_op jit(solution)/shard_map/dot_general | solution.py:29
  11.7 42.1 %psum.14 = f32[72,32]{0,1:T(8,128)S(1)} all-reduce(f32[72,32]{0,1:T(8,128)S(1)} %fusion.8), channel_id=1, replica_groups=mesh['local'=4,'dp'=8] {'local','dp'}, use_global_device_ids=true, to_apply=%region_0.0 | all-reduce | flops 2304 | bytes 18432 | tf_op jit(solution)/shard_map/psum | solution.py:30
  53.8 50.7 %while.14 = (s32[]{:T(128)}, f32[72,32]{0,1:T(8,128)S(1)}, s32[]{:T(128)}, f32[]{:T(128)}, s32[]{:T(128)}) while((s32[]{:T(128)}, f32[72,32]{0,1:T(8,128)S(1)}, s32[]{:T(128)}, f32[]{:T(128)}, s32[]{:T(128)}) %tuple.35), condition=%wide.region_3.4_spmd.clone, body=%wide.region_1.3_spmd.clone.sunk | while | flops 32610 | bytes 30609 | solution.py:22
  53.8 0.6 multiply_reduce_fusion.2
  55.1 0.1 fusion.23
  55.4 0.6 multiply_reduce_fusion.2
  56.7 0.1 fusion.23
  57.0 0.6 multiply_reduce_fusion.2
  58.3 0.1 fusion.23
  58.6 0.6 multiply_reduce_fusion.2
  60.1 0.6 multiply_reduce_fusion.2
  61.5 0.1 fusion.23
  61.7 0.6 multiply_reduce_fusion.2
  63.3 0.6 multiply_reduce_fusion.2
  64.9 0.6 multiply_reduce_fusion.2
  66.5 0.6 multiply_reduce_fusion.2
  68.1 0.6 multiply_reduce_fusion.2
  69.6 0.6 multiply_reduce_fusion.2
  71.2 0.6 multiply_reduce_fusion.2
  72.8 0.6 multiply_reduce_fusion.2
  74.4 0.6 multiply_reduce_fusion.2
  76.0 0.6 multiply_reduce_fusion.2
  77.6 0.6 multiply_reduce_fusion.2
  78.9 0.1 fusion.23
  79.2 0.6 multiply_reduce_fusion.2
  80.7 0.6 multiply_reduce_fusion.2
  82.3 0.6 multiply_reduce_fusion.2
  83.9 0.6 multiply_reduce_fusion.2
  85.5 0.6 multiply_reduce_fusion.2
  87.1 0.6 multiply_reduce_fusion.2
  88.7 0.6 multiply_reduce_fusion.2
  90.0 0.1 fusion.23
  90.2 0.6 multiply_reduce_fusion.2
  91.8 0.6 multiply_reduce_fusion.2
  93.4 0.6 multiply_reduce_fusion.2
  95.0 0.6 multiply_reduce_fusion.2
  96.6 0.6 multiply_reduce_fusion.2
  98.2 0.6 multiply_reduce_fusion.2
  99.8 0.6 multiply_reduce_fusion.2
  101.3 0.6 multiply_reduce_fusion.2
  102.9 0.6 multiply_reduce_fusion.2
  104.5 2.4 %fusion.6 = f32[7168,32]{0,1:T(8,128)} fusion(f32[72,32]{0,1:T(8,128)S(1)} %get-tuple-element.66, bf16[1,72,7168]{2,1,0:T(8,128)(2,1)S(1)} %copy-done.1, bf16[1,72,7168]{2,1,0:T(8,128)(2,1)S(1)} %copy-done.2), kind=kOutput, calls=%fused_computation.11 | convolution fusion | flops 199729152 | bytes 2991104 | tf_op jit(solution)/shard_map/dot_general | solution.py:32
  107.0 27.0 %reduce-scatter.2.cloned.1.call-done = f32[1792,32]{0,1:T(8,128)} async-done(((f32[7168,32]{0,1:T(8,128)}), f32[1792,32]{0,1:T(8,128)}) %reduce-scatter.2.cloned.1.call-update) | async-done | bytes 229392 | tf_op jit(solution)/shard_map/reduce_scatter | solution.py:33
  134.1 55.3 %all-reduce.2.cloned.1.call-done = f32[1792,32]{0,1:T(8,128)} async-done(((f32[1792,32]{0,1:T(8,128)}), f32[1792,32]{0,1:T(8,128)}) %all-reduce.2.cloned.1.call-update) | async-done | bytes 229392 | tf_op jit(solution)/shard_map/psum | solution.py:34
  189.4 14.7 %all_gather.3 = f32[7168,32]{0,1:T(8,128)S(1)} all-gather(f32[1792,32]{0,1:T(8,128)} %all-reduce.2.cloned.1.call-done), channel_id=1, replica_groups=mesh['local'=4,'dp'=8] {'local'}, dimensions={0}, use_global_device_ids=true | all-gather | bytes 1146880 | tf_op jit(solution)/shard_map/all_gather | solution.py:35
  204.1 2.9 %fusion.5 = bf16[1,72,7168]{2,1,0:T(8,128)(2,1)} fusion(f32[72,32]{0,1:T(8,128)S(1)} %get-tuple-element.66, f32[7168,32]{0,1:T(8,128)S(1)} %all_gather.3, bf16[1,72,7168]{2,1,0:T(8,128)(2,1)S(1)} %copy-done.1, bf16[1,72,7168]{2,1,0:T(8,128)(2,1)S(1)} %copy-done.2), kind=kOutput, calls=%fused_computation.10 | convolution fusion | flops 201277440 | bytes 4023296 | tf_op jit(solution)/shard_map/dot_general | solution.py:36
  207.0 0.9 copy.14
  (163 shorter events, 7.8 us)
Async XLA Ops:
  7.2 1.2 copy-start
  7.2 97.3 %copy-start.2 = (bf16[1,72,7168]{2,1,0:T(8,128)(2,1)S(1)}, bf16[1,72,7168]{2,1,0:T(8,128)(2,1)}, u32[]{:S(2)}) copy-start(bf16[1,72,7168]{2,1,0:T(8,128)(2,1)} %param.5) | copy-start | bytes 3096580
  7.2 97.3 %copy-start.1 = (bf16[1,72,7168]{2,1,0:T(8,128)(2,1)S(1)}, bf16[1,72,7168]{2,1,0:T(8,128)(2,1)}, u32[]{:S(2)}) copy-start(bf16[1,72,7168]{2,1,0:T(8,128)(2,1)} %param.6) | copy-start | bytes 3096580
  7.2 126.8 %reduce-scatter.2.cloned.1.call-start = ((), (), s32[]{:S(2)}) async-start(), calls=%async_computation.1 | async-start | bytes 1146880 | tf_op jit(solution)/shard_map/reduce_scatter | solution.py:33
  107.0 82.4 %all-reduce.2.cloned.1.call-start = ((), (), s32[]{:S(2)}) async-start(), calls=%async_computation.2 | async-start | bytes 458752 | tf_op jit(solution)/shard_map/psum | solution.py:34
Sparse Core Ops, SparseCore 0:
  107.1 26.8 reduce-scatter.1
  136.4 52.9 all-reduce.1
where the time goes:
time: 215 us
  waiting for transfers between devices  82.3 us (38%)
  blocking collectives  56.8 us (26%)
  other arithmetic  22.9 us (11%)
  loops' own time  22.8 us (11%)
  between operations  14.1 us (7%)
  matrix products  12.9 us (6%)
  local copies, waits for them, and re-layouts  2.95 us (1%)
    psum x1, waiting for transfers between devices, body(): share_rows = lax.psum(share_rows, 'dp')  55.3 us
    psum x1, blocking collectives, body(): left_sum = lax.psum(left_term, ('local', 'dp'))  42.1 us
    reduce_scatter x1, waiting for transfers between devices, body(): lax.psum_scatter(right_term, 'local', scatter_dimension=0, tiled=True)  27 us
    another operation x1, loops' own time, orthonormal(): return lax.fori_loop(0, count, sweep, matrix)  22.8 us
    reduce_sum x32, other arithmetic, sweep(): vector = vector * lax.rsqrt(jnp.sum(vector * vector) + epsilon)  19.4 us
    all_gather x1, blocking collectives, body(): new_basis = lax.all_gather(share_rows, 'local', axis=0, tiled=True)  14.7 us
  transfers between devices with their start and end apart: 2, of which 2 were waited for; matrix products, arithmetic and copies ran while one was open for 0% of the time, Pallas kernels for 0%

commit v1 on v0

v1 whole, which is shorter than its diff:
```python
import functools

import jax
import jax.numpy as jnp
from jax import lax
from jax.experimental import pallas as pl
from jax.experimental.pallas import tpu as pltpu
from jax.sharding import PartitionSpec as P

epsilon = 1e-06
AXES = ("local", "dp")
F32, BF16 = jnp.float32, jnp.bfloat16
VMEM = pltpu.VMEM


def call(kernel, outs, *args, flops=1 << 20, limit=12, scratch=()):
    spec = pl.BlockSpec(memory_space=VMEM)
    many = isinstance(outs, list)
    shapes = [jax.ShapeDtypeStruct(s, d) for s, d in (outs if many else [outs])]
    size = sum(a.size * a.dtype.itemsize for a in args)
    result = pl.pallas_call(
        kernel,
        out_shape=shapes,
        in_specs=[spec] * len(args),
        out_specs=[spec] * len(shapes),
        scratch_shapes=scratch,
        compiler_params=pltpu.CompilerParams(vmem_limit_bytes=limit << 20),
        cost_estimate=pl.CostEstimate(flops=flops, bytes_accessed=size, transcendentals=0),
    )(*args)
    return result if many else result[0]


def split(value):
    high = value.astype(BF16)
    return high, (value - high.astype(F32)).astype(BF16)


def send_kernel(g, f, out):
    half = out.shape[1]
    other = 1 - lax.rem(lax.axis_index("dp"), 2)
    span = pl.ds(pl.multiple_of(other * half, 128), half)
    out[...] = g[:, span].astype(F32) + f[:, span].astype(F32)


def left_kernel(g, f, b, out):
    rank = b.shape[0]
    high, low = split(b[...])
    pieces = jnp.concatenate([high, low], axis=0)
    dims = (((1,), (1,)), ((), ()))
    both = lax.dot_general(pieces, g[...], dims, preferred_element_type=F32)
    both += lax.dot_general(pieces, f[...], dims, preferred_element_type=F32)
    out[...] = both[:rank] + both[rank:]


def pair_kernel(g, f, got, *outs):
    width = outs[0].shape[1]
    half = got.shape[1]
    core = lax.rem(lax.axis_index("dp"), 2)
    mine = lax.axis_index("local")
    for step, out in enumerate(outs):
        chunk = partner(mine, step, len(outs))
        inner = pl.ds(pl.multiple_of(chunk * width, 128), width)
        span = pl.ds(pl.multiple_of(core * half + chunk * width, 128), width)
        out[...] = g[:, span].astype(F32) + f[:, span].astype(F32) + got[:, inner]


def partner(index, step, size):
    if size & (size - 1):
        return lax.rem(index + step, size)
    return jnp.bitwise_xor(index, step)


def gram_schmidt_kernel(block, a, b, basis, basis_t):
    rank, rows = a.shape
    lanes = 128
    total = jnp.concatenate([a[...] + b[...], jnp.zeros((lanes - rank, rows), F32)], axis=0)
    work = total.T
    lane = lax.broadcasted_iota(jnp.int32, (rows, lanes), 1)
    done = jnp.zeros((rows, lanes), F32)
    for start in range(0, rank, block):
        count = min(block, rank - start)
        columns = [jnp.broadcast_to(work[:, start + i : start + i + 1], (rows, lanes)) for i in range(count)]
        for i in range(count):
            column = columns[i]
            scale = lax.rsqrt(jnp.sum(column * column, axis=0, keepdims=True) + epsilon)
            unit = column * scale
            for k in range(i + 1, count):
                dot = jnp.sum(column * columns[k], axis=0, keepdims=True) * scale
                columns[k] = columns[k] - unit * dot
            dots = jnp.sum(column * work, axis=0, keepdims=True) * scale
            work = work - unit * dots
            done = jnp.where(lane == start + i, unit, done)
    basis[...] = done[:, :rank]
    basis_t[...] = done.T[:rank]


def right_kernel(basis_t, *refs):
    *terms, out = refs
    total = terms[0][...]
    for term in terms[1:]:
        total = total + term[...]
    out[...] = jnp.dot(basis_t[...], total, precision=lax.Precision.HIGHEST, preferred_element_type=F32)


def final_kernel(workers, g, f, basis, own, other, feedback, new_basis_t):
    chunks, rank, width = own.shape
    core = lax.rem(lax.axis_index("dp"), 2)
    high, low = split(basis[...] * (1.0 / workers))
    left = jnp.concatenate([high, low, high], axis=1)

    for part in range(2 * chunks):
        mine = core == part // chunks
        piece = jnp.where(mine, own[part % chunks], other[part % chunks])
        span = pl.ds(part * width, width)
        new_basis_t[:, span] = piece
        upper, lower = split(piece)
        right = jnp.concatenate([upper, upper, lower], axis=0)
        approx = jnp.dot(left, right, preferred_element_type=F32)
        feedback[:, span] = (g[:, span].astype(F32) + f[:, span].astype(F32) - approx).astype(BF16)


def body(gradient, feedback, basis_in):
    g, f = gradient[0], feedback[0]
    rows, columns = g.shape
    basis_t_in = basis_in.T
    rank = basis_t_in.shape[0]
    local, dp = lax.axis_size("local"), lax.axis_size("dp")
    groups = dp // 2
    half = columns // 2
    width = half // local

    def swap(value, axis, step, size, stride=1):
        pairs = []
        for source in range(lax.axis_size(axis)):
            place = source // stride % size
            if size & (size - 1):
                to = (place - step) % size
            else:
                to = place ^ step
            pairs.append((source, source + (to - place) * stride))
        return lax.ppermute(value, axis, pairs)

    def total_over(value, axis, size, stride):
        other = jnp.zeros_like(value)
        step = 1
        first = True
        while step < size:
            value = value if first else value + other
            other = swap(value, axis, step, size, stride)
            first = False
            step *= 2
        return value, other

    outgoing = call(send_kernel, ((rows, half), F32), g, f)
    got = swap(outgoing, "dp", 1, 2)
    left = call(left_kernel, ((rank, rows), F32), g, f, basis_t_in, flops=1 << 28)
    a, b = total_over(left, "local", local, 1)
    left = a + b
    got, left = lax.optimization_barrier((got, left))
    chunks = call(pair_kernel, [((rows, width), F32)] * local, g, f, got)
    terms = [chunks[0]] + [swap(chunks[s], "local", s, local) for s in range(1, local)]
    a, b = total_over(left, "dp", groups, 2)
    left = a + b
    a, b = left, swap(left, "dp", 1, 2)
    basis, basis_t = call(
        functools.partial(gram_schmidt_kernel, 4), [((rows, rank), F32), ((rank, rows), F32)], a, b, flops=1 << 24
    )
    right = call(right_kernel, ((rank, width), F32), basis_t, *terms)
    a, b = total_over(right, "dp", groups, 2)
    right = a + b
    own = lax.all_gather(right, "local", axis=0)
    other = swap(own, "dp", 1, 2)
    new_feedback, new_basis_t = call(
        functools.partial(final_kernel, local * dp),
        [((rows, columns), BF16), ((rank, columns), F32)],
        g, f, basis, own, other,
    )
    return (new_feedback[None], new_basis_t.T)


def solution(mesh):
    return jax.shard_map(
        body,
        mesh=mesh,
        in_specs=(P(("local", "dp"), None, None), P(("local", "dp"), None, None), P()),
        out_specs=(P(("local", "dp"), None, None), P()),
        check_vma=False,
    )
```

time: 215 us -> 56.7 us (0.26)
  waiting for transfers between devices: 82.3 us -> 18.5 us
  blocking collectives: 56.8 us -> 10.4 us
  other arithmetic: 22.9 us -> 0.05 us
  loops' own time: 22.8 us -> 0 us
  starting transfers between devices: 0.08 us -> 19 us
  between operations: 14.1 us -> 0.71 us
  matrix products: 12.9 us -> 0 us
  Pallas kernels: 0 us -> 4.81 us
    psum x1 -> x0, waiting for transfers between devices: 55.3 us -> none  [body(): share_rows = lax.psum(share_rows, 'dp')]
    psum x1 -> x0, blocking collectives: 42.1 us -> none  [body(): left_sum = lax.psum(left_term, ('local', 'dp'))]
    reduce_scatter x1 -> x0, waiting for transfers between devices: 27 us -> none  [body(): lax.psum_scatter(right_term, 'local', scatter_dimension=0, tiled=True)]
    another operation x1 -> x0, loops' own time: 22.8 us -> none  [orthonormal(): return lax.fori_loop(0, count, sweep, matrix)]
    reduce_sum x32 -> x0, other arithmetic: 19.4 us -> none  [sweep(): vector = vector * lax.rsqrt(jnp.sum(vector * vector) + epsilon)]
    ppermute x0 -> x12, starting transfers between devices: none -> 19 us  [swap(): return lax.ppermute(value, axis, pairs)]
    ppermute x0 -> x12, waiting for transfers between devices: none -> 18.5 us  [swap(): return lax.ppermute(value, axis, pairs)]
    dot_general x35 -> x0, matrix products: 12.9 us -> none  [the longest x32 4.11 us: sweep(): projections = jnp.dot(vector, working, precision=highest)]
  transfers between devices with their start and end apart: 2 -> 12, of which waited for: 2 -> 8; matrix products, arithmetic and copies ran while one was open for 0% -> 0% of each run, Pallas kernels for 0% -> 4%
where the time goes in v1:
time: 56.7 us; the launch traced here: 56.4 us
  starting transfers between devices  19 us (34%)
  waiting for transfers between devices  18.5 us (33%)
  blocking collectives  10.4 us (18%)
  Pallas kernels  4.81 us (8%)
  local copies, waits for them, and re-layouts  2.96 us (5%)
  between operations  0.71 us (1%)
    ppermute x12, starting transfers between devices, swap(): return lax.ppermute(value, axis, pairs)  19 us
    ppermute x12, waiting for transfers between devices, swap(): return lax.ppermute(value, axis, pairs)  18.5 us
    all_gather x1, blocking collectives, body(): own = lax.all_gather(right, 'local', axis=0)  10.4 us
    pallas_call x6, Pallas kernels, call(): pl.pallas_call(kernel, out_shape=shapes, in_specs=[spec] * len(args), out...  4.81 us
    unnamed x10, local copies, waits for them, and re-layouts  2.96 us
  transfers between devices with their start and end apart: 12, of which 8 were waited for; matrix products, arithmetic and copies ran while one was open for 0% of the time, Pallas kernels for 4%

profile of v1, /device:TPU:0, one launch (start us, length us, event | category | flops | bytes accessed | tf_op | source)
XLA Modules:
  0.0 56.4 jit_solution(3828956165547564541)
XLA Ops:
  0.6 0.0 copy-start
  0.6 1.2 %copy-done = bf16[1,72,7168]{2,1,0:T(8,128)(2,1)S(1)} copy-done((bf16[1,72,7168]{2,1,0:T(8,128)(2,1)S(1)}, bf16[1,72,7168]{2,1,0:T(8,128)(2,1)}, u32[]{:S(2)}) %copy-start) | copy-done | bytes 1032216
  1.9 0.0 copy-start.2
  1.9 1.2 %copy-done.2 = bf16[1,72,7168]{2,1,0:T(8,128)(2,1)S(1)} copy-done((bf16[1,72,7168]{2,1,0:T(8,128)(2,1)S(1)}, bf16[1,72,7168]{2,1,0:T(8,128)(2,1)}, u32[]{:S(2)}) %copy-start.2) | copy-done | bytes 1032216
  3.1 0.0 copy-start.4
  3.1 0.1 shard_map.50
  3.2 0.6 collective-permute-start
  3.7 0.5 copy-done.4
  4.3 0.7 %shard_map.51 = f32[32,72]{1,0:T(8,128)S(1)} custom-call(bf16[72,7168]{1,0:T(8,128)(2,1)S(1)} %bitcast.7, bf16[72,7168]{1,0:T(8,128)(2,1)S(1)} %bitcast.11, f32[32,7168]{1,0:T(8,128)S(1)} %bitcast.16), custom_call_target="tpu_custom_call" | custom-call | flops 268435456 | bytes 2981888 | tf_op jit(solution)/shard_map/pallas_call | solution.py:21
  5.0 3.0 %collective-permute-start.1 = (f32[32,72]{1,0:T(8,128)S(1)}, f32[32,72]{1,0:T(8,128)S(1)}, u32[]{:S(2)}, u32[]{:S(2)}) collective-permute-start(f32[32,72]{1,0:T(8,128)S(1)} %shard_map.51), channel_id=1, source_target_pairs={{0,8},{8,0},{16,24},{24,16},{1,9},{9,1},{17,25},{25,17},{2,10},{10... | collective-permute-start | bytes 27656 | tf_op jit(solution)/shard_map/ppermute | solution.py:141
  8.0 1.7 %collective-permute-done.1 = f32[32,72]{1,0:T(8,128)S(1)} collective-permute-done((f32[32,72]{1,0:T(8,128)S(1)}, f32[32,72]{1,0:T(8,128)S(1)}, u32[]{:S(2)}, u32[]{:S(2)}) %collective-permute-start.1) | collective-permute-done | bytes 9248 | tf_op jit(solution)/shard_map/ppermute | solution.py:141
  9.7 2.1 %collective-permute-start.2 = (f32[32,72]{1,0:T(8,128)S(1)}, f32[32,72]{1,0:T(8,128)S(1)}, u32[]{:S(2)}, u32[]{:S(2)}) collective-permute-start(f32[32,72]{1,0:T(8,128)S(1)} %add.18), channel_id=1, source_target_pairs={{0,16},{8,24},{16,0},{24,8},{1,17},{9,25},{17,1},{25,9},{2,18},{10... | collective-permute-start | bytes 27656 | tf_op jit(solution)/shard_map/ppermute | solution.py:141
  11.7 1.7 %collective-permute-done.2 = f32[32,72]{1,0:T(8,128)S(1)} collective-permute-done((f32[32,72]{1,0:T(8,128)S(1)}, f32[32,72]{1,0:T(8,128)S(1)}, u32[]{:S(2)}, u32[]{:S(2)}) %collective-permute-start.2) | collective-permute-done | bytes 9248 | tf_op jit(solution)/shard_map/ppermute | solution.py:141
  13.5 0.0 collective-permute-done.got
  13.5 0.2 shard_map.53
  13.6 2.1 %collective-permute-start.6 = (f32[72,896]{1,0:T(8,128)S(1)}, f32[72,896]{1,0:T(8,128)S(1)}, u32[]{:S(2)}, u32[]{:S(2)}) collective-permute-start(f32[72,896]{1,0:T(8,128)S(1)} %get-tuple-element.17), channel_id=1, source_target_pairs={{0,8},{8,0},{16,24},{24,16},{1,9},{9,1},{17,25},{25,17},{2,10},{10... | collective-permute-start | bytes 774152 | tf_op jit(solution)/shard_map/ppermute | solution.py:141
  15.7 1.5 %collective-permute-start.7 = (f32[72,896]{1,0:T(8,128)S(1)}, f32[72,896]{1,0:T(8,128)S(1)}, u32[]{:S(2)}, u32[]{:S(2)}) collective-permute-start(f32[72,896]{1,0:T(8,128)S(1)} %get-tuple-element.18), channel_id=1, source_target_pairs={{0,16},{8,24},{16,0},{24,8},{1,17},{9,25},{17,1},{25,9},{2,18},{10... | collective-permute-start | bytes 774152 | tf_op jit(solution)/shard_map/ppermute | solution.py:141
  17.2 0.0 collective-permute-start.8
  17.2 2.0 %collective-permute-start.3 = (f32[32,72]{1,0:T(8,128)S(1)}, f32[32,72]{1,0:T(8,128)S(1)}, u32[]{:S(2)}, u32[]{:S(2)}) collective-permute-start(f32[32,72]{1,0:T(8,128)S(1)} %add.19), channel_id=1, source_target_pairs={{0,2},{1,3},{2,0},{3,1},{4,6},{5,7},{6,4},{7,5},{8,10},{9,11},{10,... | collective-permute-start | bytes 27656 | tf_op jit(solution)/shard_map/ppermute | solution.py:141
  19.3 1.7 %collective-permute-done.3 = f32[32,72]{1,0:T(8,128)S(1)} collective-permute-done((f32[32,72]{1,0:T(8,128)S(1)}, f32[32,72]{1,0:T(8,128)S(1)}, u32[]{:S(2)}, u32[]{:S(2)}) %collective-permute-start.3) | collective-permute-done | bytes 9248 | tf_op jit(solution)/shard_map/ppermute | solution.py:141
  21.0 3.0 %collective-permute-start.4 = (f32[32,72]{1,0:T(8,128)S(1)}, f32[32,72]{1,0:T(8,128)S(1)}, u32[]{:S(2)}, u32[]{:S(2)}) collective-permute-start(f32[32,72]{1,0:T(8,128)S(1)} %add.20), channel_id=1, source_target_pairs={{0,4},{1,5},{2,6},{3,7},{4,0},{5,1},{6,2},{7,3},{8,12},{9,13},{10,... | collective-permute-start | bytes 27656 | tf_op jit(solution)/shard_map/ppermute | solution.py:141
  24.0 1.7 %collective-permute-done.4 = f32[32,72]{1,0:T(8,128)S(1)} collective-permute-done((f32[32,72]{1,0:T(8,128)S(1)}, f32[32,72]{1,0:T(8,128)S(1)}, u32[]{:S(2)}, u32[]{:S(2)}) %collective-permute-start.4) | collective-permute-done | bytes 9248 | tf_op jit(solution)/shard_map/ppermute | solution.py:141
  25.8 0.0 collective-permute-start.5
  25.8 1.2 %collective-permute-done.5.b = f32[32,72]{1,0:T(8,128)S(1)} collective-permute-done((f32[32,72]{1,0:T(8,128)S(1)}, f32[32,72]{1,0:T(8,128)S(1)}, u32[]{:S(2)}, u32[]{:S(2)}) %collective-permute-start.5) | collective-permute-done | bytes 9248 | tf_op jit(solution)/shard_map/ppermute | solution.py:141
  26.9 1.7 %shard_map.52 = (f32[72,32]{1,0:T(8,128)S(1)}, f32[32,72]{1,0:T(8,128)S(1)}) custom-call(f32[32,72]{1,0:T(8,128)S(1)} %add.21.a, f32[32,72]{1,0:T(8,128)S(1)} %collective-permute-done.5.b), custom_call_target="tpu_custom_call" | custom-call | flops 16777216 | bytes 18432 | tf_op jit(solution)/shard_map/pallas_call | solution.py:21
  28.7 0.0 collective-permute-done.6.refs_1_
  28.7 0.0 collective-permute-done.7.refs_2_
  28.7 0.0 collective-permute-done.8.refs_3_
  28.7 0.0 copy-start.1
  28.7 0.0 copy-start.3
  28.7 0.3 shard_map.54
  29.1 1.9 %collective-permute-start.9 = (f32[32,896]{1,0:T(8,128)S(1)}, f32[32,896]{1,0:T(8,128)S(1)}, u32[]{:S(2)}, u32[]{:S(2)}) collective-permute-start(f32[32,896]{1,0:T(8,128)S(1)} %shard_map.54), channel_id=1, source_target_pairs={{0,2},{1,3},{2,0},{3,1},{4,6},{5,7},{6,4},{7,5},{8,10},{9,11},{10,... | collective-permute-start | bytes 344072 | tf_op jit(solution)/shard_map/ppermute | solution.py:141
  31.0 3.5 %collective-permute-done.9 = f32[32,896]{1,0:T(8,128)S(1)} collective-permute-done((f32[32,896]{1,0:T(8,128)S(1)}, f32[32,896]{1,0:T(8,128)S(1)}, u32[]{:S(2)}, u32[]{:S(2)}) %collective-permute-start.9) | collective-permute-done | bytes 114720 | tf_op jit(solution)/shard_map/ppermute | solution.py:141
  34.5 2.8 %collective-permute-start.10 = (f32[32,896]{1,0:T(8,128)S(1)}, f32[32,896]{1,0:T(8,128)S(1)}, u32[]{:S(2)}, u32[]{:S(2)}) collective-permute-start(f32[32,896]{1,0:T(8,128)S(1)} %add.22), channel_id=1, source_target_pairs={{0,4},{1,5},{2,6},{3,7},{4,0},{5,1},{6,2},{7,3},{8,12},{9,13},{10,... | collective-permute-start | bytes 344072 | tf_op jit(solution)/shard_map/ppermute | solution.py:141
  37.3 5.1 %collective-permute-done.10 = f32[32,896]{1,0:T(8,128)S(1)} collective-permute-done((f32[32,896]{1,0:T(8,128)S(1)}, f32[32,896]{1,0:T(8,128)S(1)}, u32[]{:S(2)}, u32[]{:S(2)}) %collective-permute-start.10) | collective-permute-done | bytes 114720 | tf_op jit(solution)/shard_map/ppermute | solution.py:141
  42.4 10.4 %all-gather = f32[128,896]{1,0:T(8,128)S(1)} all-gather(f32[32,896]{1,0:T(8,128)S(1)} %add.23), channel_id=2, replica_groups=mesh['local'=4,'dp'=8] {'local'}, dimensions={0}, use_global_device_ids=true | all-gather | bytes 573440 | tf_op jit(solution)/shard_map/all_gather | solution.py:171
  52.8 0.0 collective-permute-start.11
  52.8 1.8 %collective-permute-done.11.other = f32[4,32,896]{2,1,0:T(8,128)S(1)} collective-permute-done((f32[4,32,896]{2,1,0:T(8,128)S(1)}, f32[4,32,896]{2,1,0:T(8,128)S(1)}, u32[]{:S(2)}, u32[]{:S(2)}) %collective-permute-start.11) | collective-permute-done | bytes 458784 | tf_op jit(solution)/shard_map/ppermute | solution.py:141
  54.7 0.0 copy-done.1
  54.7 0.0 copy-done.3
  54.7 1.8 %shard_map.55 = (bf16[72,7168]{1,0:T(8,128)(2,1)}, f32[32,7168]{1,0:T(8,128)}) custom-call(bf16[72,7168]{1,0:T(8,128)(2,1)S(1)} %bitcast.9, bf16[72,7168]{1,0:T(8,128)(2,1)S(1)} %bitcast.13, f32[72,32]{1,0:T(8,128)S(1)} %get-tuple-element.13.basis, f32[4,32,896]{2,1,0:T(8,128)S(1)} %bitcast.15, f32[4,32,896]{2,1,0:T(8,128)S(1)} %collective-permute-done.11.other), custom_call_target="tpu_custom_call" | custom-call | flops 1048576 | bytes 2991104 | tf_op jit(solution)/shard_map/pallas_call | solution.py:21
  (6 shorter events, 0.0 us)
Async XLA Ops:
  0.6 1.2 %copy-start = (bf16[1,72,7168]{2,1,0:T(8,128)(2,1)S(1)}, bf16[1,72,7168]{2,1,0:T(8,128)(2,1)}, u32[]{:S(2)}) copy-start(bf16[1,72,7168]{2,1,0:T(8,128)(2,1)} %param.3) | copy-start | bytes 3096580
  1.9 1.2 %copy-start.2 = (bf16[1,72,7168]{2,1,0:T(8,128)(2,1)S(1)}, bf16[1,72,7168]{2,1,0:T(8,128)(2,1)}, u32[]{:S(2)}) copy-start(bf16[1,72,7168]{2,1,0:T(8,128)(2,1)} %param.4) | copy-start | bytes 3096580
  3.1 1.2 %copy-start.4 = (f32[7168,32]{0,1:T(8,128)S(1)}, f32[7168,32]{0,1:T(8,128)}, u32[]{:S(2)}) copy-start(f32[7168,32]{0,1:T(8,128)} %param.5) | copy-start | bytes 2752516
  3.2 10.3 %collective-permute-start = (f32[72,3584]{1,0:T(8,128)S(1)}, f32[72,3584]{1,0:T(8,128)S(1)}, u32[]{:S(2)}, u32[]{:S(2)}) collective-permute-start(f32[72,3584]{1,0:T(8,128)S(1)} %shard_map.50), channel_id=1, source_target_pairs={{0,1},{1,0},{2,3},{3,2},{4,5},{5,4},{6,7},{7,6},{8,9},{9,8},{10,11... | collective-permute-start | bytes 3096584 | tf_op jit(solution)/shard_map/ppermute | solution.py:141
  5.0 4.7 %collective-permute-start.1 = (f32[32,72]{1,0:T(8,128)S(1)}, f32[32,72]{1,0:T(8,128)S(1)}, u32[]{:S(2)}, u32[]{:S(2)}) collective-permute-start(f32[32,72]{1,0:T(8,128)S(1)} %shard_map.51), channel_id=1, source_target_pairs={{0,8},{8,0},{16,24},{24,16},{1,9},{9,1},{17,25},{25,17},{2,10},{10... | collective-permute-start | bytes 27656 | tf_op jit(solution)/shard_map/ppermute | solution.py:141
  9.7 3.8 %collective-permute-start.2 = (f32[32,72]{1,0:T(8,128)S(1)}, f32[32,72]{1,0:T(8,128)S(1)}, u32[]{:S(2)}, u32[]{:S(2)}) collective-permute-start(f32[32,72]{1,0:T(8,128)S(1)} %add.18), channel_id=1, source_target_pairs={{0,16},{8,24},{16,0},{24,8},{1,17},{9,25},{17,1},{25,9},{2,18},{10... | collective-permute-start | bytes 27656 | tf_op jit(solution)/shard_map/ppermute | solution.py:141
  13.6 15.0 %collective-permute-start.6 = (f32[72,896]{1,0:T(8,128)S(1)}, f32[72,896]{1,0:T(8,128)S(1)}, u32[]{:S(2)}, u32[]{:S(2)}) collective-permute-start(f32[72,896]{1,0:T(8,128)S(1)} %get-tuple-element.17), channel_id=1, source_target_pairs={{0,8},{8,0},{16,24},{24,16},{1,9},{9,1},{17,25},{25,17},{2,10},{10... | collective-permute-start | bytes 774152 | tf_op jit(solution)/shard_map/ppermute | solution.py:141
  15.7 13.0 %collective-permute-start.7 = (f32[72,896]{1,0:T(8,128)S(1)}, f32[72,896]{1,0:T(8,128)S(1)}, u32[]{:S(2)}, u32[]{:S(2)}) collective-permute-start(f32[72,896]{1,0:T(8,128)S(1)} %get-tuple-element.18), channel_id=1, source_target_pairs={{0,16},{8,24},{16,0},{24,8},{1,17},{9,25},{17,1},{25,9},{2,18},{10... | collective-permute-start | bytes 774152 | tf_op jit(solution)/shard_map/ppermute | solution.py:141
  17.2 11.5 %collective-permute-start.8 = (f32[72,896]{1,0:T(8,128)S(1)}, f32[72,896]{1,0:T(8,128)S(1)}, u32[]{:S(2)}, u32[]{:S(2)}) collective-permute-start(f32[72,896]{1,0:T(8,128)S(1)} %get-tuple-element.19), channel_id=1, source_target_pairs={{0,24},{8,16},{16,8},{24,0},{1,25},{9,17},{17,9},{25,1},{2,26},{10... | collective-permute-start | bytes 774152 | tf_op jit(solution)/shard_map/ppermute | solution.py:141
  17.2 3.8 %collective-permute-start.3 = (f32[32,72]{1,0:T(8,128)S(1)}, f32[32,72]{1,0:T(8,128)S(1)}, u32[]{:S(2)}, u32[]{:S(2)}) collective-permute-start(f32[32,72]{1,0:T(8,128)S(1)} %add.19), channel_id=1, source_target_pairs={{0,2},{1,3},{2,0},{3,1},{4,6},{5,7},{6,4},{7,5},{8,10},{9,11},{10,... | collective-permute-start | bytes 27656 | tf_op jit(solution)/shard_map/ppermute | solution.py:141
  21.0 4.8 %collective-permute-start.4 = (f32[32,72]{1,0:T(8,128)S(1)}, f32[32,72]{1,0:T(8,128)S(1)}, u32[]{:S(2)}, u32[]{:S(2)}) collective-permute-start(f32[32,72]{1,0:T(8,128)S(1)} %add.20), channel_id=1, source_target_pairs={{0,4},{1,5},{2,6},{3,7},{4,0},{5,1},{6,2},{7,3},{8,12},{9,13},{10,... | collective-permute-start | bytes 27656 | tf_op jit(solution)/shard_map/ppermute | solution.py:141
  25.8 1.2 %collective-permute-start.5 = (f32[32,72]{1,0:T(8,128)S(1)}, f32[32,72]{1,0:T(8,128)S(1)}, u32[]{:S(2)}, u32[]{:S(2)}) collective-permute-start(f32[32,72]{1,0:T(8,128)S(1)} %add.21.a), channel_id=1, source_target_pairs={{0,1},{1,0},{2,3},{3,2},{4,5},{5,4},{6,7},{7,6},{8,9},{9,8},{10,11... | collective-permute-start | bytes 27656 | tf_op jit(solution)/shard_map/ppermute | solution.py:141
  28.7 25.9 %copy-start.1 = (bf16[1,72,7168]{2,1,0:T(8,128)(2,1)S(1)}, bf16[1,72,7168]{2,1,0:T(8,128)(2,1)}, u32[]{:S(2)}) copy-start(bf16[1,72,7168]{2,1,0:T(8,128)(2,1)} %param.3) | copy-start | bytes 3096580
  28.7 25.9 %copy-start.3 = (bf16[1,72,7168]{2,1,0:T(8,128)(2,1)S(1)}, bf16[1,72,7168]{2,1,0:T(8,128)(2,1)}, u32[]{:S(2)}) copy-start(bf16[1,72,7168]{2,1,0:T(8,128)(2,1)} %param.4) | copy-start | bytes 3096580
  29.1 5.4 %collective-permute-start.9 = (f32[32,896]{1,0:T(8,128)S(1)}, f32[32,896]{1,0:T(8,128)S(1)}, u32[]{:S(2)}, u32[]{:S(2)}) collective-permute-start(f32[32,896]{1,0:T(8,128)S(1)} %shard_map.54), channel_id=1, source_target_pairs={{0,2},{1,3},{2,0},{3,1},{4,6},{5,7},{6,4},{7,5},{8,10},{9,11},{10,... | collective-permute-start | bytes 344072 | tf_op jit(solution)/shard_map/ppermute | solution.py:141
  34.5 7.9 %collective-permute-start.10 = (f32[32,896]{1,0:T(8,128)S(1)}, f32[32,896]{1,0:T(8,128)S(1)}, u32[]{:S(2)}, u32[]{:S(2)}) collective-permute-start(f32[32,896]{1,0:T(8,128)S(1)} %add.22), channel_id=1, source_target_pairs={{0,4},{1,5},{2,6},{3,7},{4,0},{5,1},{6,2},{7,3},{8,12},{9,13},{10,... | collective-permute-start | bytes 344072 | tf_op jit(solution)/shard_map/ppermute | solution.py:141
  52.8 1.8 %collective-permute-start.11 = (f32[4,32,896]{2,1,0:T(8,128)S(1)}, f32[4,32,896]{2,1,0:T(8,128)S(1)}, u32[]{:S(2)}, u32[]{:S(2)}) collective-permute-start(f32[4,32,896]{2,1,0:T(8,128)S(1)} %bitcast.14), channel_id=1, source_target_pairs={{0,1},{1,0},{2,3},{3,2},{4,5},{5,4},{6,7},{7,6},{8,9},{9,8},{10,11... | collective-permute-start | bytes 1376264 | tf_op jit(solution)/shard_map/ppermute | solution.py:141

commit v2 on v1

v2 whole, which is shorter than its diff:
```python
import functools

import jax
import jax.numpy as jnp
from jax import lax
from jax.experimental import pallas as pl
from jax.experimental.pallas import tpu as pltpu
from jax.sharding import PartitionSpec as P


epsilon = 1e-06
AXES = ("local", "dp")
F32, BF16 = jnp.float32, jnp.bfloat16
VMEM = pltpu.VMEM
PIECES = 4


def call(kernel, outs, *args, flops=1 << 20, limit=12, scratch=(), space=VMEM):
    many = isinstance(outs, list)
    shapes = [jax.ShapeDtypeStruct(s, d) for s, d in (outs if many else [outs])]
    size = sum(a.size * a.dtype.itemsize for a in args)
    result = pl.pallas_call(
        kernel,
        out_shape=shapes,
        in_specs=[pl.BlockSpec(memory_space=space)] * len(args),
        out_specs=[pl.BlockSpec(memory_space=VMEM)] * len(shapes),
        scratch_shapes=scratch,
        compiler_params=pltpu.CompilerParams(vmem_limit_bytes=limit << 20),
        cost_estimate=pl.CostEstimate(flops=flops, bytes_accessed=size, transcendentals=0),
    )(*args)
    return result if many else result[0]


def split(value):
    high = value.astype(BF16)
    return high, (value - high.astype(F32)).astype(BF16)


def partner(index, step, size):
    if size & (size - 1):
        return (index + step) % size
    return index ^ step


def odd_bits(index, size):
    total = 0
    while size > 1 and not size & (size - 1):
        total, index, size = total + index % 2, index // 2, size // 2
    return total % 2


def own_half():
    local, dp = lax.axis_size("local"), lax.axis_size("dp")
    place = lax.axis_index("dp")
    return (place % 2 + odd_bits(lax.axis_index("local"), local) + odd_bits(place // 2, dp // 2)) % 2


def left_kernel(g, f, b, left, merged, send, gv, fv, bv, sems):
    rank = b.shape[0]
    pieces = sems.shape[1]
    width = g.shape[1] // pieces
    half = own_half()
    spans, copies = [], []
    for i in range(pieces):
        piece = (half * (pieces // 2) + i + pieces // 2) % pieces
        span = pl.ds(pl.multiple_of(piece * width, 128), width)
        spans.append(span)
        for j, (source, target) in enumerate(((g, gv), (f, fv), (b, bv))):
            copy = pltpu.make_async_copy(source.at[:, span], target.at[:, span], sems.at[j, i])
            copy.start()
            copies.append(copy)
    dims = (((1,), (1,)), ((), ()))
    total = None
    for i, span in enumerate(spans):
        for copy in copies[3 * i : 3 * i + 3]:
            copy.wait()
        high, low = split(bv[:, span])
        basis = jnp.concatenate([high, low], axis=0)
        one, two = gv[:, span], fv[:, span]
        part = lax.dot_general(basis, one, dims, preferred_element_type=F32)
        part += lax.dot_general(basis, two, dims, preferred_element_type=F32)
        total = part if total is None else total + part
        both = one.astype(F32) + two.astype(F32)
        merged[:, span] = both
        if i < pieces // 2:
            send[:, i * width : (i + 1) * width] = both
    left[...] = total[:rank] + total[rank:]


def pair_kernel(merged, got, *outs):
    width = outs[0].shape[1]
    mine = lax.axis_index("local")
    start = own_half() * got.shape[1]
    for step, out in enumerate(outs):
        inner = pl.multiple_of(partner(mine, step, len(outs)) * width, 128)
        span = pl.ds(pl.multiple_of(start + inner, 128), width)
        out[...] = merged[:, span] + got[:, pl.ds(inner, width)]


def gram_schmidt_kernel(block, a, b, basis, basis_t):
    rank, rows = a.shape
    lanes = 128
    total = jnp.concatenate([a[...] + b[...], jnp.zeros((lanes - rank, rows), F32)], axis=0)
    work = total.T
    lane = lax.broadcasted_iota(jnp.int32, (rows, lanes), 1)
    done = jnp.zeros((rows, lanes), F32)
    for start in range(0, rank, block):
        count = min(block, rank - start)
        columns = [jnp.broadcast_to(work[:, start + i : start + i + 1], (rows, lanes)) for i in range(count)]
        for i in range(count):
            column = columns[i]
            scale = lax.rsqrt(jnp.sum(column * column, axis=0, keepdims=True) + epsilon)
            unit = column * scale
            for k in range(i + 1, count):
                dot = jnp.sum(column * columns[k], axis=0, keepdims=True) * scale
                columns[k] = columns[k] - unit * dot
            dots = jnp.sum(column * work, axis=0, keepdims=True) * scale
            work = work - unit * dots
            done = jnp.where(lane == start + i, unit, done)
    basis[...] = done[:, :rank]
    basis_t[...] = done.T[:rank]


def right_kernel(basis_t, *refs):
    *terms, out = refs
    total = terms[0][...]
    for term in terms[1:]:
        total = total + term[...]
    out[...] = jnp.dot(basis_t[...], total, precision=lax.Precision.HIGHEST, preferred_element_type=F32)


def final_kernel(workers, merged, basis, *refs):
    *blocks, feedback, new_basis_t = refs
    chunks = len(blocks) // 2
    width = blocks[0].shape[1]
    mine = lax.axis_index("local")
    half = own_half()
    high, low = split(basis[...] * (1.0 / workers))
    left = jnp.concatenate([high, low, high], axis=1)
    for i, block in enumerate(blocks):
        side = half if i < chunks else 1 - half
        start = (side * chunks + partner(mine, i % chunks, chunks)) * width
        span = pl.ds(pl.multiple_of(start, 128), width)
        piece = block[...]
        new_basis_t[:, span] = piece
        upper, lower = split(piece)
        right = jnp.concatenate([upper, upper, lower], axis=0)
        approx = jnp.dot(left, right, preferred_element_type=F32)
        feedback[:, span] = (merged[:, span] - approx).astype(BF16)


def body(gradient, feedback, basis_in):
    g, f = gradient[0], feedback[0]
    rows, columns = g.shape
    b = basis_in.T
    rank = b.shape[0]
    local, dp = lax.axis_size("local"), lax.axis_size("dp")
    groups = dp // 2
    half = columns // 2
    width = half // local

    def permute(value, along_local, step):
        pairs = []
        for x in range(local):
            for z in range(groups):
                to = (partner(x, step, local), z) if along_local else (x, partner(z, step, groups))
                flip = odd_bits(step, local if along_local else groups)
                for core in range(2):
                    pairs.append((x * dp + 2 * z + core, to[0] * dp + 2 * to[1] + (core ^ flip)))
        if partner(0, step, local if along_local else groups) != step:
            pairs = [(to, source) for source, to in pairs]
        return lax.ppermute(value, AXES, pairs)

    def swap(value):
        return lax.ppermute(value, AXES, [(i, i ^ 1) for i in range(local * dp)])

    def total_over(value, along_local):
        size = local if along_local else groups
        double = not size & (size - 1)
        first = value
        step = 1
        while step < size:
            other = permute(value if double else first, along_local, step)
            value = value + other
            step = 2 * step if double else step + 1
        return value

    pieces = PIECES if columns % (128 * PIECES) == 0 else 2
    g, f, b = (pltpu.with_memory_space_constraint(x, pltpu.HBM) for x in (g, f, b))
    left, merged, send = call(
        left_kernel, [((rank, rows), F32), ((rows, columns), F32), ((rows, half), F32)],
        g, f, b, flops=1 << 27, limit=16,
        scratch=[VMEM(g.shape, g.dtype), VMEM(f.shape, f.dtype), VMEM(b.shape, b.dtype),
                 pltpu.SemaphoreType.DMA((3, pieces))],
        space=pltpu.HBM,
    )
    got = swap(send)
    left = total_over(left, True)
    chunks = call(pair_kernel, [((rows, width), F32)] * local, merged, got)
    terms = [chunks[0]] + [permute(chunks[s], True, s) for s in range(1, local)]
    left = total_over(left, False)
    basis, basis_t = call(
        functools.partial(gram_schmidt_kernel, 4),
        [((rows, rank), F32), ((rank, rows), F32)],
        left, swap(left), flops=1 << 26,
    )
    right = call(right_kernel, ((rank, width), F32), basis_t, *terms, flops=1 << 25)
    own = total_over(right, False)
    blocks = [own] + [permute(own, True, s) for s in range(1, local)]
    blocks += [swap(block) for block in blocks]
    new_feedback, new_basis_t = call(
        functools.partial(final_kernel, local * dp),
        [((rows, columns), BF16), ((rank, columns), F32)],
        merged, basis, *blocks, flops=1 << 27, limit=16,
    )
    return (new_feedback[None], new_basis_t.T)


def solution(mesh):
    return jax.shard_map(
        body,
        mesh=mesh,
        in_specs=(P(("local", "dp"), None, None), P(("local", "dp"), None, None), P()),
        out_specs=(P(("local", "dp"), None, None), P()),
        check_vma=False,
    )
```

time: 56.7 us -> 61.3 us (1.081)
  waiting for transfers between devices: 18.5 us -> 32.8 us
  blocking collectives: 10.4 us -> 0 us
  local copies, waits for them, and re-layouts: 2.96 us -> 0 us
  starting transfers between devices: 19 us -> 20.9 us
  Pallas kernels: 4.81 us -> 6.69 us
    ppermute x12 -> x18, waiting for transfers between devices: 18.5 us -> 32.8 us  [the longest x12 28.5 us: permute(): return lax.ppermute(value, AXES, pairs)]
    all_gather x1 -> x0, blocking collectives: 10.4 us -> none  [body(): own = lax.all_gather(right, 'local', axis=0)]
    unnamed x10 -> x0, local copies, waits for them, and re-layouts: 2.96 us -> none
    pallas_call x6 -> x5, Pallas kernels: 4.81 us -> 6.69 us  [call(): pl.pallas_call(kernel, out_shape=shapes, in_specs=[pl.BlockSpec(memory_sp...]
    ppermute x12 -> x18, starting transfers between devices: 19 us -> 20.9 us  [the longest x12 19.7 us: permute(): return lax.ppermute(value, AXES, pairs)]
  transfers between devices with their start and end apart: 12 -> 18, of which waited for: 8 -> 12; matrix products, arithmetic and copies ran while one was open for 0% -> 0% of each run, Pallas kernels for 4% -> 3%
where the time goes in v2:
time: 61.3 us; the launch traced here: 61.1 us
  waiting for transfers between devices  32.8 us (54%)
  starting transfers between devices  20.9 us (34%)
  Pallas kernels  6.69 us (11%)
  between operations  0.68 us (1%)
    ppermute x12, waiting for transfers between devices, permute(): return lax.ppermute(value, AXES, pairs)  28.5 us
    ppermute x12, starting transfers between devices, permute(): return lax.ppermute(value, AXES, pairs)  19.7 us
    pallas_call x5, Pallas kernels, call(): pl.pallas_call(kernel, out_shape=shapes, in_specs=[pl.BlockSpec(memory_sp...  6.69 us
    ppermute x6, waiting for transfers between devices, swap(): return lax.ppermute(value, AXES, [(i, i ^ 1) for i in range(local * dp)])  4.33 us
  transfers between devices with their start and end apart: 18, of which 12 were waited for; matrix products, arithmetic and copies ran while one was open for 0% of the time, Pallas kernels for 3%

profile of v2, /device:TPU:0, one launch (start us, length us, event | category | flops | bytes accessed | tf_op | source)
XLA Modules:
  0.0 61.1 jit_solution(8005196452208137549)
XLA Ops:
  0.6 2.9 %shard_map.50 = (f32[32,72]{1,0:T(8,128)S(1)}, f32[72,7168]{1,0:T(8,128)S(1)}, f32[72,3584]{1,0:T(8,128)S(1)}) custom-call(bf16[72,7168]{1,0:T(8,128)(2,1)} %bitcast.5, bf16[72,7168]{1,0:T(8,128)(2,1)} %bitcast.6, f32[32,7168]{1,0:T(8,128)} %bitcast.7), custom_call_target="tpu_custom_call" | custom-call | flops 134217728 | bytes 2981888 | tf_op jit(solution)/shard_map/pallas_call | solution.py:22
  3.5 0.6 collective-permute-start.5
  4.1 2.3 %collective-permute-done.5.got = f32[72,3584]{1,0:T(8,128)S(1)} collective-permute-done((f32[72,3584]{1,0:T(8,128)S(1)}, f32[72,3584]{1,0:T(8,128)S(1)}, u32[]{:S(2)}, u32[]{:S(2)}) %collective-permute-start.5) | collective-permute-done | bytes 1032224 | tf_op jit(solution)/shard_map/ppermute | solution.py:175
  6.4 0.1 shard_map.52
  6.5 2.7 %collective-permute-start.6 = (f32[72,896]{1,0:T(8,128)S(1)}, f32[72,896]{1,0:T(8,128)S(1)}, u32[]{:S(2)}, u32[]{:S(2)}) collective-permute-start(f32[72,896]{1,0:T(8,128)S(1)} %get-tuple-element.19), channel_id=1, source_target_pairs={{0,9},{1,8},{2,11},{3,10},{4,13},{5,12},{6,15},{7,14},{8,1},{9,0},... | collective-permute-start | bytes 774152 | tf_op jit(solution)/shard_map/ppermute | solution.py:172
  9.1 1.5 %collective-permute-start.7 = (f32[72,896]{1,0:T(8,128)S(1)}, f32[72,896]{1,0:T(8,128)S(1)}, u32[]{:S(2)}, u32[]{:S(2)}) collective-permute-start(f32[72,896]{1,0:T(8,128)S(1)} %get-tuple-element.20), channel_id=1, source_target_pairs={{0,17},{1,16},{2,19},{3,18},{4,21},{5,20},{6,23},{7,22},{8,25},{9,... | collective-permute-start | bytes 774152 | tf_op jit(solution)/shard_map/ppermute | solution.py:172
  10.6 0.0 collective-permute-start.8
  10.7 1.4 %collective-permute-start = (f32[32,72]{1,0:T(8,128)S(1)}, f32[32,72]{1,0:T(8,128)S(1)}, u32[]{:S(2)}, u32[]{:S(2)}) collective-permute-start(f32[32,72]{1,0:T(8,128)S(1)} %get-tuple-element.14), channel_id=1, source_target_pairs={{0,9},{1,8},{2,11},{3,10},{4,13},{5,12},{6,15},{7,14},{8,1},{9,0},... | collective-permute-start | bytes 27656 | tf_op jit(solution)/shard_map/ppermute | solution.py:172
  12.1 9.3 %collective-permute-done = f32[32,72]{1,0:T(8,128)S(1)} collective-permute-done((f32[32,72]{1,0:T(8,128)S(1)}, f32[32,72]{1,0:T(8,128)S(1)}, u32[]{:S(2)}, u32[]{:S(2)}) %collective-permute-start) | collective-permute-done | bytes 9248 | tf_op jit(solution)/shard_map/ppermute | solution.py:172
  21.4 2.2 %collective-permute-start.1 = (f32[32,72]{1,0:T(8,128)S(1)}, f32[32,72]{1,0:T(8,128)S(1)}, u32[]{:S(2)}, u32[]{:S(2)}) collective-permute-start(f32[32,72]{1,0:T(8,128)S(1)} %add.18), channel_id=1, source_target_pairs={{0,17},{1,16},{2,19},{3,18},{4,21},{5,20},{6,23},{7,22},{8,25},{9,... | collective-permute-start | bytes 27656 | tf_op jit(solution)/shard_map/ppermute | solution.py:172
  23.6 1.4 %collective-permute-done.1 = f32[32,72]{1,0:T(8,128)S(1)} collective-permute-done((f32[32,72]{1,0:T(8,128)S(1)}, f32[32,72]{1,0:T(8,128)S(1)}, u32[]{:S(2)}, u32[]{:S(2)}) %collective-permute-start.1) | collective-permute-done | bytes 9248 | tf_op jit(solution)/shard_map/ppermute | solution.py:172
  25.0 1.8 %collective-permute-start.2 = (f32[32,72]{1,0:T(8,128)S(1)}, f32[32,72]{1,0:T(8,128)S(1)}, u32[]{:S(2)}, u32[]{:S(2)}) collective-permute-start(f32[32,72]{1,0:T(8,128)S(1)} %add.19), channel_id=1, source_target_pairs={{0,3},{1,2},{2,1},{3,0},{4,7},{5,6},{6,5},{7,4},{8,11},{9,10},{10,... | collective-permute-start | bytes 27656 | tf_op jit(solution)/shard_map/ppermute | solution.py:172
  26.8 1.4 %collective-permute-done.2 = f32[32,72]{1,0:T(8,128)S(1)} collective-permute-done((f32[32,72]{1,0:T(8,128)S(1)}, f32[32,72]{1,0:T(8,128)S(1)}, u32[]{:S(2)}, u32[]{:S(2)}) %collective-permute-start.2) | collective-permute-done | bytes 9248 | tf_op jit(solution)/shard_map/ppermute | solution.py:172
  28.3 2.7 %collective-permute-start.3 = (f32[32,72]{1,0:T(8,128)S(1)}, f32[32,72]{1,0:T(8,128)S(1)}, u32[]{:S(2)}, u32[]{:S(2)}) collective-permute-start(f32[32,72]{1,0:T(8,128)S(1)} %add.20), channel_id=1, source_target_pairs={{0,5},{1,4},{2,7},{3,6},{4,1},{5,0},{6,3},{7,2},{8,13},{9,12},{10,... | collective-permute-start | bytes 27656 | tf_op jit(solution)/shard_map/ppermute | solution.py:172
  31.0 1.4 %collective-permute-done.3 = f32[32,72]{1,0:T(8,128)S(1)} collective-permute-done((f32[32,72]{1,0:T(8,128)S(1)}, f32[32,72]{1,0:T(8,128)S(1)}, u32[]{:S(2)}, u32[]{:S(2)}) %collective-permute-start.3) | collective-permute-done | bytes 9248 | tf_op jit(solution)/shard_map/ppermute | solution.py:172
  32.4 0.1 collective-permute-start.4
  32.5 1.1 %collective-permute-done.4.b = f32[32,72]{1,0:T(8,128)S(1)} collective-permute-done((f32[32,72]{1,0:T(8,128)S(1)}, f32[32,72]{1,0:T(8,128)S(1)}, u32[]{:S(2)}, u32[]{:S(2)}) %collective-permute-start.4) | collective-permute-done | bytes 9248 | tf_op jit(solution)/shard_map/ppermute | solution.py:175
  33.6 1.7 %shard_map.51 = (f32[72,32]{1,0:T(8,128)S(1)}, f32[32,72]{1,0:T(8,128)S(1)}) custom-call(f32[32,72]{1,0:T(8,128)S(1)} %add.21.a, f32[32,72]{1,0:T(8,128)S(1)} %collective-permute-done.4.b), custom_call_target="tpu_custom_call" | custom-call | flops 67108864 | bytes 18432 | tf_op jit(solution)/shard_map/pallas_call | solution.py:22
  35.4 0.0 collective-permute-done.6.refs_1_
  35.4 0.0 collective-permute-done.7.refs_2_
  35.4 0.0 collective-permute-done.8.refs_3_
  35.4 0.3 shard_map.53
  35.7 1.6 %collective-permute-start.9 = (f32[32,896]{1,0:T(8,128)S(1)}, f32[32,896]{1,0:T(8,128)S(1)}, u32[]{:S(2)}, u32[]{:S(2)}) collective-permute-start(f32[32,896]{1,0:T(8,128)S(1)} %shard_map.53), channel_id=1, source_target_pairs={{0,3},{1,2},{2,1},{3,0},{4,7},{5,6},{6,5},{7,4},{8,11},{9,10},{10,... | collective-permute-start | bytes 344072 | tf_op jit(solution)/shard_map/ppermute | solution.py:172
  37.3 3.5 %collective-permute-done.9 = f32[32,896]{1,0:T(8,128)S(1)} collective-permute-done((f32[32,896]{1,0:T(8,128)S(1)}, f32[32,896]{1,0:T(8,128)S(1)}, u32[]{:S(2)}, u32[]{:S(2)}) %collective-permute-start.9) | collective-permute-done | bytes 114720 | tf_op jit(solution)/shard_map/ppermute | solution.py:172
  40.9 2.5 %collective-permute-start.10 = (f32[32,896]{1,0:T(8,128)S(1)}, f32[32,896]{1,0:T(8,128)S(1)}, u32[]{:S(2)}, u32[]{:S(2)}) collective-permute-start(f32[32,896]{1,0:T(8,128)S(1)} %add.22), channel_id=1, source_target_pairs={{0,5},{1,4},{2,7},{3,6},{4,1},{5,0},{6,3},{7,2},{8,13},{9,12},{10,... | collective-permute-start | bytes 344072 | tf_op jit(solution)/shard_map/ppermute | solution.py:172
  43.4 6.0 %collective-permute-done.10 = f32[32,896]{1,0:T(8,128)S(1)} collective-permute-done((f32[32,896]{1,0:T(8,128)S(1)}, f32[32,896]{1,0:T(8,128)S(1)}, u32[]{:S(2)}, u32[]{:S(2)}) %collective-permute-start.10) | collective-permute-done | bytes 114720 | tf_op jit(solution)/shard_map/ppermute | solution.py:172
  49.4 2.3 %collective-permute-start.13 = (f32[32,896]{1,0:T(8,128)S(1)}, f32[32,896]{1,0:T(8,128)S(1)}, u32[]{:S(2)}, u32[]{:S(2)}) collective-permute-start(f32[32,896]{1,0:T(8,128)S(1)} %add.23.refs_0_), channel_id=1, source_target_pairs={{0,24},{1,25},{2,26},{3,27},{4,28},{5,29},{6,30},{7,31},{8,16},{9,... | collective-permute-start | bytes 344072 | tf_op jit(solution)/shard_map/ppermute | solution.py:172
  51.7 0.1 collective-permute-start.12
  51.8 0.9 %collective-permute-start.11 = (f32[32,896]{1,0:T(8,128)S(1)}, f32[32,896]{1,0:T(8,128)S(1)}, u32[]{:S(2)}, u32[]{:S(2)}) collective-permute-start(f32[32,896]{1,0:T(8,128)S(1)} %add.23.refs_0_), channel_id=1, source_target_pairs={{0,9},{1,8},{2,11},{3,10},{4,13},{5,12},{6,15},{7,14},{8,1},{9,0},... | collective-permute-start | bytes 344072 | tf_op jit(solution)/shard_map/ppermute | solution.py:172
  52.7 0.0 collective-permute-start.14
  52.7 3.0 %collective-permute-done.13.refs_3_ = f32[32,896]{1,0:T(8,128)S(1)} collective-permute-done((f32[32,896]{1,0:T(8,128)S(1)}, f32[32,896]{1,0:T(8,128)S(1)}, u32[]{:S(2)}, u32[]{:S(2)}) %collective-permute-start.13) | collective-permute-done | bytes 114720 | tf_op jit(solution)/shard_map/ppermute | solution.py:172
  55.7 0.0 collective-permute-start.17
  55.7 2.3 %collective-permute-done.12.refs_2_ = f32[32,896]{1,0:T(8,128)S(1)} collective-permute-done((f32[32,896]{1,0:T(8,128)S(1)}, f32[32,896]{1,0:T(8,128)S(1)}, u32[]{:S(2)}, u32[]{:S(2)}) %collective-permute-start.12) | collective-permute-done | bytes 114720 | tf_op jit(solution)/shard_map/ppermute | solution.py:172
  58.0 0.1 collective-permute-start.16
  58.1 0.0 collective-permute-done.11.refs_1_
  58.1 0.4 collective-permute-start.15
  58.5 0.0 collective-permute-done.14.refs_4_
  58.5 0.0 collective-permute-done.17.refs_7_
  58.5 0.8 %collective-permute-done.16.refs_6_ = f32[32,896]{1,0:T(8,128)S(1)} collective-permute-done((f32[32,896]{1,0:T(8,128)S(1)}, f32[32,896]{1,0:T(8,128)S(1)}, u32[]{:S(2)}, u32[]{:S(2)}) %collective-permute-start.16) | collective-permute-done | bytes 114720 | tf_op jit(solution)/shard_map/ppermute | solution.py:175
  59.3 0.2 collective-permute-done.15.refs_5_
  59.5 1.6 %shard_map.54 = (bf16[72,7168]{1,0:T(8,128)(2,1)}, f32[32,7168]{1,0:T(8,128)}) custom-call(f32[72,7168]{1,0:T(8,128)S(1)} %get-tuple-element.13.merged, f32[72,32]{1,0:T(8,128)S(1)} %get-tuple-element.15.basis, f32[32,896]{1,0:T(8,128)S(1)} %add.23.refs_0_, f32[32,896]{1,0:T(8,128)S(1)} %collective-permute-done.11.refs_1_, ...), custom_call_target="tpu_custom_call" | custom-call | flops 134217728 | bytes 2991104 | tf_op jit(solution)/shard_map/pallas_call | solution.py:22
  (6 shorter events, 0.1 us)
Async XLA Ops:
  3.5 2.8 %collective-permute-start.5 = (f32[72,3584]{1,0:T(8,128)S(1)}, f32[72,3584]{1,0:T(8,128)S(1)}, u32[]{:S(2)}, u32[]{:S(2)}) collective-permute-start(f32[72,3584]{1,0:T(8,128)S(1)} %get-tuple-element.17), channel_id=1, source_target_pairs={{0,1},{1,0},{2,3},{3,2},{4,5},{5,4},{6,7},{7,6},{8,9},{9,8},{10,11... | collective-permute-start | bytes 3096584 | tf_op jit(solution)/shard_map/ppermute | solution.py:175
  6.5 28.9 %collective-permute-start.6 = (f32[72,896]{1,0:T(8,128)S(1)}, f32[72,896]{1,0:T(8,128)S(1)}, u32[]{:S(2)}, u32[]{:S(2)}) collective-permute-start(f32[72,896]{1,0:T(8,128)S(1)} %get-tuple-element.19), channel_id=1, source_target_pairs={{0,9},{1,8},{2,11},{3,10},{4,13},{5,12},{6,15},{7,14},{8,1},{9,0},... | collective-permute-start | bytes 774152 | tf_op jit(solution)/shard_map/ppermute | solution.py:172
  9.1 26.3 %collective-permute-start.7 = (f32[72,896]{1,0:T(8,128)S(1)}, f32[72,896]{1,0:T(8,128)S(1)}, u32[]{:S(2)}, u32[]{:S(2)}) collective-permute-start(f32[72,896]{1,0:T(8,128)S(1)} %get-tuple-element.20), channel_id=1, source_target_pairs={{0,17},{1,16},{2,19},{3,18},{4,21},{5,20},{6,23},{7,22},{8,25},{9,... | collective-permute-start | bytes 774152 | tf_op jit(solution)/shard_map/ppermute | solution.py:172
  10.6 24.8 %collective-permute-start.8 = (f32[72,896]{1,0:T(8,128)S(1)}, f32[72,896]{1,0:T(8,128)S(1)}, u32[]{:S(2)}, u32[]{:S(2)}) collective-permute-start(f32[72,896]{1,0:T(8,128)S(1)} %get-tuple-element.21), channel_id=1, source_target_pairs={{0,24},{1,25},{2,26},{3,27},{4,28},{5,29},{6,30},{7,31},{8,16},{9,... | collective-permute-start | bytes 774152 | tf_op jit(solution)/shard_map/ppermute | solution.py:172
  10.7 10.7 %collective-permute-start = (f32[32,72]{1,0:T(8,128)S(1)}, f32[32,72]{1,0:T(8,128)S(1)}, u32[]{:S(2)}, u32[]{:S(2)}) collective-permute-start(f32[32,72]{1,0:T(8,128)S(1)} %get-tuple-element.14), channel_id=1, source_target_pairs={{0,9},{1,8},{2,11},{3,10},{4,13},{5,12},{6,15},{7,14},{8,1},{9,0},... | collective-permute-start | bytes 27656 | tf_op jit(solution)/shard_map/ppermute | solution.py:172
  21.4 3.7 %collective-permute-start.1 = (f32[32,72]{1,0:T(8,128)S(1)}, f32[32,72]{1,0:T(8,128)S(1)}, u32[]{:S(2)}, u32[]{:S(2)}) collective-permute-start(f32[32,72]{1,0:T(8,128)S(1)} %add.18), channel_id=1, source_target_pairs={{0,17},{1,16},{2,19},{3,18},{4,21},{5,20},{6,23},{7,22},{8,25},{9,... | collective-permute-start | bytes 27656 | tf_op jit(solution)/shard_map/ppermute | solution.py:172
  25.0 3.2 %collective-permute-start.2 = (f32[32,72]{1,0:T(8,128)S(1)}, f32[32,72]{1,0:T(8,128)S(1)}, u32[]{:S(2)}, u32[]{:S(2)}) collective-permute-start(f32[32,72]{1,0:T(8,128)S(1)} %add.19), channel_id=1, source_target_pairs={{0,3},{1,2},{2,1},{3,0},{4,7},{5,6},{6,5},{7,4},{8,11},{9,10},{10,... | collective-permute-start | bytes 27656 | tf_op jit(solution)/shard_map/ppermute | solution.py:172
  28.3 4.2 %collective-permute-start.3 = (f32[32,72]{1,0:T(8,128)S(1)}, f32[32,72]{1,0:T(8,128)S(1)}, u32[]{:S(2)}, u32[]{:S(2)}) collective-permute-start(f32[32,72]{1,0:T(8,128)S(1)} %add.20), channel_id=1, source_target_pairs={{0,5},{1,4},{2,7},{3,6},{4,1},{5,0},{6,3},{7,2},{8,13},{9,12},{10,... | collective-permute-start | bytes 27656 | tf_op jit(solution)/shard_map/ppermute | solution.py:172
  32.4 1.2 %collective-permute-start.4 = (f32[32,72]{1,0:T(8,128)S(1)}, f32[32,72]{1,0:T(8,128)S(1)}, u32[]{:S(2)}, u32[]{:S(2)}) collective-permute-start(f32[32,72]{1,0:T(8,128)S(1)} %add.21.a), channel_id=1, source_target_pairs={{0,1},{1,0},{2,3},{3,2},{4,5},{5,4},{6,7},{7,6},{8,9},{9,8},{10,11... | collective-permute-start | bytes 27656 | tf_op jit(solution)/shard_map/ppermute | solution.py:175
  35.7 5.1 %collective-permute-start.9 = (f32[32,896]{1,0:T(8,128)S(1)}, f32[32,896]{1,0:T(8,128)S(1)}, u32[]{:S(2)}, u32[]{:S(2)}) collective-permute-start(f32[32,896]{1,0:T(8,128)S(1)} %shard_map.53), channel_id=1, source_target_pairs={{0,3},{1,2},{2,1},{3,0},{4,7},{5,6},{6,5},{7,4},{8,11},{9,10},{10,... | collective-permute-start | bytes 344072 | tf_op jit(solution)/shard_map/ppermute | solution.py:172
  40.9 8.5 %collective-permute-start.10 = (f32[32,896]{1,0:T(8,128)S(1)}, f32[32,896]{1,0:T(8,128)S(1)}, u32[]{:S(2)}, u32[]{:S(2)}) collective-permute-start(f32[32,896]{1,0:T(8,128)S(1)} %add.22), channel_id=1, source_target_pairs={{0,5},{1,4},{2,7},{3,6},{4,1},{5,0},{6,3},{7,2},{8,13},{9,12},{10,... | collective-permute-start | bytes 344072 | tf_op jit(solution)/shard_map/ppermute | solution.py:172
  49.4 6.3 %collective-permute-start.13 = (f32[32,896]{1,0:T(8,128)S(1)}, f32[32,896]{1,0:T(8,128)S(1)}, u32[]{:S(2)}, u32[]{:S(2)}) collective-permute-start(f32[32,896]{1,0:T(8,128)S(1)} %add.23.refs_0_), channel_id=1, source_target_pairs={{0,24},{1,25},{2,26},{3,27},{4,28},{5,29},{6,30},{7,31},{8,16},{9,... | collective-permute-start | bytes 344072 | tf_op jit(solution)/shard_map/ppermute | solution.py:172
  51.7 6.3 %collective-permute-start.12 = (f32[32,896]{1,0:T(8,128)S(1)}, f32[32,896]{1,0:T(8,128)S(1)}, u32[]{:S(2)}, u32[]{:S(2)}) collective-permute-start(f32[32,896]{1,0:T(8,128)S(1)} %add.23.refs_0_), channel_id=1, source_target_pairs={{0,17},{1,16},{2,19},{3,18},{4,21},{5,20},{6,23},{7,22},{8,25},{9,... | collective-permute-start | bytes 344072 | tf_op jit(solution)/shard_map/ppermute | solution.py:172
  51.8 6.3 %collective-permute-start.11 = (f32[32,896]{1,0:T(8,128)S(1)}, f32[32,896]{1,0:T(8,128)S(1)}, u32[]{:S(2)}, u32[]{:S(2)}) collective-permute-start(f32[32,896]{1,0:T(8,128)S(1)} %add.23.refs_0_), channel_id=1, source_target_pairs={{0,9},{1,8},{2,11},{3,10},{4,13},{5,12},{6,15},{7,14},{8,1},{9,0},... | collective-permute-start | bytes 344072 | tf_op jit(solution)/shard_map/ppermute | solution.py:172
  52.7 5.9 %collective-permute-start.14 = (f32[32,896]{1,0:T(8,128)S(1)}, f32[32,896]{1,0:T(8,128)S(1)}, u32[]{:S(2)}, u32[]{:S(2)}) collective-permute-start(f32[32,896]{1,0:T(8,128)S(1)} %add.23.refs_0_), channel_id=1, source_target_pairs={{0,1},{1,0},{2,3},{3,2},{4,5},{5,4},{6,7},{7,6},{8,9},{9,8},{10,11... | collective-permute-start | bytes 344072 | tf_op jit(solution)/shard_map/ppermute | solution.py:175
  55.7 2.9 %collective-permute-start.17 = (f32[32,896]{1,0:T(8,128)S(1)}, f32[32,896]{1,0:T(8,128)S(1)}, u32[]{:S(2)}, u32[]{:S(2)}) collective-permute-start(f32[32,896]{1,0:T(8,128)S(1)} %collective-permute-done.13.refs_3_), channel_id=1, source_target_pairs={{0,1},{1,0},{2,3},{3,2},{4,5},{5,4},{6,7},{7,6},{8,9},{9,8},{10,11... | collective-permute-start | bytes 344072 | tf_op jit(solution)/shard_map/ppermute | solution.py:175
  58.0 1.3 %collective-permute-start.16 = (f32[32,896]{1,0:T(8,128)S(1)}, f32[32,896]{1,0:T(8,128)S(1)}, u32[]{:S(2)}, u32[]{:S(2)}) collective-permute-start(f32[32,896]{1,0:T(8,128)S(1)} %collective-permute-done.12.refs_2_), channel_id=1, source_target_pairs={{0,1},{1,0},{2,3},{3,2},{4,5},{5,4},{6,7},{7,6},{8,9},{9,8},{10,11... | collective-permute-start | bytes 344072 | tf_op jit(solution)/shard_map/ppermute | solution.py:175
  58.1 1.4 %collective-permute-start.15 = (f32[32,896]{1,0:T(8,128)S(1)}, f32[32,896]{1,0:T(8,128)S(1)}, u32[]{:S(2)}, u32[]{:S(2)}) collective-permute-start(f32[32,896]{1,0:T(8,128)S(1)} %collective-permute-done.11.refs_1_), channel_id=1, source_target_pairs={{0,1},{1,0},{2,3},{3,2},{4,5},{5,4},{6,7},{7,6},{8,9},{9,8},{10,11... | collective-permute-start | bytes 344072 | tf_op jit(solution)/shard_map/ppermute | solution.py:175

commit v3 on v2

--- a/solution.py
+++ b/solution.py
@@ -13,6 +13,7 @@
 F32, BF16 = jnp.float32, jnp.bfloat16
 VMEM = pltpu.VMEM
 PIECES = 4
+PARTS = 2
 
 
 def call(kernel, outs, *args, flops=1 << 20, limit=12, scratch=(), space=VMEM):
@@ -122,26 +123,30 @@
 
 
 def right_kernel(basis_t, *refs):
-    *terms, out = refs
+    terms, outs = refs[:-PARTS], refs[-PARTS:]
     total = terms[0][...]
     for term in terms[1:]:
         total = total + term[...]
-    out[...] = jnp.dot(basis_t[...], total, precision=lax.Precision.HIGHEST, preferred_element_type=F32)
+    both = jnp.dot(basis_t[...], total, precision=lax.Precision.HIGHEST, preferred_element_type=F32)
+    size = outs[0].shape[0]
+    for i, out in enumerate(outs):
+        out[...] = both[i * size : (i + 1) * size]
 
 
 def final_kernel(workers, merged, basis, *refs):
     *blocks, feedback, new_basis_t = refs
-    chunks = len(blocks) // 2
+    count = len(blocks) // PARTS
+    chunks = count // 2
     width = blocks[0].shape[1]
     mine = lax.axis_index("local")
     half = own_half()
     high, low = split(basis[...] * (1.0 / workers))
     left = jnp.concatenate([high, low, high], axis=1)
-    for i, block in enumerate(blocks):
+    for i in range(count):
         side = half if i < chunks else 1 - half
         start = (side * chunks + partner(mine, i % chunks, chunks)) * width
         span = pl.ds(pl.multiple_of(start, 128), width)
-        piece = block[...]
+        piece = jnp.concatenate([block[...] for block in blocks[i::count]], axis=0)
         new_basis_t[:, span] = piece
         upper, lower = split(piece)
         right = jnp.concatenate([upper, upper, lower], axis=0)
@@ -174,9 +179,9 @@
     def swap(value):
         return lax.ppermute(value, AXES, [(i, i ^ 1) for i in range(local * dp)])
 
-    def total_over(value, along_local):
+    def total_over(value, along_local, direct=False):
         size = local if along_local else groups
-        double = not size & (size - 1)
+        double = not direct and not size & (size - 1)
         first = value
         step = 1
         while step < size:
@@ -195,7 +200,7 @@
         space=pltpu.HBM,
     )
     got = swap(send)
-    left = total_over(left, True)
+    left = total_over(left, True, direct=True)
     chunks = call(pair_kernel, [((rows, width), F32)] * local, merged, got)
     terms = [chunks[0]] + [permute(chunks[s], True, s) for s in range(1, local)]
     left = total_over(left, False)
@@ -204,10 +209,12 @@
         [((rows, rank), F32), ((rank, rows), F32)],
         left, swap(left), flops=1 << 26,
     )
-    right = call(right_kernel, ((rank, width), F32), basis_t, *terms, flops=1 << 25)
-    own = total_over(right, False)
-    blocks = [own] + [permute(own, True, s) for s in range(1, local)]
-    blocks += [swap(block) for block in blocks]
+    rights = call(right_kernel, [((rank // PARTS, width), F32)] * PARTS, basis_t, *terms, flops=1 << 25)
+    blocks = []
+    for right in rights:
+        own = total_over(right, False)
+        gathered = [own] + [permute(own, True, s) for s in range(1, local)]
+        blocks += gathered + [swap(block) for block in gathered]
     new_feedback, new_basis_t = call(
         functools.partial(final_kernel, local * dp),
         [((rows, columns), BF16), ((rank, columns), F32)],

time: 61.3 us -> 48.2 us (0.79)
  the two profiles are of different devices: /device:TPU:0 before, /device:TPU:27 now
where the time goes in v3:
time: 48.2 us; the launch traced here: 48 us
  waiting for transfers between devices  20.4 us (42%)
  starting transfers between devices  20.2 us (42%)
  Pallas kernels  6.69 us (14%)
  between operations  0.7 us (1%)
    ppermute x18, waiting for transfers between devices, permute(): return lax.ppermute(value, AXES, pairs)  18.1 us
    ppermute x18, starting transfers between devices, permute(): return lax.ppermute(value, AXES, pairs)  16.1 us
    pallas_call x5, Pallas kernels, call(): pl.pallas_call(kernel, out_shape=shapes, in_specs=[pl.BlockSpec(memory_sp...  6.69 us
    ppermute x10, starting transfers between devices, swap(): return lax.ppermute(value, AXES, [(i, i ^ 1) for i in range(local * dp)])  4.15 us
    ppermute x10, waiting for transfers between devices, swap(): return lax.ppermute(value, AXES, [(i, i ^ 1) for i in range(local * dp)])  2.31 us
  transfers between devices with their start and end apart: 28, of which 14 were waited for; matrix products, arithmetic and copies ran while one was open for 0% of the time, Pallas kernels for 4%

profile of v3, /device:TPU:27, one launch (start us, length us, event | category | flops | bytes accessed | tf_op | source)
XLA Modules:
  0.0 48.0 jit_solution(1048939746066324761)
XLA Ops:
  0.6 2.9 %shard_map.50 = (f32[32,72]{1,0:T(8,128)S(1)}, f32[72,7168]{1,0:T(8,128)S(1)}, f32[72,3584]{1,0:T(8,128)S(1)}) custom-call(bf16[72,7168]{1,0:T(8,128)(2,1)} %bitcast.5, bf16[72,7168]{1,0:T(8,128)(2,1)} %bitcast.6, f32[32,7168]{1,0:T(8,128)} %bitcast.7), custom_call_target="tpu_custom_call" | custom-call | flops 134217728 | bytes 2981888 | tf_op jit(solution)/shard_map/pallas_call | solution.py:23
  3.5 0.7 %collective-permute-start.6 = (f32[72,3584]{1,0:T(8,128)S(1)}, f32[72,3584]{1,0:T(8,128)S(1)}, u32[]{:S(2)}, u32[]{:S(2)}) collective-permute-start(f32[72,3584]{1,0:T(8,128)S(1)} %get-tuple-element.19), channel_id=1, source_target_pairs={{0,1},{1,0},{2,3},{3,2},{4,5},{5,4},{6,7},{7,6},{8,9},{9,8},{10,11... | collective-permute-start | bytes 3096584 | tf_op jit(solution)/shard_map/ppermute | solution.py:180
  4.3 1.2 %collective-permute-start.2 = (f32[32,72]{1,0:T(8,128)S(1)}, f32[32,72]{1,0:T(8,128)S(1)}, u32[]{:S(2)}, u32[]{:S(2)}) collective-permute-start(f32[32,72]{1,0:T(8,128)S(1)} %get-tuple-element.16), channel_id=1, source_target_pairs={{0,24},{1,25},{2,26},{3,27},{4,28},{5,29},{6,30},{7,31},{8,16},{9,... | collective-permute-start | bytes 27656 | tf_op jit(solution)/shard_map/ppermute | solution.py:177
  5.5 0.5 collective-permute-start.1
  6.0 1.3 %collective-permute-start = (f32[32,72]{1,0:T(8,128)S(1)}, f32[32,72]{1,0:T(8,128)S(1)}, u32[]{:S(2)}, u32[]{:S(2)}) collective-permute-start(f32[32,72]{1,0:T(8,128)S(1)} %get-tuple-element.16), channel_id=1, source_target_pairs={{0,9},{1,8},{2,11},{3,10},{4,13},{5,12},{6,15},{7,14},{8,1},{9,0},... | collective-permute-start | bytes 27656 | tf_op jit(solution)/shard_map/ppermute | solution.py:177
  7.2 0.1 shard_map.52
  7.3 0.6 %collective-permute-start.7 = (f32[72,896]{1,0:T(8,128)S(1)}, f32[72,896]{1,0:T(8,128)S(1)}, u32[]{:S(2)}, u32[]{:S(2)}) collective-permute-start(f32[72,896]{1,0:T(8,128)S(1)} %get-tuple-element.21), channel_id=1, source_target_pairs={{0,9},{1,8},{2,11},{3,10},{4,13},{5,12},{6,15},{7,14},{8,1},{9,0},... | collective-permute-start | bytes 774152 | tf_op jit(solution)/shard_map/ppermute | solution.py:177
  7.9 1.3 %collective-permute-start.8 = (f32[72,896]{1,0:T(8,128)S(1)}, f32[72,896]{1,0:T(8,128)S(1)}, u32[]{:S(2)}, u32[]{:S(2)}) collective-permute-start(f32[72,896]{1,0:T(8,128)S(1)} %get-tuple-element.22), channel_id=1, source_target_pairs={{0,17},{1,16},{2,19},{3,18},{4,21},{5,20},{6,23},{7,22},{8,25},{9,... | collective-permute-start | bytes 774152 | tf_op jit(solution)/shard_map/ppermute | solution.py:177
  9.2 0.0 collective-permute-done.2
  9.2 1.2 %collective-permute-start.9 = (f32[72,896]{1,0:T(8,128)S(1)}, f32[72,896]{1,0:T(8,128)S(1)}, u32[]{:S(2)}, u32[]{:S(2)}) collective-permute-start(f32[72,896]{1,0:T(8,128)S(1)} %get-tuple-element.23), channel_id=1, source_target_pairs={{0,24},{1,25},{2,26},{3,27},{4,28},{5,29},{6,30},{7,31},{8,16},{9,... | collective-permute-start | bytes 774152 | tf_op jit(solution)/shard_map/ppermute | solution.py:177
  10.3 0.8 %collective-permute-start.3 = (f32[32,72]{1,0:T(8,128)S(1)}, f32[32,72]{1,0:T(8,128)S(1)}, u32[]{:S(2)}, u32[]{:S(2)}) collective-permute-start(f32[32,72]{1,0:T(8,128)S(1)} %add_add_fusion), channel_id=1, source_target_pairs={{0,3},{1,2},{2,1},{3,0},{4,7},{5,6},{6,5},{7,4},{8,11},{9,10},{10,... | collective-permute-start | bytes 27656 | tf_op jit(solution)/shard_map/ppermute | solution.py:177
  11.1 2.9 %collective-permute-done.3 = f32[32,72]{1,0:T(8,128)S(1)} collective-permute-done((f32[32,72]{1,0:T(8,128)S(1)}, f32[32,72]{1,0:T(8,128)S(1)}, u32[]{:S(2)}, u32[]{:S(2)}) %collective-permute-start.3) | collective-permute-done | bytes 9248 | tf_op jit(solution)/shard_map/ppermute | solution.py:177
  14.0 0.3 collective-permute-start.4
  14.3 4.1 %collective-permute-done.4 = f32[32,72]{1,0:T(8,128)S(1)} collective-permute-done((f32[32,72]{1,0:T(8,128)S(1)}, f32[32,72]{1,0:T(8,128)S(1)}, u32[]{:S(2)}, u32[]{:S(2)}) %collective-permute-start.4) | collective-permute-done | bytes 9248 | tf_op jit(solution)/shard_map/ppermute | solution.py:177
  18.4 1.2 %collective-permute-done.5.b = f32[32,72]{1,0:T(8,128)S(1)} collective-permute-done((f32[32,72]{1,0:T(8,128)S(1)}, f32[32,72]{1,0:T(8,128)S(1)}, u32[]{:S(2)}, u32[]{:S(2)}) %collective-permute-start.5) | collective-permute-done | bytes 9248 | tf_op jit(solution)/shard_map/ppermute | solution.py:180
  19.6 1.7 %shard_map.51 = (f32[72,32]{1,0:T(8,128)S(1)}, f32[32,72]{1,0:T(8,128)S(1)}) custom-call(f32[32,72]{1,0:T(8,128)S(1)} %add.31.a, f32[32,72]{1,0:T(8,128)S(1)} %collective-permute-done.5.b), custom_call_target="tpu_custom_call" | custom-call | flops 67108864 | bytes 18432 | tf_op jit(solution)/shard_map/pallas_call | solution.py:23
  21.4 0.0 collective-permute-done.8.refs_2_
  21.4 0.6 %collective-permute-done.9.refs_3_ = f32[72,896]{1,0:T(8,128)S(1)} collective-permute-done((f32[72,896]{1,0:T(8,128)S(1)}, f32[72,896]{1,0:T(8,128)S(1)}, u32[]{:S(2)}, u32[]{:S(2)}) %collective-permute-start.9) | collective-permute-done | bytes 258080 | tf_op jit(solution)/shard_map/ppermute | solution.py:177
  22.0 0.3 shard_map.53
  22.3 0.8 %collective-permute-start.10 = (f32[16,896]{1,0:T(8,128)S(1)}, f32[16,896]{1,0:T(8,128)S(1)}, u32[]{:S(2)}, u32[]{:S(2)}) collective-permute-start(f32[16,896]{1,0:T(8,128)S(1)} %get-tuple-element.24), channel_id=1, source_target_pairs={{0,3},{1,2},{2,1},{3,0},{4,7},{5,6},{6,5},{7,4},{8,11},{9,10},{10,... | collective-permute-start | bytes 172040 | tf_op jit(solution)/shard_map/ppermute | solution.py:177
  23.1 1.0 %collective-permute-start.19 = (f32[16,896]{1,0:T(8,128)S(1)}, f32[16,896]{1,0:T(8,128)S(1)}, u32[]{:S(2)}, u32[]{:S(2)}) collective-permute-start(f32[16,896]{1,0:T(8,128)S(1)} %get-tuple-element.25), channel_id=1, source_target_pairs={{0,3},{1,2},{2,1},{3,0},{4,7},{5,6},{6,5},{7,4},{8,11},{9,10},{10,... | collective-permute-start | bytes 172040 | tf_op jit(solution)/shard_map/ppermute | solution.py:177
  24.1 2.7 %collective-permute-done.10 = f32[16,896]{1,0:T(8,128)S(1)} collective-permute-done((f32[16,896]{1,0:T(8,128)S(1)}, f32[16,896]{1,0:T(8,128)S(1)}, u32[]{:S(2)}, u32[]{:S(2)}) %collective-permute-start.10) | collective-permute-done | bytes 57376 | tf_op jit(solution)/shard_map/ppermute | solution.py:177
  26.8 0.5 %collective-permute-start.11 = (f32[16,896]{1,0:T(8,128)S(1)}, f32[16,896]{1,0:T(8,128)S(1)}, u32[]{:S(2)}, u32[]{:S(2)}) collective-permute-start(f32[16,896]{1,0:T(8,128)S(1)} %add.32), channel_id=1, source_target_pairs={{0,5},{1,4},{2,7},{3,6},{4,1},{5,0},{6,3},{7,2},{8,13},{9,12},{10,... | collective-permute-start | bytes 172040 | tf_op jit(solution)/shard_map/ppermute | solution.py:177
  27.3 0.7 %collective-permute-done.19 = f32[16,896]{1,0:T(8,128)S(1)} collective-permute-done((f32[16,896]{1,0:T(8,128)S(1)}, f32[16,896]{1,0:T(8,128)S(1)}, u32[]{:S(2)}, u32[]{:S(2)}) %collective-permute-start.19) | collective-permute-done | bytes 57376 | tf_op jit(solution)/shard_map/ppermute | solution.py:177
  28.1 1.6 %collective-permute-start.20 = (f32[16,896]{1,0:T(8,128)S(1)}, f32[16,896]{1,0:T(8,128)S(1)}, u32[]{:S(2)}, u32[]{:S(2)}) collective-permute-start(f32[16,896]{1,0:T(8,128)S(1)} %add.34), channel_id=1, source_target_pairs={{0,5},{1,4},{2,7},{3,6},{4,1},{5,0},{6,3},{7,2},{8,13},{9,12},{10,... | collective-permute-start | bytes 172040 | tf_op jit(solution)/shard_map/ppermute | solution.py:177
  29.6 4.7 %collective-permute-done.11 = f32[16,896]{1,0:T(8,128)S(1)} collective-permute-done((f32[16,896]{1,0:T(8,128)S(1)}, f32[16,896]{1,0:T(8,128)S(1)}, u32[]{:S(2)}, u32[]{:S(2)}) %collective-permute-start.11) | collective-permute-done | bytes 57376 | tf_op jit(solution)/shard_map/ppermute | solution.py:177
  34.3 0.4 collective-permute-start.15
  34.8 0.5 %collective-permute-start.14 = (f32[16,896]{1,0:T(8,128)S(1)}, f32[16,896]{1,0:T(8,128)S(1)}, u32[]{:S(2)}, u32[]{:S(2)}) collective-permute-start(f32[16,896]{1,0:T(8,128)S(1)} %add.33.refs_0_), channel_id=1, source_target_pairs={{0,24},{1,25},{2,26},{3,27},{4,28},{5,29},{6,30},{7,31},{8,16},{9,... | collective-permute-start | bytes 172040 | tf_op jit(solution)/shard_map/ppermute | solution.py:177
  35.3 1.3 %collective-permute-start.13 = (f32[16,896]{1,0:T(8,128)S(1)}, f32[16,896]{1,0:T(8,128)S(1)}, u32[]{:S(2)}, u32[]{:S(2)}) collective-permute-start(f32[16,896]{1,0:T(8,128)S(1)} %add.33.refs_0_), channel_id=1, source_target_pairs={{0,17},{1,16},{2,19},{3,18},{4,21},{5,20},{6,23},{7,22},{8,25},{9,... | collective-permute-start | bytes 172040 | tf_op jit(solution)/shard_map/ppermute | solution.py:177
  36.6 1.1 %collective-permute-start.12 = (f32[16,896]{1,0:T(8,128)S(1)}, f32[16,896]{1,0:T(8,128)S(1)}, u32[]{:S(2)}, u32[]{:S(2)}) collective-permute-start(f32[16,896]{1,0:T(8,128)S(1)} %add.33.refs_0_), channel_id=1, source_target_pairs={{0,9},{1,8},{2,11},{3,10},{4,13},{5,12},{6,15},{7,14},{8,1},{9,0},... | collective-permute-start | bytes 172040 | tf_op jit(solution)/shard_map/ppermute | solution.py:177
  37.7 0.5 %collective-permute-start.24 = (f32[16,896]{1,0:T(8,128)S(1)}, f32[16,896]{1,0:T(8,128)S(1)}, u32[]{:S(2)}, u32[]{:S(2)}) collective-permute-start(f32[16,896]{1,0:T(8,128)S(1)} %add.35.refs_8_), channel_id=1, source_target_pairs={{0,1},{1,0},{2,3},{3,2},{4,5},{5,4},{6,7},{7,6},{8,9},{9,8},{10,11... | collective-permute-start | bytes 172040 | tf_op jit(solution)/shard_map/ppermute | solution.py:180
  38.2 0.8 %collective-permute-start.23 = (f32[16,896]{1,0:T(8,128)S(1)}, f32[16,896]{1,0:T(8,128)S(1)}, u32[]{:S(2)}, u32[]{:S(2)}) collective-permute-start(f32[16,896]{1,0:T(8,128)S(1)} %add.35.refs_8_), channel_id=1, source_target_pairs={{0,24},{1,25},{2,26},{3,27},{4,28},{5,29},{6,30},{7,31},{8,16},{9,... | collective-permute-start | bytes 172040 | tf_op jit(solution)/shard_map/ppermute | solution.py:177
  39.0 1.2 %collective-permute-start.22 = (f32[16,896]{1,0:T(8,128)S(1)}, f32[16,896]{1,0:T(8,128)S(1)}, u32[]{:S(2)}, u32[]{:S(2)}) collective-permute-start(f32[16,896]{1,0:T(8,128)S(1)} %add.35.refs_8_), channel_id=1, source_target_pairs={{0,17},{1,16},{2,19},{3,18},{4,21},{5,20},{6,23},{7,22},{8,25},{9,... | collective-permute-start | bytes 172040 | tf_op jit(solution)/shard_map/ppermute | solution.py:177
  40.2 0.6 %collective-permute-done.13.refs_2_ = f32[16,896]{1,0:T(8,128)S(1)} collective-permute-done((f32[16,896]{1,0:T(8,128)S(1)}, f32[16,896]{1,0:T(8,128)S(1)}, u32[]{:S(2)}, u32[]{:S(2)}) %collective-permute-start.13) | collective-permute-done | bytes 57376 | tf_op jit(solution)/shard_map/ppermute | solution.py:177
  40.8 0.4 collective-permute-start.21
  41.2 0.3 collective-permute-start.18
  41.5 0.2 collective-permute-start.17
  41.7 0.8 %collective-permute-done.23.refs_11_ = f32[16,896]{1,0:T(8,128)S(1)} collective-permute-done((f32[16,896]{1,0:T(8,128)S(1)}, f32[16,896]{1,0:T(8,128)S(1)}, u32[]{:S(2)}, u32[]{:S(2)}) %collective-permute-start.23) | collective-permute-done | bytes 57376 | tf_op jit(solution)/shard_map/ppermute | solution.py:177
  42.5 1.0 %collective-permute-start.16 = (f32[16,896]{1,0:T(8,128)S(1)}, f32[16,896]{1,0:T(8,128)S(1)}, u32[]{:S(2)}, u32[]{:S(2)}) collective-permute-start(f32[16,896]{1,0:T(8,128)S(1)} %collective-permute-done.12.refs_1_), channel_id=1, source_target_pairs={{0,1},{1,0},{2,3},{3,2},{4,5},{5,4},{6,7},{7,6},{8,9},{9,8},{10,11... | collective-permute-start | bytes 172040 | tf_op jit(solution)/shard_map/ppermute | solution.py:180
  43.5 0.7 %collective-permute-done.22.refs_10_ = f32[16,896]{1,0:T(8,128)S(1)} collective-permute-done((f32[16,896]{1,0:T(8,128)S(1)}, f32[16,896]{1,0:T(8,128)S(1)}, u32[]{:S(2)}, u32[]{:S(2)}) %collective-permute-start.22) | collective-permute-done | bytes 57376 | tf_op jit(solution)/shard_map/ppermute | solution.py:177
  44.2 0.4 collective-permute-start.27
  44.7 0.1 collective-permute-done.21.refs_9_
  44.8 0.4 collective-permute-start.26
  45.2 0.1 collective-permute-start.25
  45.3 0.3 collective-permute-done.27.refs_15_
  45.5 0.5 %collective-permute-done.26.refs_14_ = f32[16,896]{1,0:T(8,128)S(1)} collective-permute-done((f32[16,896]{1,0:T(8,128)S(1)}, f32[16,896]{1,0:T(8,128)S(1)}, u32[]{:S(2)}, u32[]{:S(2)}) %collective-permute-start.26) | collective-permute-done | bytes 57376 | tf_op jit(solution)/shard_map/ppermute | solution.py:180
  46.0 0.4 collective-permute-done.25.refs_13_
  46.4 1.6 %shard_map.54 = (bf16[72,7168]{1,0:T(8,128)(2,1)}, f32[32,7168]{1,0:T(8,128)}) custom-call(f32[72,7168]{1,0:T(8,128)S(1)} %get-tuple-element.15.merged, f32[72,32]{1,0:T(8,128)S(1)} %get-tuple-element.17.basis, f32[16,896]{1,0:T(8,128)S(1)} %add.33.refs_0_, f32[16,896]{1,0:T(8,128)S(1)} %collective-permute-done.12.refs_1_, ...), custom_call_target="tpu_custom_call" | custom-call | flops 134217728 | bytes 2991104 | tf_op jit(solution)/shard_map/pallas_call | solution.py:23
  (20 shorter events, 0.1 us)
Async XLA Ops:
  3.5 3.7 %collective-permute-start.6 = (f32[72,3584]{1,0:T(8,128)S(1)}, f32[72,3584]{1,0:T(8,128)S(1)}, u32[]{:S(2)}, u32[]{:S(2)}) collective-permute-start(f32[72,3584]{1,0:T(8,128)S(1)} %get-tuple-element.19), channel_id=1, source_target_pairs={{0,1},{1,0},{2,3},{3,2},{4,5},{5,4},{6,7},{7,6},{8,9},{9,8},{10,11... | collective-permute-start | bytes 3096584 | tf_op jit(solution)/shard_map/ppermute | solution.py:180
  4.3 4.9 %collective-permute-start.2 = (f32[32,72]{1,0:T(8,128)S(1)}, f32[32,72]{1,0:T(8,128)S(1)}, u32[]{:S(2)}, u32[]{:S(2)}) collective-permute-start(f32[32,72]{1,0:T(8,128)S(1)} %get-tuple-element.16), channel_id=1, source_target_pairs={{0,24},{1,25},{2,26},{3,27},{4,28},{5,29},{6,30},{7,31},{8,16},{9,... | collective-permute-start | bytes 27656 | tf_op jit(solution)/shard_map/ppermute | solution.py:177
  5.5 4.8 %collective-permute-start.1 = (f32[32,72]{1,0:T(8,128)S(1)}, f32[32,72]{1,0:T(8,128)S(1)}, u32[]{:S(2)}, u32[]{:S(2)}) collective-permute-start(f32[32,72]{1,0:T(8,128)S(1)} %get-tuple-element.16), channel_id=1, source_target_pairs={{0,17},{1,16},{2,19},{3,18},{4,21},{5,20},{6,23},{7,22},{8,25},{9,... | collective-permute-start | bytes 27656 | tf_op jit(solution)/shard_map/ppermute | solution.py:177
  6.0 4.4 %collective-permute-start = (f32[32,72]{1,0:T(8,128)S(1)}, f32[32,72]{1,0:T(8,128)S(1)}, u32[]{:S(2)}, u32[]{:S(2)}) collective-permute-start(f32[32,72]{1,0:T(8,128)S(1)} %get-tuple-element.16), channel_id=1, source_target_pairs={{0,9},{1,8},{2,11},{3,10},{4,13},{5,12},{6,15},{7,14},{8,1},{9,0},... | collective-permute-start | bytes 27656 | tf_op jit(solution)/shard_map/ppermute | solution.py:177
  7.3 14.0 %collective-permute-start.7 = (f32[72,896]{1,0:T(8,128)S(1)}, f32[72,896]{1,0:T(8,128)S(1)}, u32[]{:S(2)}, u32[]{:S(2)}) collective-permute-start(f32[72,896]{1,0:T(8,128)S(1)} %get-tuple-element.21), channel_id=1, source_target_pairs={{0,9},{1,8},{2,11},{3,10},{4,13},{5,12},{6,15},{7,14},{8,1},{9,0},... | collective-permute-start | bytes 774152 | tf_op jit(solution)/shard_map/ppermute | solution.py:177
  7.9 13.5 %collective-permute-start.8 = (f32[72,896]{1,0:T(8,128)S(1)}, f32[72,896]{1,0:T(8,128)S(1)}, u32[]{:S(2)}, u32[]{:S(2)}) collective-permute-start(f32[72,896]{1,0:T(8,128)S(1)} %get-tuple-element.22), channel_id=1, source_target_pairs={{0,17},{1,16},{2,19},{3,18},{4,21},{5,20},{6,23},{7,22},{8,25},{9,... | collective-permute-start | bytes 774152 | tf_op jit(solution)/shard_map/ppermute | solution.py:177
  9.2 12.9 %collective-permute-start.9 = (f32[72,896]{1,0:T(8,128)S(1)}, f32[72,896]{1,0:T(8,128)S(1)}, u32[]{:S(2)}, u32[]{:S(2)}) collective-permute-start(f32[72,896]{1,0:T(8,128)S(1)} %get-tuple-element.23), channel_id=1, source_target_pairs={{0,24},{1,25},{2,26},{3,27},{4,28},{5,29},{6,30},{7,31},{8,16},{9,... | collective-permute-start | bytes 774152 | tf_op jit(solution)/shard_map/ppermute | solution.py:177
  10.3 3.6 %collective-permute-start.3 = (f32[32,72]{1,0:T(8,128)S(1)}, f32[32,72]{1,0:T(8,128)S(1)}, u32[]{:S(2)}, u32[]{:S(2)}) collective-permute-start(f32[32,72]{1,0:T(8,128)S(1)} %add_add_fusion), channel_id=1, source_target_pairs={{0,3},{1,2},{2,1},{3,0},{4,7},{5,6},{6,5},{7,4},{8,11},{9,10},{10,... | collective-permute-start | bytes 27656 | tf_op jit(solution)/shard_map/ppermute | solution.py:177
  14.0 4.4 %collective-permute-start.4 = (f32[32,72]{1,0:T(8,128)S(1)}, f32[32,72]{1,0:T(8,128)S(1)}, u32[]{:S(2)}, u32[]{:S(2)}) collective-permute-start(f32[32,72]{1,0:T(8,128)S(1)} %add.30), channel_id=1, source_target_pairs={{0,5},{1,4},{2,7},{3,6},{4,1},{5,0},{6,3},{7,2},{8,13},{9,12},{10,... | collective-permute-start | bytes 27656 | tf_op jit(solution)/shard_map/ppermute | solution.py:177
  18.4 1.2 %collective-permute-start.5 = (f32[32,72]{1,0:T(8,128)S(1)}, f32[32,72]{1,0:T(8,128)S(1)}, u32[]{:S(2)}, u32[]{:S(2)}) collective-permute-start(f32[32,72]{1,0:T(8,128)S(1)} %add.31.a), channel_id=1, source_target_pairs={{0,1},{1,0},{2,3},{3,2},{4,5},{5,4},{6,7},{7,6},{8,9},{9,8},{10,11... | collective-permute-start | bytes 27656 | tf_op jit(solution)/shard_map/ppermute | solution.py:180
  22.3 4.5 %collective-permute-start.10 = (f32[16,896]{1,0:T(8,128)S(1)}, f32[16,896]{1,0:T(8,128)S(1)}, u32[]{:S(2)}, u32[]{:S(2)}) collective-permute-start(f32[16,896]{1,0:T(8,128)S(1)} %get-tuple-element.24), channel_id=1, source_target_pairs={{0,3},{1,2},{2,1},{3,0},{4,7},{5,6},{6,5},{7,4},{8,11},{9,10},{10,... | collective-permute-start | bytes 172040 | tf_op jit(solution)/shard_map/ppermute | solution.py:177
  23.1 4.9 %collective-permute-start.19 = (f32[16,896]{1,0:T(8,128)S(1)}, f32[16,896]{1,0:T(8,128)S(1)}, u32[]{:S(2)}, u32[]{:S(2)}) collective-permute-start(f32[16,896]{1,0:T(8,128)S(1)} %get-tuple-element.25), channel_id=1, source_target_pairs={{0,3},{1,2},{2,1},{3,0},{4,7},{5,6},{6,5},{7,4},{8,11},{9,10},{10,... | collective-permute-start | bytes 172040 | tf_op jit(solution)/shard_map/ppermute | solution.py:177
  26.8 7.5 %collective-permute-start.11 = (f32[16,896]{1,0:T(8,128)S(1)}, f32[16,896]{1,0:T(8,128)S(1)}, u32[]{:S(2)}, u32[]{:S(2)}) collective-permute-start(f32[16,896]{1,0:T(8,128)S(1)} %add.32), channel_id=1, source_target_pairs={{0,5},{1,4},{2,7},{3,6},{4,1},{5,0},{6,3},{7,2},{8,13},{9,12},{10,... | collective-permute-start | bytes 172040 | tf_op jit(solution)/shard_map/ppermute | solution.py:177
  28.1 9.6 %collective-permute-start.20 = (f32[16,896]{1,0:T(8,128)S(1)}, f32[16,896]{1,0:T(8,128)S(1)}, u32[]{:S(2)}, u32[]{:S(2)}) collective-permute-start(f32[16,896]{1,0:T(8,128)S(1)} %add.34), channel_id=1, source_target_pairs={{0,5},{1,4},{2,7},{3,6},{4,1},{5,0},{6,3},{7,2},{8,13},{9,12},{10,... | collective-permute-start | bytes 172040 | tf_op jit(solution)/shard_map/ppermute | solution.py:177
  34.3 3.9 %collective-permute-start.15 = (f32[16,896]{1,0:T(8,128)S(1)}, f32[16,896]{1,0:T(8,128)S(1)}, u32[]{:S(2)}, u32[]{:S(2)}) collective-permute-start(f32[16,896]{1,0:T(8,128)S(1)} %add.33.refs_0_), channel_id=1, source_target_pairs={{0,1},{1,0},{2,3},{3,2},{4,5},{5,4},{6,7},{7,6},{8,9},{9,8},{10,11... | collective-permute-start | bytes 172040 | tf_op jit(solution)/shard_map/ppermute | solution.py:180
  34.8 4.2 %collective-permute-start.14 = (f32[16,896]{1,0:T(8,128)S(1)}, f32[16,896]{1,0:T(8,128)S(1)}, u32[]{:S(2)}, u32[]{:S(2)}) collective-permute-start(f32[16,896]{1,0:T(8,128)S(1)} %add.33.refs_0_), channel_id=1, source_target_pairs={{0,24},{1,25},{2,26},{3,27},{4,28},{5,29},{6,30},{7,31},{8,16},{9,... | collective-permute-start | bytes 172040 | tf_op jit(solution)/shard_map/ppermute | solution.py:177
  35.3 5.5 %collective-permute-start.13 = (f32[16,896]{1,0:T(8,128)S(1)}, f32[16,896]{1,0:T(8,128)S(1)}, u32[]{:S(2)}, u32[]{:S(2)}) collective-permute-start(f32[16,896]{1,0:T(8,128)S(1)} %add.33.refs_0_), channel_id=1, source_target_pairs={{0,17},{1,16},{2,19},{3,18},{4,21},{5,20},{6,23},{7,22},{8,25},{9,... | collective-permute-start | bytes 172040 | tf_op jit(solution)/shard_map/ppermute | solution.py:177
  36.6 4.6 %collective-permute-start.12 = (f32[16,896]{1,0:T(8,128)S(1)}, f32[16,896]{1,0:T(8,128)S(1)}, u32[]{:S(2)}, u32[]{:S(2)}) collective-permute-start(f32[16,896]{1,0:T(8,128)S(1)} %add.33.refs_0_), channel_id=1, source_target_pairs={{0,9},{1,8},{2,11},{3,10},{4,13},{5,12},{6,15},{7,14},{8,1},{9,0},... | collective-permute-start | bytes 172040 | tf_op jit(solution)/shard_map/ppermute | solution.py:177
  37.7 3.8 %collective-permute-start.24 = (f32[16,896]{1,0:T(8,128)S(1)}, f32[16,896]{1,0:T(8,128)S(1)}, u32[]{:S(2)}, u32[]{:S(2)}) collective-permute-start(f32[16,896]{1,0:T(8,128)S(1)} %add.35.refs_8_), channel_id=1, source_target_pairs={{0,1},{1,0},{2,3},{3,2},{4,5},{5,4},{6,7},{7,6},{8,9},{9,8},{10,11... | collective-permute-start | bytes 172040 | tf_op jit(solution)/shard_map/ppermute | solution.py:180
  38.2 4.3 %collective-permute-start.23 = (f32[16,896]{1,0:T(8,128)S(1)}, f32[16,896]{1,0:T(8,128)S(1)}, u32[]{:S(2)}, u32[]{:S(2)}) collective-permute-start(f32[16,896]{1,0:T(8,128)S(1)} %add.35.refs_8_), channel_id=1, source_target_pairs={{0,24},{1,25},{2,26},{3,27},{4,28},{5,29},{6,30},{7,31},{8,16},{9,... | collective-permute-start | bytes 172040 | tf_op jit(solution)/shard_map/ppermute | solution.py:177
  39.0 5.2 %collective-permute-start.22 = (f32[16,896]{1,0:T(8,128)S(1)}, f32[16,896]{1,0:T(8,128)S(1)}, u32[]{:S(2)}, u32[]{:S(2)}) collective-permute-start(f32[16,896]{1,0:T(8,128)S(1)} %add.35.refs_8_), channel_id=1, source_target_pairs={{0,17},{1,16},{2,19},{3,18},{4,21},{5,20},{6,23},{7,22},{8,25},{9,... | collective-permute-start | bytes 172040 | tf_op jit(solution)/shard_map/ppermute | solution.py:177
  40.8 3.9 %collective-permute-start.21 = (f32[16,896]{1,0:T(8,128)S(1)}, f32[16,896]{1,0:T(8,128)S(1)}, u32[]{:S(2)}, u32[]{:S(2)}) collective-permute-start(f32[16,896]{1,0:T(8,128)S(1)} %add.35.refs_8_), channel_id=1, source_target_pairs={{0,9},{1,8},{2,11},{3,10},{4,13},{5,12},{6,15},{7,14},{8,1},{9,0},... | collective-permute-start | bytes 172040 | tf_op jit(solution)/shard_map/ppermute | solution.py:177
  41.2 3.9 %collective-permute-start.18 = (f32[16,896]{1,0:T(8,128)S(1)}, f32[16,896]{1,0:T(8,128)S(1)}, u32[]{:S(2)}, u32[]{:S(2)}) collective-permute-start(f32[16,896]{1,0:T(8,128)S(1)} %collective-permute-done.14.refs_3_), channel_id=1, source_target_pairs={{0,1},{1,0},{2,3},{3,2},{4,5},{5,4},{6,7},{7,6},{8,9},{9,8},{10,11... | collective-permute-start | bytes 172040 | tf_op jit(solution)/shard_map/ppermute | solution.py:180
  41.5 3.8 %collective-permute-start.17 = (f32[16,896]{1,0:T(8,128)S(1)}, f32[16,896]{1,0:T(8,128)S(1)}, u32[]{:S(2)}, u32[]{:S(2)}) collective-permute-start(f32[16,896]{1,0:T(8,128)S(1)} %collective-permute-done.13.refs_2_), channel_id=1, source_target_pairs={{0,1},{1,0},{2,3},{3,2},{4,5},{5,4},{6,7},{7,6},{8,9},{9,8},{10,11... | collective-permute-start | bytes 172040 | tf_op jit(solution)/shard_map/ppermute | solution.py:180
  42.5 2.8 %collective-permute-start.16 = (f32[16,896]{1,0:T(8,128)S(1)}, f32[16,896]{1,0:T(8,128)S(1)}, u32[]{:S(2)}, u32[]{:S(2)}) collective-permute-start(f32[16,896]{1,0:T(8,128)S(1)} %collective-permute-done.12.refs_1_), channel_id=1, source_target_pairs={{0,1},{1,0},{2,3},{3,2},{4,5},{5,4},{6,7},{7,6},{8,9},{9,8},{10,11... | collective-permute-start | bytes 172040 | tf_op jit(solution)/shard_map/ppermute | solution.py:180
  44.2 1.3 %collective-permute-start.27 = (f32[16,896]{1,0:T(8,128)S(1)}, f32[16,896]{1,0:T(8,128)S(1)}, u32[]{:S(2)}, u32[]{:S(2)}) collective-permute-start(f32[16,896]{1,0:T(8,128)S(1)} %collective-permute-done.23.refs_11_), channel_id=1, source_target_pairs={{0,1},{1,0},{2,3},{3,2},{4,5},{5,4},{6,7},{7,6},{8,9},{9,8},{10,11... | collective-permute-start | bytes 172040 | tf_op jit(solution)/shard_map/ppermute | solution.py:180
  44.8 1.3 %collective-permute-start.26 = (f32[16,896]{1,0:T(8,128)S(1)}, f32[16,896]{1,0:T(8,128)S(1)}, u32[]{:S(2)}, u32[]{:S(2)}) collective-permute-start(f32[16,896]{1,0:T(8,128)S(1)} %collective-permute-done.22.refs_10_), channel_id=1, source_target_pairs={{0,1},{1,0},{2,3},{3,2},{4,5},{5,4},{6,7},{7,6},{8,9},{9,8},{10,11... | collective-permute-start | bytes 172040 | tf_op jit(solution)/shard_map/ppermute | solution.py:180
  45.2 1.2 %collective-permute-start.25 = (f32[16,896]{1,0:T(8,128)S(1)}, f32[16,896]{1,0:T(8,128)S(1)}, u32[]{:S(2)}, u32[]{:S(2)}) collective-permute-start(f32[16,896]{1,0:T(8,128)S(1)} %collective-permute-done.21.refs_9_), channel_id=1, source_target_pairs={{0,1},{1,0},{2,3},{3,2},{4,5},{5,4},{6,7},{7,6},{8,9},{9,8},{10,11... | collective-permute-start | bytes 172040 | tf_op jit(solution)/shard_map/ppermute | solution.py:180

commit v4 on v3

--- a/solution.py
+++ b/solution.py
@@ -12,19 +12,20 @@
 AXES = ("local", "dp")
 F32, BF16 = jnp.float32, jnp.bfloat16
 VMEM = pltpu.VMEM
-PIECES = 4
 PARTS = 2
 
 
-def call(kernel, outs, *args, flops=1 << 20, limit=12, scratch=(), space=VMEM):
+def call(kernel, outs, *args, flops=1 << 20, limit=12, scratch=(), space=VMEM, target=VMEM, aliased=0):
     many = isinstance(outs, list)
     shapes = [jax.ShapeDtypeStruct(s, d) for s, d in (outs if many else [outs])]
     size = sum(a.size * a.dtype.itemsize for a in args)
+    plain = len(args) - aliased
     result = pl.pallas_call(
         kernel,
         out_shape=shapes,
-        in_specs=[pl.BlockSpec(memory_space=space)] * len(args),
-        out_specs=[pl.BlockSpec(memory_space=VMEM)] * len(shapes),
+        in_specs=[pl.BlockSpec(memory_space=space)] * plain + [pl.BlockSpec(memory_space=target)] * aliased,
+        out_specs=[pl.BlockSpec(memory_space=target)] * len(shapes),
+        input_output_aliases={plain + i: i for i in range(aliased)},
         scratch_shapes=scratch,
         compiler_params=pltpu.CompilerParams(vmem_limit_bytes=limit << 20),
         cost_estimate=pl.CostEstimate(flops=flops, bytes_accessed=size, transcendentals=0),
@@ -56,46 +57,40 @@
     return (place % 2 + odd_bits(lax.axis_index("local"), local) + odd_bits(place // 2, dp // 2)) % 2
 
 
-def left_kernel(g, f, b, left, merged, send, gv, fv, bv, sems):
+def load_kernel(g, f, gv, fv, send, sems):
+    copies = [pltpu.make_async_copy(x, y, sems.at[i]) for i, (x, y) in enumerate(((g, gv), (f, fv)))]
+    for copy in copies:
+        copy.start()
+    for copy in copies:
+        copy.wait()
+    width = send.shape[1]
+    half = own_half()
+    for side in range(2):
+
+        @pl.when(half == 1 - side)
+        def _():
+            span = slice(side * width, (side + 1) * width)
+            send[...] = gv[:, span].astype(F32) + fv[:, span].astype(F32)
+
+
+def left_kernel(g, f, b, left):
     rank = b.shape[0]
-    pieces = sems.shape[1]
-    width = g.shape[1] // pieces
-    half = own_half()
-    spans, copies = [], []
-    for i in range(pieces):
-        piece = (half * (pieces // 2) + i + pieces // 2) % pieces
-        span = pl.ds(pl.multiple_of(piece * width, 128), width)
-        spans.append(span)
-        for j, (source, target) in enumerate(((g, gv), (f, fv), (b, bv))):
-            copy = pltpu.make_async_copy(source.at[:, span], target.at[:, span], sems.at[j, i])
-            copy.start()
-            copies.append(copy)
+    high, low = split(b[...])
+    basis = jnp.concatenate([high, low], axis=0)
     dims = (((1,), (1,)), ((), ()))
-    total = None
-    for i, span in enumerate(spans):
-        for copy in copies[3 * i : 3 * i + 3]:
-            copy.wait()
-        high, low = split(bv[:, span])
-        basis = jnp.concatenate([high, low], axis=0)
-        one, two = gv[:, span], fv[:, span]
-        part = lax.dot_general(basis, one, dims, preferred_element_type=F32)
-        part += lax.dot_general(basis, two, dims, preferred_element_type=F32)
-        total = part if total is None else total + part
-        both = one.astype(F32) + two.astype(F32)
-        merged[:, span] = both
-        if i < pieces // 2:
-            send[:, i * width : (i + 1) * width] = both
-    left[...] = total[:rank] + total[rank:]
-
-
-def pair_kernel(merged, got, *outs):
+    both = lax.dot_general(basis, g[...], dims, preferred_element_type=F32)
+    both += lax.dot_general(basis, f[...], dims, preferred_element_type=F32)
+    left[...] = both[:rank] + both[rank:]
+
+
+def pair_kernel(g, f, got, *outs):
     width = outs[0].shape[1]
     mine = lax.axis_index("local")
     start = own_half() * got.shape[1]
     for step, out in enumerate(outs):
         inner = pl.multiple_of(partner(mine, step, len(outs)) * width, 128)
         span = pl.ds(pl.multiple_of(start + inner, 128), width)
-        out[...] = merged[:, span] + got[:, pl.ds(inner, width)]
+        out[...] = g[:, span].astype(F32) + f[:, span].astype(F32) + got[:, pl.ds(inner, width)]
 
 
 def gram_schmidt_kernel(block, a, b, basis, basis_t):
@@ -133,25 +128,37 @@
         out[...] = both[i * size : (i + 1) * size]
 
 
-def final_kernel(workers, merged, basis, *refs):
-    *blocks, feedback, new_basis_t = refs
-    count = len(blocks) // PARTS
-    chunks = count // 2
-    width = blocks[0].shape[1]
+def final_kernel(workers, other, g, f, basis, *refs):
+    feedback, new_basis_t, staged, sems = refs[-4:]
+    blocks = refs[: len(refs) - (6 if other else 4)]
+    chunks = len(blocks) // PARTS
+    size, width = blocks[0].shape
     mine = lax.axis_index("local")
-    half = own_half()
+    side = (own_half() + other) % 2
     high, low = split(basis[...] * (1.0 / workers))
     left = jnp.concatenate([high, low, high], axis=1)
-    for i in range(count):
-        side = half if i < chunks else 1 - half
-        start = (side * chunks + partner(mine, i % chunks, chunks)) * width
-        span = pl.ds(pl.multiple_of(start, 128), width)
-        piece = jnp.concatenate([block[...] for block in blocks[i::count]], axis=0)
-        new_basis_t[:, span] = piece
-        upper, lower = split(piece)
+    copies = []
+
+    def put(source, target, i, j):
+        copies.append(pltpu.make_async_copy(source, target, sems.at[i, j]))
+        copies[-1].start()
+
+    spans = []
+    for i in range(chunks):
+        start = (side * chunks + partner(mine, i, chunks)) * width
+        spans.append(pl.ds(pl.multiple_of(start, 128), width))
+        for part in range(PARTS):
+            rows = pl.ds(part * size, size)
+            put(blocks[part * chunks + i], new_basis_t.at[rows, spans[i]], i, part)
+    for i, span in enumerate(spans):
+        upper, lower = split(jnp.concatenate([block[...] for block in blocks[i::chunks]], axis=0))
         right = jnp.concatenate([upper, upper, lower], axis=0)
         approx = jnp.dot(left, right, preferred_element_type=F32)
-        feedback[:, span] = (merged[:, span] - approx).astype(BF16)
+        merged = g[:, span].astype(F32) + f[:, span].astype(F32)
+        staged[:, i * width : (i + 1) * width] = (merged - approx).astype(BF16)
+        put(staged.at[:, i * width : (i + 1) * width], feedback.at[:, span], i, PARTS)
+    for copy in copies:
+        copy.wait()
 
 
 def body(gradient, feedback, basis_in):
@@ -190,18 +197,16 @@
             step = 2 * step if double else step + 1
         return value
 
-    pieces = PIECES if columns % (128 * PIECES) == 0 else 2
-    g, f, b = (pltpu.with_memory_space_constraint(x, pltpu.HBM) for x in (g, f, b))
-    left, merged, send = call(
-        left_kernel, [((rank, rows), F32), ((rows, columns), F32), ((rows, half), F32)],
-        g, f, b, flops=1 << 27, limit=16,
-        scratch=[VMEM(g.shape, g.dtype), VMEM(f.shape, f.dtype), VMEM(b.shape, b.dtype),
-                 pltpu.SemaphoreType.DMA((3, pieces))],
-        space=pltpu.HBM,
+    g, f, send = call(
+        load_kernel,
+        [(g.shape, g.dtype), (f.shape, f.dtype), ((rows, half), F32)],
+        *(pltpu.with_memory_space_constraint(x, pltpu.HBM) for x in (g, f)),
+        scratch=[pltpu.SemaphoreType.DMA((2,))], space=pltpu.HBM,
     )
+    left = call(left_kernel, ((rank, rows), F32), g, f, b, flops=1 << 27)
     got = swap(send)
     left = total_over(left, True, direct=True)
-    chunks = call(pair_kernel, [((rows, width), F32)] * local, merged, got)
+    chunks = call(pair_kernel, [((rows, width), F32)] * local, g, f, got)
     terms = [chunks[0]] + [permute(chunks[s], True, s) for s in range(1, local)]
     left = total_over(left, False)
     basis, basis_t = call(
@@ -210,17 +215,21 @@
         left, swap(left), flops=1 << 26,
     )
     rights = call(right_kernel, [((rank // PARTS, width), F32)] * PARTS, basis_t, *terms, flops=1 << 25)
-    blocks = []
+    blocks, others = [], []
     for right in rights:
         own = total_over(right, False)
         gathered = [own] + [permute(own, True, s) for s in range(1, local)]
-        blocks += gathered + [swap(block) for block in gathered]
-    new_feedback, new_basis_t = call(
-        functools.partial(final_kernel, local * dp),
-        [((rows, columns), BF16), ((rank, columns), F32)],
-        merged, basis, *blocks, flops=1 << 27, limit=16,
-    )
-    return (new_feedback[None], new_basis_t.T)
+        blocks += gathered
+        others += [swap(block) for block in gathered]
+    outs = ()
+    for other, arrays in enumerate((blocks, others)):
+        outs = call(
+            functools.partial(final_kernel, local * dp, other),
+            [((rows, columns), BF16), ((rank, columns), F32)],
+            g, f, basis, *arrays, *outs, flops=1 << 27, aliased=len(outs), target=pltpu.HBM,
+            scratch=[VMEM((rows, half), BF16), pltpu.SemaphoreType.DMA((local, PARTS + 1))],
+        )
+    return (outs[0][None], outs[1].T)
 
 
 def solution(mesh):

time: 48.2 us -> 47.4 us (0.983)
  waiting for transfers between devices: 20.4 us -> 19.3 us
    ppermute x10, waiting for transfers between devices: 2.31 us -> 1.2 us  [swap(): return lax.ppermute(value, AXES, [(i, i ^ 1) for i in range(local * dp)])]
    pallas_call x5 -> x7, Pallas kernels: 6.69 us -> 7 us  [call(): pl.pallas_call(kernel, out_shape=shapes, in_specs=[pl.BlockSpec(memory_sp...]
  transfers between devices with their start and end apart: 28 -> 28, of which waited for: 14 -> 10; matrix products, arithmetic and copies ran while one was open for 0% -> 0% of each run, Pallas kernels for 4% -> 8%
where the time goes in v4:
time: 47.4 us; the launch traced here: 47.3 us
  starting transfers between devices  20.2 us (43%)
  waiting for transfers between devices  19.3 us (41%)
  Pallas kernels  7 us (15%)
  between operations  0.75 us (2%)
    ppermute x18, waiting for transfers between devices, permute(): return lax.ppermute(value, AXES, pairs)  18.1 us
    ppermute x18, starting transfers between devices, permute(): return lax.ppermute(value, AXES, pairs)  16.2 us
    pallas_call x7, Pallas kernels, call(): pl.pallas_call(kernel, out_shape=shapes, in_specs=[pl.BlockSpec(memory_sp...  7 us
    ppermute x10, starting transfers between devices, swap(): return lax.ppermute(value, AXES, [(i, i ^ 1) for i in range(local * dp)])  4.06 us
    ppermute x10, waiting for transfers between devices, swap(): return lax.ppermute(value, AXES, [(i, i ^ 1) for i in range(local * dp)])  1.2 us
  transfers between devices with their start and end apart: 28, of which 10 were waited for; matrix products, arithmetic and copies ran while one was open for 0% of the time, Pallas kernels for 8%

profile of v4, /device:TPU:27, one launch (start us, length us, event | category | flops | bytes accessed | tf_op | source)
XLA Modules:
  0.0 47.3 jit_solution(16370179783998227787)
XLA Ops:
  0.6 1.7 %shard_map.50 = (bf16[72,7168]{1,0:T(8,128)(2,1)S(1)}, bf16[72,7168]{1,0:T(8,128)(2,1)S(1)}, f32[72,3584]{1,0:T(8,128)S(1)}) custom-call(bf16[72,7168]{1,0:T(8,128)(2,1)} %bitcast.7, bf16[72,7168]{1,0:T(8,128)(2,1)} %bitcast.8), custom_call_target="tpu_custom_call" | custom-call | flops 1048576 | bytes 2064384 | tf_op jit(solution)/shard_map/pallas_call | solution.py:23
  2.4 0.7 %collective-permute-start.6 = (f32[72,3584]{1,0:T(8,128)S(1)}, f32[72,3584]{1,0:T(8,128)S(1)}, u32[]{:S(2)}, u32[]{:S(2)}) collective-permute-start(f32[72,3584]{1,0:T(8,128)S(1)} %get-tuple-element.21), channel_id=1, source_target_pairs={{0,1},{1,0},{2,3},{3,2},{4,5},{5,4},{6,7},{7,6},{8,9},{9,8},{10,11... | collective-permute-start | bytes 3096584 | tf_op jit(solution)/shard_map/ppermute | solution.py:187
  3.1 0.7 %shard_map.51 = f32[32,72]{1,0:T(8,128)S(1)} custom-call(bf16[72,7168]{1,0:T(8,128)(2,1)S(1)} %get-tuple-element.17.g, bf16[72,7168]{1,0:T(8,128)(2,1)S(1)} %get-tuple-element.18.f, f32[32,7168]{1,0:T(8,128)S(1)} %bitcast.5), custom_call_target="tpu_custom_call" | custom-call | flops 134217728 | bytes 2981888 | tf_op jit(solution)/shard_map/pallas_call | solution.py:23
  3.9 1.2 %collective-permute-start.2 = (f32[32,72]{1,0:T(8,128)S(1)}, f32[32,72]{1,0:T(8,128)S(1)}, u32[]{:S(2)}, u32[]{:S(2)}) collective-permute-start(f32[32,72]{1,0:T(8,128)S(1)} %shard_map.51), channel_id=1, source_target_pairs={{0,24},{1,25},{2,26},{3,27},{4,28},{5,29},{6,30},{7,31},{8,16},{9,... | collective-permute-start | bytes 27656 | tf_op jit(solution)/shard_map/ppermute | solution.py:184
  5.1 0.4 collective-permute-start.1
  5.5 1.3 %collective-permute-start = (f32[32,72]{1,0:T(8,128)S(1)}, f32[32,72]{1,0:T(8,128)S(1)}, u32[]{:S(2)}, u32[]{:S(2)}) collective-permute-start(f32[32,72]{1,0:T(8,128)S(1)} %shard_map.51), channel_id=1, source_target_pairs={{0,9},{1,8},{2,11},{3,10},{4,13},{5,12},{6,15},{7,14},{8,1},{9,0},... | collective-permute-start | bytes 27656 | tf_op jit(solution)/shard_map/ppermute | solution.py:184
  6.8 0.2 shard_map.53
  7.0 0.5 %collective-permute-start.7 = (f32[72,896]{1,0:T(8,128)S(1)}, f32[72,896]{1,0:T(8,128)S(1)}, u32[]{:S(2)}, u32[]{:S(2)}) collective-permute-start(f32[72,896]{1,0:T(8,128)S(1)} %get-tuple-element.23), channel_id=1, source_target_pairs={{0,9},{1,8},{2,11},{3,10},{4,13},{5,12},{6,15},{7,14},{8,1},{9,0},... | collective-permute-start | bytes 774152 | tf_op jit(solution)/shard_map/ppermute | solution.py:184
  7.5 1.3 %collective-permute-start.8 = (f32[72,896]{1,0:T(8,128)S(1)}, f32[72,896]{1,0:T(8,128)S(1)}, u32[]{:S(2)}, u32[]{:S(2)}) collective-permute-start(f32[72,896]{1,0:T(8,128)S(1)} %get-tuple-element.24), channel_id=1, source_target_pairs={{0,17},{1,16},{2,19},{3,18},{4,21},{5,20},{6,23},{7,22},{8,25},{9,... | collective-permute-start | bytes 774152 | tf_op jit(solution)/shard_map/ppermute | solution.py:184
  8.8 1.2 %collective-permute-start.9 = (f32[72,896]{1,0:T(8,128)S(1)}, f32[72,896]{1,0:T(8,128)S(1)}, u32[]{:S(2)}, u32[]{:S(2)}) collective-permute-start(f32[72,896]{1,0:T(8,128)S(1)} %get-tuple-element.25), channel_id=1, source_target_pairs={{0,24},{1,25},{2,26},{3,27},{4,28},{5,29},{6,30},{7,31},{8,16},{9,... | collective-permute-start | bytes 774152 | tf_op jit(solution)/shard_map/ppermute | solution.py:184
  10.0 0.0 collective-permute-done
  10.0 0.7 %collective-permute-start.3 = (f32[32,72]{1,0:T(8,128)S(1)}, f32[32,72]{1,0:T(8,128)S(1)}, u32[]{:S(2)}, u32[]{:S(2)}) collective-permute-start(f32[32,72]{1,0:T(8,128)S(1)} %add_add_fusion), channel_id=1, source_target_pairs={{0,3},{1,2},{2,1},{3,0},{4,7},{5,6},{6,5},{7,4},{8,11},{9,10},{10,... | collective-permute-start | bytes 27656 | tf_op jit(solution)/shard_map/ppermute | solution.py:184
  10.7 2.9 %collective-permute-done.3 = f32[32,72]{1,0:T(8,128)S(1)} collective-permute-done((f32[32,72]{1,0:T(8,128)S(1)}, f32[32,72]{1,0:T(8,128)S(1)}, u32[]{:S(2)}, u32[]{:S(2)}) %collective-permute-start.3) | collective-permute-done | bytes 9248 | tf_op jit(solution)/shard_map/ppermute | solution.py:184
  13.6 0.2 collective-permute-start.4
  13.8 4.2 %collective-permute-done.4 = f32[32,72]{1,0:T(8,128)S(1)} collective-permute-done((f32[32,72]{1,0:T(8,128)S(1)}, f32[32,72]{1,0:T(8,128)S(1)}, u32[]{:S(2)}, u32[]{:S(2)}) %collective-permute-start.4) | collective-permute-done | bytes 9248 | tf_op jit(solution)/shard_map/ppermute | solution.py:184
  18.0 1.2 %collective-permute-done.5.b = f32[32,72]{1,0:T(8,128)S(1)} collective-permute-done((f32[32,72]{1,0:T(8,128)S(1)}, f32[32,72]{1,0:T(8,128)S(1)}, u32[]{:S(2)}, u32[]{:S(2)}) %collective-permute-start.5) | collective-permute-done | bytes 9248 | tf_op jit(solution)/shard_map/ppermute | solution.py:187
  19.2 1.7 %shard_map.52 = (f32[72,32]{1,0:T(8,128)S(1)}, f32[32,72]{1,0:T(8,128)S(1)}) custom-call(f32[32,72]{1,0:T(8,128)S(1)} %add.31.a, f32[32,72]{1,0:T(8,128)S(1)} %collective-permute-done.5.b), custom_call_target="tpu_custom_call" | custom-call | flops 67108864 | bytes 18432 | tf_op jit(solution)/shard_map/pallas_call | solution.py:23
  20.9 0.0 collective-permute-done.7.refs_1_
  20.9 0.0 collective-permute-done.8.refs_2_
  21.0 0.6 %collective-permute-done.9.refs_3_ = f32[72,896]{1,0:T(8,128)S(1)} collective-permute-done((f32[72,896]{1,0:T(8,128)S(1)}, f32[72,896]{1,0:T(8,128)S(1)}, u32[]{:S(2)}, u32[]{:S(2)}) %collective-permute-start.9) | collective-permute-done | bytes 258080 | tf_op jit(solution)/shard_map/ppermute | solution.py:184
  21.5 0.3 shard_map.54
  21.8 0.9 %collective-permute-start.10 = (f32[16,896]{1,0:T(8,128)S(1)}, f32[16,896]{1,0:T(8,128)S(1)}, u32[]{:S(2)}, u32[]{:S(2)}) collective-permute-start(f32[16,896]{1,0:T(8,128)S(1)} %get-tuple-element.26), channel_id=1, source_target_pairs={{0,3},{1,2},{2,1},{3,0},{4,7},{5,6},{6,5},{7,4},{8,11},{9,10},{10,... | collective-permute-start | bytes 172040 | tf_op jit(solution)/shard_map/ppermute | solution.py:184
  22.7 0.9 %collective-permute-start.19 = (f32[16,896]{1,0:T(8,128)S(1)}, f32[16,896]{1,0:T(8,128)S(1)}, u32[]{:S(2)}, u32[]{:S(2)}) collective-permute-start(f32[16,896]{1,0:T(8,128)S(1)} %get-tuple-element.27), channel_id=1, source_target_pairs={{0,3},{1,2},{2,1},{3,0},{4,7},{5,6},{6,5},{7,4},{8,11},{9,10},{10,... | collective-permute-start | bytes 172040 | tf_op jit(solution)/shard_map/ppermute | solution.py:184
  23.6 2.6 %collective-permute-done.10 = f32[16,896]{1,0:T(8,128)S(1)} collective-permute-done((f32[16,896]{1,0:T(8,128)S(1)}, f32[16,896]{1,0:T(8,128)S(1)}, u32[]{:S(2)}, u32[]{:S(2)}) %collective-permute-start.10) | collective-permute-done | bytes 57376 | tf_op jit(solution)/shard_map/ppermute | solution.py:184
  26.2 0.7 %collective-permute-start.11 = (f32[16,896]{1,0:T(8,128)S(1)}, f32[16,896]{1,0:T(8,128)S(1)}, u32[]{:S(2)}, u32[]{:S(2)}) collective-permute-start(f32[16,896]{1,0:T(8,128)S(1)} %add.32), channel_id=1, source_target_pairs={{0,5},{1,4},{2,7},{3,6},{4,1},{5,0},{6,3},{7,2},{8,13},{9,12},{10,... | collective-permute-start | bytes 172040 | tf_op jit(solution)/shard_map/ppermute | solution.py:184
  26.9 0.5 %collective-permute-done.19 = f32[16,896]{1,0:T(8,128)S(1)} collective-permute-done((f32[16,896]{1,0:T(8,128)S(1)}, f32[16,896]{1,0:T(8,128)S(1)}, u32[]{:S(2)}, u32[]{:S(2)}) %collective-permute-start.19) | collective-permute-done | bytes 57376 | tf_op jit(solution)/shard_map/ppermute | solution.py:184
  27.5 1.6 %collective-permute-start.20 = (f32[16,896]{1,0:T(8,128)S(1)}, f32[16,896]{1,0:T(8,128)S(1)}, u32[]{:S(2)}, u32[]{:S(2)}) collective-permute-start(f32[16,896]{1,0:T(8,128)S(1)} %add.34), channel_id=1, source_target_pairs={{0,5},{1,4},{2,7},{3,6},{4,1},{5,0},{6,3},{7,2},{8,13},{9,12},{10,... | collective-permute-start | bytes 172040 | tf_op jit(solution)/shard_map/ppermute | solution.py:184
  29.0 4.9 %collective-permute-done.11 = f32[16,896]{1,0:T(8,128)S(1)} collective-permute-done((f32[16,896]{1,0:T(8,128)S(1)}, f32[16,896]{1,0:T(8,128)S(1)}, u32[]{:S(2)}, u32[]{:S(2)}) %collective-permute-start.11) | collective-permute-done | bytes 57376 | tf_op jit(solution)/shard_map/ppermute | solution.py:184
  33.9 0.9 %collective-permute-start.17 = (f32[16,896]{1,0:T(8,128)S(1)}, f32[16,896]{1,0:T(8,128)S(1)}, u32[]{:S(2)}, u32[]{:S(2)}) collective-permute-start(f32[16,896]{1,0:T(8,128)S(1)} %add.33.refs_0_), channel_id=1, source_target_pairs={{0,24},{1,25},{2,26},{3,27},{4,28},{5,29},{6,30},{7,31},{8,16},{9,... | collective-permute-start | bytes 172040 | tf_op jit(solution)/shard_map/ppermute | solution.py:184
  34.9 1.0 %collective-permute-start.15 = (f32[16,896]{1,0:T(8,128)S(1)}, f32[16,896]{1,0:T(8,128)S(1)}, u32[]{:S(2)}, u32[]{:S(2)}) collective-permute-start(f32[16,896]{1,0:T(8,128)S(1)} %add.33.refs_0_), channel_id=1, source_target_pairs={{0,17},{1,16},{2,19},{3,18},{4,21},{5,20},{6,23},{7,22},{8,25},{9,... | collective-permute-start | bytes 172040 | tf_op jit(solution)/shard_map/ppermute | solution.py:184
  35.8 1.1 %collective-permute-start.13 = (f32[16,896]{1,0:T(8,128)S(1)}, f32[16,896]{1,0:T(8,128)S(1)}, u32[]{:S(2)}, u32[]{:S(2)}) collective-permute-start(f32[16,896]{1,0:T(8,128)S(1)} %add.33.refs_0_), channel_id=1, source_target_pairs={{0,9},{1,8},{2,11},{3,10},{4,13},{5,12},{6,15},{7,14},{8,1},{9,0},... | collective-permute-start | bytes 172040 | tf_op jit(solution)/shard_map/ppermute | solution.py:184
  36.9 0.7 %collective-permute-start.12 = (f32[16,896]{1,0:T(8,128)S(1)}, f32[16,896]{1,0:T(8,128)S(1)}, u32[]{:S(2)}, u32[]{:S(2)}) collective-permute-start(f32[16,896]{1,0:T(8,128)S(1)} %add.33.refs_0_), channel_id=1, source_target_pairs={{0,1},{1,0},{2,3},{3,2},{4,5},{5,4},{6,7},{7,6},{8,9},{9,8},{10,11... | collective-permute-start | bytes 172040 | tf_op jit(solution)/shard_map/ppermute | solution.py:187
  37.6 0.0 collective-permute-done.20
  37.6 0.7 %collective-permute-start.26 = (f32[16,896]{1,0:T(8,128)S(1)}, f32[16,896]{1,0:T(8,128)S(1)}, u32[]{:S(2)}, u32[]{:S(2)}) collective-permute-start(f32[16,896]{1,0:T(8,128)S(1)} %add.35.refs_4_), channel_id=1, source_target_pairs={{0,24},{1,25},{2,26},{3,27},{4,28},{5,29},{6,30},{7,31},{8,16},{9,... | collective-permute-start | bytes 172040 | tf_op jit(solution)/shard_map/ppermute | solution.py:184
  38.3 1.1 %collective-permute-start.24 = (f32[16,896]{1,0:T(8,128)S(1)}, f32[16,896]{1,0:T(8,128)S(1)}, u32[]{:S(2)}, u32[]{:S(2)}) collective-permute-start(f32[16,896]{1,0:T(8,128)S(1)} %add.35.refs_4_), channel_id=1, source_target_pairs={{0,17},{1,16},{2,19},{3,18},{4,21},{5,20},{6,23},{7,22},{8,25},{9,... | collective-permute-start | bytes 172040 | tf_op jit(solution)/shard_map/ppermute | solution.py:184
  39.4 0.6 %collective-permute-done.15.refs_2_ = f32[16,896]{1,0:T(8,128)S(1)} collective-permute-done((f32[16,896]{1,0:T(8,128)S(1)}, f32[16,896]{1,0:T(8,128)S(1)}, u32[]{:S(2)}, u32[]{:S(2)}) %collective-permute-start.15) | collective-permute-done | bytes 57376 | tf_op jit(solution)/shard_map/ppermute | solution.py:184
  40.0 0.6 %collective-permute-start.22 = (f32[16,896]{1,0:T(8,128)S(1)}, f32[16,896]{1,0:T(8,128)S(1)}, u32[]{:S(2)}, u32[]{:S(2)}) collective-permute-start(f32[16,896]{1,0:T(8,128)S(1)} %add.35.refs_4_), channel_id=1, source_target_pairs={{0,9},{1,8},{2,11},{3,10},{4,13},{5,12},{6,15},{7,14},{8,1},{9,0},... | collective-permute-start | bytes 172040 | tf_op jit(solution)/shard_map/ppermute | solution.py:184
  40.6 0.3 collective-permute-start.21
  40.9 0.2 collective-permute-start.18
  41.1 0.9 %collective-permute-done.26.refs_7_ = f32[16,896]{1,0:T(8,128)S(1)} collective-permute-done((f32[16,896]{1,0:T(8,128)S(1)}, f32[16,896]{1,0:T(8,128)S(1)}, u32[]{:S(2)}, u32[]{:S(2)}) %collective-permute-start.26) | collective-permute-done | bytes 57376 | tf_op jit(solution)/shard_map/ppermute | solution.py:184
  42.1 1.0 %collective-permute-start.16 = (f32[16,896]{1,0:T(8,128)S(1)}, f32[16,896]{1,0:T(8,128)S(1)}, u32[]{:S(2)}, u32[]{:S(2)}) collective-permute-start(f32[16,896]{1,0:T(8,128)S(1)} %collective-permute-done.15.refs_2_), channel_id=1, source_target_pairs={{0,1},{1,0},{2,3},{3,2},{4,5},{5,4},{6,7},{7,6},{8,9},{9,8},{10,11... | collective-permute-start | bytes 172040 | tf_op jit(solution)/shard_map/ppermute | solution.py:187
  43.0 0.7 %collective-permute-done.24.refs_6_ = f32[16,896]{1,0:T(8,128)S(1)} collective-permute-done((f32[16,896]{1,0:T(8,128)S(1)}, f32[16,896]{1,0:T(8,128)S(1)}, u32[]{:S(2)}, u32[]{:S(2)}) %collective-permute-start.24) | collective-permute-done | bytes 57376 | tf_op jit(solution)/shard_map/ppermute | solution.py:184
  43.7 0.4 collective-permute-start.14
  44.2 0.2 collective-permute-start.27
  44.4 0.3 collective-permute-start.25
  44.7 0.2 collective-permute-start.23
  44.9 1.1 %shard_map.55 = (bf16[72,7168]{1,0:T(8,128)(2,1)}, f32[32,7168]{1,0:T(8,128)}) custom-call(bf16[72,7168]{1,0:T(8,128)(2,1)S(1)} %get-tuple-element.17.g, bf16[72,7168]{1,0:T(8,128)(2,1)S(1)} %get-tuple-element.18.f, f32[72,32]{1,0:T(8,128)S(1)} %get-tuple-element.19.basis, f32[16,896]{1,0:T(8,128)S(1)} %add.33.refs_0_, ...), custom_call_target="tpu_custom_call" | custom-call | flops 134217728 | bytes 2532352 | tf_op jit(solution)/shard_map/pallas_call | solution.py:23
  46.1 1.2 %shard_map.56 = (bf16[72,7168]{1,0:T(8,128)(2,1)}, f32[32,7168]{1,0:T(8,128)}) custom-call(bf16[72,7168]{1,0:T(8,128)(2,1)S(1)} %get-tuple-element.17.g, bf16[72,7168]{1,0:T(8,128)(2,1)S(1)} %get-tuple-element.18.f, f32[72,32]{1,0:T(8,128)S(1)} %get-tuple-element.19.basis, ...), custom_call_target="tpu_custom_call", output_to_operand_aliasing={{0}: (11, {}), {1}: (12, {})} | custom-call | flops 134217728 | bytes 4482048 | tf_op jit(solution)/shard_map/pallas_call | solution.py:23
  (24 shorter events, 0.1 us)
Async XLA Ops:
  0.6 2.5 %copy-start = (f32[7168,32]{0,1:T(8,128)S(1)}, f32[7168,32]{0,1:T(8,128)}, u32[]{:S(2)}) copy-start(f32[7168,32]{0,1:T(8,128)} %param.5) | copy-start | bytes 2752516
  2.4 4.4 %collective-permute-start.6 = (f32[72,3584]{1,0:T(8,128)S(1)}, f32[72,3584]{1,0:T(8,128)S(1)}, u32[]{:S(2)}, u32[]{:S(2)}) collective-permute-start(f32[72,3584]{1,0:T(8,128)S(1)} %get-tuple-element.21), channel_id=1, source_target_pairs={{0,1},{1,0},{2,3},{3,2},{4,5},{5,4},{6,7},{7,6},{8,9},{9,8},{10,11... | collective-permute-start | bytes 3096584 | tf_op jit(solution)/shard_map/ppermute | solution.py:187
  3.9 5.0 %collective-permute-start.2 = (f32[32,72]{1,0:T(8,128)S(1)}, f32[32,72]{1,0:T(8,128)S(1)}, u32[]{:S(2)}, u32[]{:S(2)}) collective-permute-start(f32[32,72]{1,0:T(8,128)S(1)} %shard_map.51), channel_id=1, source_target_pairs={{0,24},{1,25},{2,26},{3,27},{4,28},{5,29},{6,30},{7,31},{8,16},{9,... | collective-permute-start | bytes 27656 | tf_op jit(solution)/shard_map/ppermute | solution.py:184
  5.1 4.9 %collective-permute-start.1 = (f32[32,72]{1,0:T(8,128)S(1)}, f32[32,72]{1,0:T(8,128)S(1)}, u32[]{:S(2)}, u32[]{:S(2)}) collective-permute-start(f32[32,72]{1,0:T(8,128)S(1)} %shard_map.51), channel_id=1, source_target_pairs={{0,17},{1,16},{2,19},{3,18},{4,21},{5,20},{6,23},{7,22},{8,25},{9,... | collective-permute-start | bytes 27656 | tf_op jit(solution)/shard_map/ppermute | solution.py:184
  5.5 4.5 %collective-permute-start = (f32[32,72]{1,0:T(8,128)S(1)}, f32[32,72]{1,0:T(8,128)S(1)}, u32[]{:S(2)}, u32[]{:S(2)}) collective-permute-start(f32[32,72]{1,0:T(8,128)S(1)} %shard_map.51), channel_id=1, source_target_pairs={{0,9},{1,8},{2,11},{3,10},{4,13},{5,12},{6,15},{7,14},{8,1},{9,0},... | collective-permute-start | bytes 27656 | tf_op jit(solution)/shard_map/ppermute | solution.py:184
  7.0 14.0 %collective-permute-start.7 = (f32[72,896]{1,0:T(8,128)S(1)}, f32[72,896]{1,0:T(8,128)S(1)}, u32[]{:S(2)}, u32[]{:S(2)}) collective-permute-start(f32[72,896]{1,0:T(8,128)S(1)} %get-tuple-element.23), channel_id=1, source_target_pairs={{0,9},{1,8},{2,11},{3,10},{4,13},{5,12},{6,15},{7,14},{8,1},{9,0},... | collective-permute-start | bytes 774152 | tf_op jit(solution)/shard_map/ppermute | solution.py:184
  7.5 13.5 %collective-permute-start.8 = (f32[72,896]{1,0:T(8,128)S(1)}, f32[72,896]{1,0:T(8,128)S(1)}, u32[]{:S(2)}, u32[]{:S(2)}) collective-permute-start(f32[72,896]{1,0:T(8,128)S(1)} %get-tuple-element.24), channel_id=1, source_target_pairs={{0,17},{1,16},{2,19},{3,18},{4,21},{5,20},{6,23},{7,22},{8,25},{9,... | collective-permute-start | bytes 774152 | tf_op jit(solution)/shard_map/ppermute | solution.py:184
  8.8 12.7 %collective-permute-start.9 = (f32[72,896]{1,0:T(8,128)S(1)}, f32[72,896]{1,0:T(8,128)S(1)}, u32[]{:S(2)}, u32[]{:S(2)}) collective-permute-start(f32[72,896]{1,0:T(8,128)S(1)} %get-tuple-element.25), channel_id=1, source_target_pairs={{0,24},{1,25},{2,26},{3,27},{4,28},{5,29},{6,30},{7,31},{8,16},{9,... | collective-permute-start | bytes 774152 | tf_op jit(solution)/shard_map/ppermute | solution.py:184
  10.0 3.6 %collective-permute-start.3 = (f32[32,72]{1,0:T(8,128)S(1)}, f32[32,72]{1,0:T(8,128)S(1)}, u32[]{:S(2)}, u32[]{:S(2)}) collective-permute-start(f32[32,72]{1,0:T(8,128)S(1)} %add_add_fusion), channel_id=1, source_target_pairs={{0,3},{1,2},{2,1},{3,0},{4,7},{5,6},{6,5},{7,4},{8,11},{9,10},{10,... | collective-permute-start | bytes 27656 | tf_op jit(solution)/shard_map/ppermute | solution.py:184
  13.6 4.4 %collective-permute-start.4 = (f32[32,72]{1,0:T(8,128)S(1)}, f32[32,72]{1,0:T(8,128)S(1)}, u32[]{:S(2)}, u32[]{:S(2)}) collective-permute-start(f32[32,72]{1,0:T(8,128)S(1)} %add.30), channel_id=1, source_target_pairs={{0,5},{1,4},{2,7},{3,6},{4,1},{5,0},{6,3},{7,2},{8,13},{9,12},{10,... | collective-permute-start | bytes 27656 | tf_op jit(solution)/shard_map/ppermute | solution.py:184
  18.0 1.2 %collective-permute-start.5 = (f32[32,72]{1,0:T(8,128)S(1)}, f32[32,72]{1,0:T(8,128)S(1)}, u32[]{:S(2)}, u32[]{:S(2)}) collective-permute-start(f32[32,72]{1,0:T(8,128)S(1)} %add.31.a), channel_id=1, source_target_pairs={{0,1},{1,0},{2,3},{3,2},{4,5},{5,4},{6,7},{7,6},{8,9},{9,8},{10,11... | collective-permute-start | bytes 27656 | tf_op jit(solution)/shard_map/ppermute | solution.py:187
  21.8 4.4 %collective-permute-start.10 = (f32[16,896]{1,0:T(8,128)S(1)}, f32[16,896]{1,0:T(8,128)S(1)}, u32[]{:S(2)}, u32[]{:S(2)}) collective-permute-start(f32[16,896]{1,0:T(8,128)S(1)} %get-tuple-element.26), channel_id=1, source_target_pairs={{0,3},{1,2},{2,1},{3,0},{4,7},{5,6},{6,5},{7,4},{8,11},{9,10},{10,... | collective-permute-start | bytes 172040 | tf_op jit(solution)/shard_map/ppermute | solution.py:184
  22.7 4.7 %collective-permute-start.19 = (f32[16,896]{1,0:T(8,128)S(1)}, f32[16,896]{1,0:T(8,128)S(1)}, u32[]{:S(2)}, u32[]{:S(2)}) collective-permute-start(f32[16,896]{1,0:T(8,128)S(1)} %get-tuple-element.27), channel_id=1, source_target_pairs={{0,3},{1,2},{2,1},{3,0},{4,7},{5,6},{6,5},{7,4},{8,11},{9,10},{10,... | collective-permute-start | bytes 172040 | tf_op jit(solution)/shard_map/ppermute | solution.py:184
  26.2 7.7 %collective-permute-start.11 = (f32[16,896]{1,0:T(8,128)S(1)}, f32[16,896]{1,0:T(8,128)S(1)}, u32[]{:S(2)}, u32[]{:S(2)}) collective-permute-start(f32[16,896]{1,0:T(8,128)S(1)} %add.32), channel_id=1, source_target_pairs={{0,5},{1,4},{2,7},{3,6},{4,1},{5,0},{6,3},{7,2},{8,13},{9,12},{10,... | collective-permute-start | bytes 172040 | tf_op jit(solution)/shard_map/ppermute | solution.py:184
  27.5 10.1 %collective-permute-start.20 = (f32[16,896]{1,0:T(8,128)S(1)}, f32[16,896]{1,0:T(8,128)S(1)}, u32[]{:S(2)}, u32[]{:S(2)}) collective-permute-start(f32[16,896]{1,0:T(8,128)S(1)} %add.34), channel_id=1, source_target_pairs={{0,5},{1,4},{2,7},{3,6},{4,1},{5,0},{6,3},{7,2},{8,13},{9,12},{10,... | collective-permute-start | bytes 172040 | tf_op jit(solution)/shard_map/ppermute | solution.py:184
  33.9 4.4 %collective-permute-start.17 = (f32[16,896]{1,0:T(8,128)S(1)}, f32[16,896]{1,0:T(8,128)S(1)}, u32[]{:S(2)}, u32[]{:S(2)}) collective-permute-start(f32[16,896]{1,0:T(8,128)S(1)} %add.33.refs_0_), channel_id=1, source_target_pairs={{0,24},{1,25},{2,26},{3,27},{4,28},{5,29},{6,30},{7,31},{8,16},{9,... | collective-permute-start | bytes 172040 | tf_op jit(solution)/shard_map/ppermute | solution.py:184
  34.9 5.2 %collective-permute-start.15 = (f32[16,896]{1,0:T(8,128)S(1)}, f32[16,896]{1,0:T(8,128)S(1)}, u32[]{:S(2)}, u32[]{:S(2)}) collective-permute-start(f32[16,896]{1,0:T(8,128)S(1)} %add.33.refs_0_), channel_id=1, source_target_pairs={{0,17},{1,16},{2,19},{3,18},{4,21},{5,20},{6,23},{7,22},{8,25},{9,... | collective-permute-start | bytes 172040 | tf_op jit(solution)/shard_map/ppermute | solution.py:184
  35.8 4.8 %collective-permute-start.13 = (f32[16,896]{1,0:T(8,128)S(1)}, f32[16,896]{1,0:T(8,128)S(1)}, u32[]{:S(2)}, u32[]{:S(2)}) collective-permute-start(f32[16,896]{1,0:T(8,128)S(1)} %add.33.refs_0_), channel_id=1, source_target_pairs={{0,9},{1,8},{2,11},{3,10},{4,13},{5,12},{6,15},{7,14},{8,1},{9,0},... | collective-permute-start | bytes 172040 | tf_op jit(solution)/shard_map/ppermute | solution.py:184
  36.9 4.0 %collective-permute-start.12 = (f32[16,896]{1,0:T(8,128)S(1)}, f32[16,896]{1,0:T(8,128)S(1)}, u32[]{:S(2)}, u32[]{:S(2)}) collective-permute-start(f32[16,896]{1,0:T(8,128)S(1)} %add.33.refs_0_), channel_id=1, source_target_pairs={{0,1},{1,0},{2,3},{3,2},{4,5},{5,4},{6,7},{7,6},{8,9},{9,8},{10,11... | collective-permute-start | bytes 172040 | tf_op jit(solution)/shard_map/ppermute | solution.py:187
  37.6 4.4 %collective-permute-start.26 = (f32[16,896]{1,0:T(8,128)S(1)}, f32[16,896]{1,0:T(8,128)S(1)}, u32[]{:S(2)}, u32[]{:S(2)}) collective-permute-start(f32[16,896]{1,0:T(8,128)S(1)} %add.35.refs_4_), channel_id=1, source_target_pairs={{0,24},{1,25},{2,26},{3,27},{4,28},{5,29},{6,30},{7,31},{8,16},{9,... | collective-permute-start | bytes 172040 | tf_op jit(solution)/shard_map/ppermute | solution.py:184
  38.3 5.4 %collective-permute-start.24 = (f32[16,896]{1,0:T(8,128)S(1)}, f32[16,896]{1,0:T(8,128)S(1)}, u32[]{:S(2)}, u32[]{:S(2)}) collective-permute-start(f32[16,896]{1,0:T(8,128)S(1)} %add.35.refs_4_), channel_id=1, source_target_pairs={{0,17},{1,16},{2,19},{3,18},{4,21},{5,20},{6,23},{7,22},{8,25},{9,... | collective-permute-start | bytes 172040 | tf_op jit(solution)/shard_map/ppermute | solution.py:184
  40.0 4.1 %collective-permute-start.22 = (f32[16,896]{1,0:T(8,128)S(1)}, f32[16,896]{1,0:T(8,128)S(1)}, u32[]{:S(2)}, u32[]{:S(2)}) collective-permute-start(f32[16,896]{1,0:T(8,128)S(1)} %add.35.refs_4_), channel_id=1, source_target_pairs={{0,9},{1,8},{2,11},{3,10},{4,13},{5,12},{6,15},{7,14},{8,1},{9,0},... | collective-permute-start | bytes 172040 | tf_op jit(solution)/shard_map/ppermute | solution.py:184
  40.6 3.7 %collective-permute-start.21 = (f32[16,896]{1,0:T(8,128)S(1)}, f32[16,896]{1,0:T(8,128)S(1)}, u32[]{:S(2)}, u32[]{:S(2)}) collective-permute-start(f32[16,896]{1,0:T(8,128)S(1)} %add.35.refs_4_), channel_id=1, source_target_pairs={{0,1},{1,0},{2,3},{3,2},{4,5},{5,4},{6,7},{7,6},{8,9},{9,8},{10,11... | collective-permute-start | bytes 172040 | tf_op jit(solution)/shard_map/ppermute | solution.py:187
  40.9 3.8 %collective-permute-start.18 = (f32[16,896]{1,0:T(8,128)S(1)}, f32[16,896]{1,0:T(8,128)S(1)}, u32[]{:S(2)}, u32[]{:S(2)}) collective-permute-start(f32[16,896]{1,0:T(8,128)S(1)} %collective-permute-done.17.refs_3_), channel_id=1, source_target_pairs={{0,1},{1,0},{2,3},{3,2},{4,5},{5,4},{6,7},{7,6},{8,9},{9,8},{10,11... | collective-permute-start | bytes 172040 | tf_op jit(solution)/shard_map/ppermute | solution.py:187
  42.1 4.0 %collective-permute-start.16 = (f32[16,896]{1,0:T(8,128)S(1)}, f32[16,896]{1,0:T(8,128)S(1)}, u32[]{:S(2)}, u32[]{:S(2)}) collective-permute-start(f32[16,896]{1,0:T(8,128)S(1)} %collective-permute-done.15.refs_2_), channel_id=1, source_target_pairs={{0,1},{1,0},{2,3},{3,2},{4,5},{5,4},{6,7},{7,6},{8,9},{9,8},{10,11... | collective-permute-start | bytes 172040 | tf_op jit(solution)/shard_map/ppermute | solution.py:187
  43.7 2.3 %collective-permute-start.14 = (f32[16,896]{1,0:T(8,128)S(1)}, f32[16,896]{1,0:T(8,128)S(1)}, u32[]{:S(2)}, u32[]{:S(2)}) collective-permute-start(f32[16,896]{1,0:T(8,128)S(1)} %collective-permute-done.13.refs_1_), channel_id=1, source_target_pairs={{0,1},{1,0},{2,3},{3,2},{4,5},{5,4},{6,7},{7,6},{8,9},{9,8},{10,11... | collective-permute-start | bytes 172040 | tf_op jit(solution)/shard_map/ppermute | solution.py:187
  44.2 1.9 %collective-permute-start.27 = (f32[16,896]{1,0:T(8,128)S(1)}, f32[16,896]{1,0:T(8,128)S(1)}, u32[]{:S(2)}, u32[]{:S(2)}) collective-permute-start(f32[16,896]{1,0:T(8,128)S(1)} %collective-permute-done.26.refs_7_), channel_id=1, source_target_pairs={{0,1},{1,0},{2,3},{3,2},{4,5},{5,4},{6,7},{7,6},{8,9},{9,8},{10,11... | collective-permute-start | bytes 172040 | tf_op jit(solution)/shard_map/ppermute | solution.py:187
  44.4 1.7 %collective-permute-start.25 = (f32[16,896]{1,0:T(8,128)S(1)}, f32[16,896]{1,0:T(8,128)S(1)}, u32[]{:S(2)}, u32[]{:S(2)}) collective-permute-start(f32[16,896]{1,0:T(8,128)S(1)} %collective-permute-done.24.refs_6_), channel_id=1, source_target_pairs={{0,1},{1,0},{2,3},{3,2},{4,5},{5,4},{6,7},{7,6},{8,9},{9,8},{10,11... | collective-permute-start | bytes 172040 | tf_op jit(solution)/shard_map/ppermute | solution.py:187
  44.7 1.4 %collective-permute-start.23 = (f32[16,896]{1,0:T(8,128)S(1)}, f32[16,896]{1,0:T(8,128)S(1)}, u32[]{:S(2)}, u32[]{:S(2)}) collective-permute-start(f32[16,896]{1,0:T(8,128)S(1)} %collective-permute-done.22.refs_5_), channel_id=1, source_target_pairs={{0,1},{1,0},{2,3},{3,2},{4,5},{5,4},{6,7},{7,6},{8,9},{9,8},{10,11... | collective-permute-start | bytes 172040 | tf_op jit(solution)/shard_map/ppermute | solution.py:187

commit v5 on v4

--- a/solution.py
+++ b/solution.py
@@ -128,11 +128,18 @@
         out[...] = both[i * size : (i + 1) * size]
 
 
+def pack_kernel(*refs):
+    *blocks, out = refs
+    size = blocks[0].shape[0]
+    for i, block in enumerate(blocks):
+        out[i * size : (i + 1) * size] = block[...]
+
+
 def final_kernel(workers, other, g, f, basis, *refs):
+    parts = refs[:PARTS]
     feedback, new_basis_t, staged, sems = refs[-4:]
-    blocks = refs[: len(refs) - (6 if other else 4)]
-    chunks = len(blocks) // PARTS
-    size, width = blocks[0].shape
+    chunks = sems.shape[0]
+    size, width = parts[0].shape[0] // chunks, parts[0].shape[1]
     mine = lax.axis_index("local")
     side = (own_half() + other) % 2
     high, low = split(basis[...] * (1.0 / workers))
@@ -147,11 +154,11 @@
     for i in range(chunks):
         start = (side * chunks + partner(mine, i, chunks)) * width
         spans.append(pl.ds(pl.multiple_of(start, 128), width))
-        for part in range(PARTS):
-            rows = pl.ds(part * size, size)
-            put(blocks[part * chunks + i], new_basis_t.at[rows, spans[i]], i, part)
+        for j, part in enumerate(parts):
+            put(part.at[pl.ds(i * size, size)], new_basis_t.at[pl.ds(j * size, size), spans[i]], i, j)
     for i, span in enumerate(spans):
-        upper, lower = split(jnp.concatenate([block[...] for block in blocks[i::chunks]], axis=0))
+        piece = jnp.concatenate([part[i * size : (i + 1) * size] for part in parts], axis=0)
+        upper, lower = split(piece)
         right = jnp.concatenate([upper, upper, lower], axis=0)
         approx = jnp.dot(left, right, preferred_element_type=F32)
         merged = g[:, span].astype(F32) + f[:, span].astype(F32)
@@ -196,6 +203,18 @@
             value = value + other
             step = 2 * step if double else step + 1
         return value
+
+    def gather(own, turn):
+        if local & (local - 1):
+            return [own] + [permute(own, True, s) for s in range(1, local)]
+        blocks = {0: own}
+        steps = [1 << i for i in range(local.bit_length() - 1)]
+        for step in steps[::-1] if turn else steps:
+            new = {}
+            for place, block in blocks.items():
+                new[place ^ step] = permute(block, True, step)
+            blocks.update(new)
+        return [blocks[place] for place in range(local)]
 
     g, f, send = call(
         load_kernel,
@@ -216,11 +235,11 @@
     )
     rights = call(right_kernel, [((rank // PARTS, width), F32)] * PARTS, basis_t, *terms, flops=1 << 25)
     blocks, others = [], []
-    for right in rights:
+    for part, right in enumerate(rights):
         own = total_over(right, False)
-        gathered = [own] + [permute(own, True, s) for s in range(1, local)]
-        blocks += gathered
-        others += [swap(block) for block in gathered]
+        gathered = gather(own, part % 2)
+        blocks.append(call(pack_kernel, ((local * own.shape[0], width), F32), *gathered))
+        others.append(swap(blocks[-1]))
     outs = ()
     for other, arrays in enumerate((blocks, others)):
         outs = call(

time: 47.4 us -> 47.2 us (level)
  the two profiles are of different devices: /device:TPU:27 before, /device:TPU:0 now
where the time goes in v5:
time: 47.2 us; the launch traced here: 47 us
  starting transfers between devices  25.2 us (53%)
  waiting for transfers between devices  14 us (30%)
  Pallas kernels  6.99 us (15%)
  between operations  0.72 us (2%)
    ppermute x18, starting transfers between devices, permute(): return lax.ppermute(value, AXES, pairs)  23.1 us
    ppermute x18, waiting for transfers between devices, permute(): return lax.ppermute(value, AXES, pairs)  13.2 us
    pallas_call x9, Pallas kernels, call(): pl.pallas_call(kernel, out_shape=shapes, in_specs=[pl.BlockSpec(memory_sp...  6.99 us
    ppermute x4, starting transfers between devices, swap(): return lax.ppermute(value, AXES, [(i, i ^ 1) for i in range(local * dp)])  2.16 us
  transfers between devices with their start and end apart: 22, of which 12 were waited for; matrix products, arithmetic and copies ran while one was open for 0% of the time, Pallas kernels for 8%

profile of v5, /device:TPU:0, one launch (start us, length us, event | category | flops | bytes accessed | tf_op | source)
XLA Modules:
  0.0 47.0 jit_solution(10030507435236033079)
XLA Ops:
  0.6 1.7 %shard_map.50 = (bf16[72,7168]{1,0:T(8,128)(2,1)S(1)}, bf16[72,7168]{1,0:T(8,128)(2,1)S(1)}, f32[72,3584]{1,0:T(8,128)S(1)}) custom-call(bf16[72,7168]{1,0:T(8,128)(2,1)} %bitcast.7, bf16[72,7168]{1,0:T(8,128)(2,1)} %bitcast.8), custom_call_target="tpu_custom_call" | custom-call | flops 1048576 | bytes 2064384 | tf_op jit(solution)/shard_map/pallas_call | solution.py:23
  2.4 0.6 %collective-permute-start.6 = (f32[72,3584]{1,0:T(8,128)S(1)}, f32[72,3584]{1,0:T(8,128)S(1)}, u32[]{:S(2)}, u32[]{:S(2)}) collective-permute-start(f32[72,3584]{1,0:T(8,128)S(1)} %get-tuple-element.21), channel_id=1, source_target_pairs={{0,1},{1,0},{2,3},{3,2},{4,5},{5,4},{6,7},{7,6},{8,9},{9,8},{10,11... | collective-permute-start | bytes 3096584 | tf_op jit(solution)/shard_map/ppermute | solution.py:194
  2.9 0.7 %shard_map.51 = f32[32,72]{1,0:T(8,128)S(1)} custom-call(bf16[72,7168]{1,0:T(8,128)(2,1)S(1)} %get-tuple-element.17.g, bf16[72,7168]{1,0:T(8,128)(2,1)S(1)} %get-tuple-element.18.f, f32[32,7168]{1,0:T(8,128)S(1)} %bitcast.5), custom_call_target="tpu_custom_call" | custom-call | flops 134217728 | bytes 2981888 | tf_op jit(solution)/shard_map/pallas_call | solution.py:23
  3.7 3.5 %collective-permute-start.2 = (f32[32,72]{1,0:T(8,128)S(1)}, f32[32,72]{1,0:T(8,128)S(1)}, u32[]{:S(2)}, u32[]{:S(2)}) collective-permute-start(f32[32,72]{1,0:T(8,128)S(1)} %shard_map.51), channel_id=1, source_target_pairs={{0,24},{1,25},{2,26},{3,27},{4,28},{5,29},{6,30},{7,31},{8,16},{9,... | collective-permute-start | bytes 27656 | tf_op jit(solution)/shard_map/ppermute | solution.py:191
  7.1 0.3 collective-permute-start.1
  7.5 0.0 collective-permute-start
  7.5 0.0 collective-permute-done.6.got
  7.5 0.2 shard_map.53
  7.7 1.8 %collective-permute-start.7 = (f32[72,896]{1,0:T(8,128)S(1)}, f32[72,896]{1,0:T(8,128)S(1)}, u32[]{:S(2)}, u32[]{:S(2)}) collective-permute-start(f32[72,896]{1,0:T(8,128)S(1)} %get-tuple-element.23), channel_id=1, source_target_pairs={{0,9},{1,8},{2,11},{3,10},{4,13},{5,12},{6,15},{7,14},{8,1},{9,0},... | collective-permute-start | bytes 774152 | tf_op jit(solution)/shard_map/ppermute | solution.py:191
  9.4 1.4 %collective-permute-start.8 = (f32[72,896]{1,0:T(8,128)S(1)}, f32[72,896]{1,0:T(8,128)S(1)}, u32[]{:S(2)}, u32[]{:S(2)}) collective-permute-start(f32[72,896]{1,0:T(8,128)S(1)} %get-tuple-element.24), channel_id=1, source_target_pairs={{0,17},{1,16},{2,19},{3,18},{4,21},{5,20},{6,23},{7,22},{8,25},{9,... | collective-permute-start | bytes 774152 | tf_op jit(solution)/shard_map/ppermute | solution.py:191
  10.9 0.9 %collective-permute-start.9 = (f32[72,896]{1,0:T(8,128)S(1)}, f32[72,896]{1,0:T(8,128)S(1)}, u32[]{:S(2)}, u32[]{:S(2)}) collective-permute-start(f32[72,896]{1,0:T(8,128)S(1)} %get-tuple-element.25), channel_id=1, source_target_pairs={{0,24},{1,25},{2,26},{3,27},{4,28},{5,29},{6,30},{7,31},{8,16},{9,... | collective-permute-start | bytes 774152 | tf_op jit(solution)/shard_map/ppermute | solution.py:191
  11.8 0.0 collective-permute-done.1
  11.8 0.0 collective-permute-done
  11.8 0.7 %collective-permute-start.3 = (f32[32,72]{1,0:T(8,128)S(1)}, f32[32,72]{1,0:T(8,128)S(1)}, u32[]{:S(2)}, u32[]{:S(2)}) collective-permute-start(f32[32,72]{1,0:T(8,128)S(1)} %add_add_fusion), channel_id=1, source_target_pairs={{0,3},{1,2},{2,1},{3,0},{4,7},{5,6},{6,5},{7,4},{8,11},{9,10},{10,... | collective-permute-start | bytes 27656 | tf_op jit(solution)/shard_map/ppermute | solution.py:191
  12.5 2.6 %collective-permute-done.3 = f32[32,72]{1,0:T(8,128)S(1)} collective-permute-done((f32[32,72]{1,0:T(8,128)S(1)}, f32[32,72]{1,0:T(8,128)S(1)}, u32[]{:S(2)}, u32[]{:S(2)}) %collective-permute-start.3) | collective-permute-done | bytes 9248 | tf_op jit(solution)/shard_map/ppermute | solution.py:191
  15.1 2.4 %collective-permute-start.4 = (f32[32,72]{1,0:T(8,128)S(1)}, f32[32,72]{1,0:T(8,128)S(1)}, u32[]{:S(2)}, u32[]{:S(2)}) collective-permute-start(f32[32,72]{1,0:T(8,128)S(1)} %add.30), channel_id=1, source_target_pairs={{0,5},{1,4},{2,7},{3,6},{4,1},{5,0},{6,3},{7,2},{8,13},{9,12},{10,... | collective-permute-start | bytes 27656 | tf_op jit(solution)/shard_map/ppermute | solution.py:191
  17.5 1.7 %collective-permute-done.4 = f32[32,72]{1,0:T(8,128)S(1)} collective-permute-done((f32[32,72]{1,0:T(8,128)S(1)}, f32[32,72]{1,0:T(8,128)S(1)}, u32[]{:S(2)}, u32[]{:S(2)}) %collective-permute-start.4) | collective-permute-done | bytes 9248 | tf_op jit(solution)/shard_map/ppermute | solution.py:191
  19.2 0.5 %collective-permute-start.5 = (f32[32,72]{1,0:T(8,128)S(1)}, f32[32,72]{1,0:T(8,128)S(1)}, u32[]{:S(2)}, u32[]{:S(2)}) collective-permute-start(f32[32,72]{1,0:T(8,128)S(1)} %add.31.a), channel_id=1, source_target_pairs={{0,1},{1,0},{2,3},{3,2},{4,5},{5,4},{6,7},{7,6},{8,9},{9,8},{10,11... | collective-permute-start | bytes 27656 | tf_op jit(solution)/shard_map/ppermute | solution.py:194
  19.7 0.8 %collective-permute-done.5.b = f32[32,72]{1,0:T(8,128)S(1)} collective-permute-done((f32[32,72]{1,0:T(8,128)S(1)}, f32[32,72]{1,0:T(8,128)S(1)}, u32[]{:S(2)}, u32[]{:S(2)}) %collective-permute-start.5) | collective-permute-done | bytes 9248 | tf_op jit(solution)/shard_map/ppermute | solution.py:194
  20.5 1.7 %shard_map.52 = (f32[72,32]{1,0:T(8,128)S(1)}, f32[32,72]{1,0:T(8,128)S(1)}) custom-call(f32[32,72]{1,0:T(8,128)S(1)} %add.31.a, f32[32,72]{1,0:T(8,128)S(1)} %collective-permute-done.5.b), custom_call_target="tpu_custom_call" | custom-call | flops 67108864 | bytes 18432 | tf_op jit(solution)/shard_map/pallas_call | solution.py:23
  22.3 0.0 collective-permute-done.7.refs_1_
  22.3 0.3 collective-permute-done.8.refs_2_
  22.5 0.7 %collective-permute-done.9.refs_3_ = f32[72,896]{1,0:T(8,128)S(1)} collective-permute-done((f32[72,896]{1,0:T(8,128)S(1)}, f32[72,896]{1,0:T(8,128)S(1)}, u32[]{:S(2)}, u32[]{:S(2)}) %collective-permute-start.9) | collective-permute-done | bytes 258080 | tf_op jit(solution)/shard_map/ppermute | solution.py:191
  23.3 0.3 shard_map.54
  23.6 1.3 %collective-permute-start.16 = (f32[16,896]{1,0:T(8,128)S(1)}, f32[16,896]{1,0:T(8,128)S(1)}, u32[]{:S(2)}, u32[]{:S(2)}) collective-permute-start(f32[16,896]{1,0:T(8,128)S(1)} %get-tuple-element.27), channel_id=1, source_target_pairs={{0,3},{1,2},{2,1},{3,0},{4,7},{5,6},{6,5},{7,4},{8,11},{9,10},{10,... | collective-permute-start | bytes 172040 | tf_op jit(solution)/shard_map/ppermute | solution.py:191
  24.8 0.5 %collective-permute-start.10 = (f32[16,896]{1,0:T(8,128)S(1)}, f32[16,896]{1,0:T(8,128)S(1)}, u32[]{:S(2)}, u32[]{:S(2)}) collective-permute-start(f32[16,896]{1,0:T(8,128)S(1)} %get-tuple-element.26), channel_id=1, source_target_pairs={{0,3},{1,2},{2,1},{3,0},{4,7},{5,6},{6,5},{7,4},{8,11},{9,10},{10,... | collective-permute-start | bytes 172040 | tf_op jit(solution)/shard_map/ppermute | solution.py:191
  25.3 2.2 %collective-permute-done.16 = f32[16,896]{1,0:T(8,128)S(1)} collective-permute-done((f32[16,896]{1,0:T(8,128)S(1)}, f32[16,896]{1,0:T(8,128)S(1)}, u32[]{:S(2)}, u32[]{:S(2)}) %collective-permute-start.16) | collective-permute-done | bytes 57376 | tf_op jit(solution)/shard_map/ppermute | solution.py:191
  27.6 2.3 %collective-permute-start.17 = (f32[16,896]{1,0:T(8,128)S(1)}, f32[16,896]{1,0:T(8,128)S(1)}, u32[]{:S(2)}, u32[]{:S(2)}) collective-permute-start(f32[16,896]{1,0:T(8,128)S(1)} %add.34), channel_id=1, source_target_pairs={{0,5},{1,4},{2,7},{3,6},{4,1},{5,0},{6,3},{7,2},{8,13},{9,12},{10,... | collective-permute-start | bytes 172040 | tf_op jit(solution)/shard_map/ppermute | solution.py:191
  29.9 0.0 collective-permute-done.10
  29.9 1.3 %collective-permute-start.11 = (f32[16,896]{1,0:T(8,128)S(1)}, f32[16,896]{1,0:T(8,128)S(1)}, u32[]{:S(2)}, u32[]{:S(2)}) collective-permute-start(f32[16,896]{1,0:T(8,128)S(1)} %add.32), channel_id=1, source_target_pairs={{0,5},{1,4},{2,7},{3,6},{4,1},{5,0},{6,3},{7,2},{8,13},{9,12},{10,... | collective-permute-start | bytes 172040 | tf_op jit(solution)/shard_map/ppermute | solution.py:191
  31.2 1.3 %collective-permute-done.17 = f32[16,896]{1,0:T(8,128)S(1)} collective-permute-done((f32[16,896]{1,0:T(8,128)S(1)}, f32[16,896]{1,0:T(8,128)S(1)}, u32[]{:S(2)}, u32[]{:S(2)}) %collective-permute-start.17) | collective-permute-done | bytes 57376 | tf_op jit(solution)/shard_map/ppermute | solution.py:191
  32.5 0.9 %collective-permute-start.19 = (f32[16,896]{1,0:T(8,128)S(1)}, f32[16,896]{1,0:T(8,128)S(1)}, u32[]{:S(2)}, u32[]{:S(2)}) collective-permute-start(f32[16,896]{1,0:T(8,128)S(1)} %add.35.refs_0_), channel_id=1, source_target_pairs={{0,17},{1,16},{2,19},{3,18},{4,21},{5,20},{6,23},{7,22},{8,25},{9,... | collective-permute-start | bytes 172040 | tf_op jit(solution)/shard_map/ppermute | solution.py:191
  33.3 1.4 %collective-permute-done.11 = f32[16,896]{1,0:T(8,128)S(1)} collective-permute-done((f32[16,896]{1,0:T(8,128)S(1)}, f32[16,896]{1,0:T(8,128)S(1)}, u32[]{:S(2)}, u32[]{:S(2)}) %collective-permute-start.11) | collective-permute-done | bytes 57376 | tf_op jit(solution)/shard_map/ppermute | solution.py:191
  34.8 2.8 %collective-permute-start.12 = (f32[16,896]{1,0:T(8,128)S(1)}, f32[16,896]{1,0:T(8,128)S(1)}, u32[]{:S(2)}, u32[]{:S(2)}) collective-permute-start(f32[16,896]{1,0:T(8,128)S(1)} %add.33.refs_0_), channel_id=1, source_target_pairs={{0,9},{1,8},{2,11},{3,10},{4,13},{5,12},{6,15},{7,14},{8,1},{9,0},... | collective-permute-start | bytes 172040 | tf_op jit(solution)/shard_map/ppermute | solution.py:191
  37.6 0.1 collective-permute-start.18
  37.7 0.0 collective-permute-done.19.refs_2_
  37.7 1.7 %collective-permute-start.20 = (f32[16,896]{1,0:T(8,128)S(1)}, f32[16,896]{1,0:T(8,128)S(1)}, u32[]{:S(2)}, u32[]{:S(2)}) collective-permute-start(f32[16,896]{1,0:T(8,128)S(1)} %collective-permute-done.19.refs_2_), channel_id=1, source_target_pairs={{0,9},{1,8},{2,11},{3,10},{4,13},{5,12},{6,15},{7,14},{8,1},{9,0},... | collective-permute-start | bytes 172040 | tf_op jit(solution)/shard_map/ppermute | solution.py:191
  39.4 0.0 collective-permute-start.13
  39.4 0.6 %collective-permute-done.12.refs_1_ = f32[16,896]{1,0:T(8,128)S(1)} collective-permute-done((f32[16,896]{1,0:T(8,128)S(1)}, f32[16,896]{1,0:T(8,128)S(1)}, u32[]{:S(2)}, u32[]{:S(2)}) %collective-permute-start.12) | collective-permute-done | bytes 57376 | tf_op jit(solution)/shard_map/ppermute | solution.py:191
  39.9 1.2 %collective-permute-start.14 = (f32[16,896]{1,0:T(8,128)S(1)}, f32[16,896]{1,0:T(8,128)S(1)}, u32[]{:S(2)}, u32[]{:S(2)}) collective-permute-start(f32[16,896]{1,0:T(8,128)S(1)} %collective-permute-done.12.refs_1_), channel_id=1, source_target_pairs={{0,17},{1,16},{2,19},{3,18},{4,21},{5,20},{6,23},{7,22},{8,25},{9,... | collective-permute-start | bytes 172040 | tf_op jit(solution)/shard_map/ppermute | solution.py:191
  41.1 0.2 collective-permute-done.18.refs_1_
  41.3 1.2 %collective-permute-done.20.refs_3_ = f32[16,896]{1,0:T(8,128)S(1)} collective-permute-done((f32[16,896]{1,0:T(8,128)S(1)}, f32[16,896]{1,0:T(8,128)S(1)}, u32[]{:S(2)}, u32[]{:S(2)}) %collective-permute-start.20) | collective-permute-done | bytes 57376 | tf_op jit(solution)/shard_map/ppermute | solution.py:191
  42.6 0.7 %collective-permute-start.21 = (f32[64,896]{1,0:T(8,128)S(1)}, f32[64,896]{1,0:T(8,128)S(1)}, u32[]{:S(2)}, u32[]{:S(2)}) collective-permute-start(f32[64,896]{1,0:T(8,128)S(1)} %shard_map.56.refs_1_), channel_id=1, source_target_pairs={{0,1},{1,0},{2,3},{3,2},{4,5},{5,4},{6,7},{7,6},{8,9},{9,8},{10,11... | collective-permute-start | bytes 688136 | tf_op jit(solution)/shard_map/ppermute | solution.py:194
  43.3 0.0 collective-permute-done.13.refs_2_
  43.3 1.0 %collective-permute-done.14.refs_3_ = f32[16,896]{1,0:T(8,128)S(1)} collective-permute-done((f32[16,896]{1,0:T(8,128)S(1)}, f32[16,896]{1,0:T(8,128)S(1)}, u32[]{:S(2)}, u32[]{:S(2)}) %collective-permute-start.14) | collective-permute-done | bytes 57376 | tf_op jit(solution)/shard_map/ppermute | solution.py:191
  44.3 0.4 collective-permute-start.15
  44.7 1.1 %shard_map.57 = (bf16[72,7168]{1,0:T(8,128)(2,1)}, f32[32,7168]{1,0:T(8,128)}) custom-call(bf16[72,7168]{1,0:T(8,128)(2,1)S(1)} %get-tuple-element.17.g, bf16[72,7168]{1,0:T(8,128)(2,1)S(1)} %get-tuple-element.18.f, f32[72,32]{1,0:T(8,128)S(1)} %get-tuple-element.19.basis, f32[64,896]{1,0:T(8,128)S(1)} %shard_map.55.refs_0_, f32[64,896]{1,0:T(8,128)S(1)} %shard_map.56.refs_1_), custom_call_target="tpu_custom_call" | custom-call | flops 134217728 | bytes 2532352 | tf_op jit(solution)/shard_map/pallas_call | solution.py:23
  45.9 1.2 %shard_map.58 = (bf16[72,7168]{1,0:T(8,128)(2,1)}, f32[32,7168]{1,0:T(8,128)}) custom-call(bf16[72,7168]{1,0:T(8,128)(2,1)S(1)} %get-tuple-element.17.g, bf16[72,7168]{1,0:T(8,128)(2,1)S(1)} %get-tuple-element.18.f, f32[72,32]{1,0:T(8,128)S(1)} %get-tuple-element.19.basis, ...), custom_call_target="tpu_custom_call", output_to_operand_aliasing={{0}: (5, {}), {1}: (6, {})} | custom-call | flops 134217728 | bytes 4482048 | tf_op jit(solution)/shard_map/pallas_call | solution.py:23
  (14 shorter events, 0.1 us)
Async XLA Ops:
  0.6 2.3 %copy-start = (f32[7168,32]{0,1:T(8,128)S(1)}, f32[7168,32]{0,1:T(8,128)}, u32[]{:S(2)}) copy-start(f32[7168,32]{0,1:T(8,128)} %param.5) | copy-start | bytes 2752516
  2.4 5.1 %collective-permute-start.6 = (f32[72,3584]{1,0:T(8,128)S(1)}, f32[72,3584]{1,0:T(8,128)S(1)}, u32[]{:S(2)}, u32[]{:S(2)}) collective-permute-start(f32[72,3584]{1,0:T(8,128)S(1)} %get-tuple-element.21), channel_id=1, source_target_pairs={{0,1},{1,0},{2,3},{3,2},{4,5},{5,4},{6,7},{7,6},{8,9},{9,8},{10,11... | collective-permute-start | bytes 3096584 | tf_op jit(solution)/shard_map/ppermute | solution.py:194
  3.7 7.2 %collective-permute-start.2 = (f32[32,72]{1,0:T(8,128)S(1)}, f32[32,72]{1,0:T(8,128)S(1)}, u32[]{:S(2)}, u32[]{:S(2)}) collective-permute-start(f32[32,72]{1,0:T(8,128)S(1)} %shard_map.51), channel_id=1, source_target_pairs={{0,24},{1,25},{2,26},{3,27},{4,28},{5,29},{6,30},{7,31},{8,16},{9,... | collective-permute-start | bytes 27656 | tf_op jit(solution)/shard_map/ppermute | solution.py:191
  7.1 4.7 %collective-permute-start.1 = (f32[32,72]{1,0:T(8,128)S(1)}, f32[32,72]{1,0:T(8,128)S(1)}, u32[]{:S(2)}, u32[]{:S(2)}) collective-permute-start(f32[32,72]{1,0:T(8,128)S(1)} %shard_map.51), channel_id=1, source_target_pairs={{0,17},{1,16},{2,19},{3,18},{4,21},{5,20},{6,23},{7,22},{8,25},{9,... | collective-permute-start | bytes 27656 | tf_op jit(solution)/shard_map/ppermute | solution.py:191
  7.5 4.3 %collective-permute-start = (f32[32,72]{1,0:T(8,128)S(1)}, f32[32,72]{1,0:T(8,128)S(1)}, u32[]{:S(2)}, u32[]{:S(2)}) collective-permute-start(f32[32,72]{1,0:T(8,128)S(1)} %shard_map.51), channel_id=1, source_target_pairs={{0,9},{1,8},{2,11},{3,10},{4,13},{5,12},{6,15},{7,14},{8,1},{9,0},... | collective-permute-start | bytes 27656 | tf_op jit(solution)/shard_map/ppermute | solution.py:191
  7.7 14.6 %collective-permute-start.7 = (f32[72,896]{1,0:T(8,128)S(1)}, f32[72,896]{1,0:T(8,128)S(1)}, u32[]{:S(2)}, u32[]{:S(2)}) collective-permute-start(f32[72,896]{1,0:T(8,128)S(1)} %get-tuple-element.23), channel_id=1, source_target_pairs={{0,9},{1,8},{2,11},{3,10},{4,13},{5,12},{6,15},{7,14},{8,1},{9,0},... | collective-permute-start | bytes 774152 | tf_op jit(solution)/shard_map/ppermute | solution.py:191
  9.4 13.1 %collective-permute-start.8 = (f32[72,896]{1,0:T(8,128)S(1)}, f32[72,896]{1,0:T(8,128)S(1)}, u32[]{:S(2)}, u32[]{:S(2)}) collective-permute-start(f32[72,896]{1,0:T(8,128)S(1)} %get-tuple-element.24), channel_id=1, source_target_pairs={{0,17},{1,16},{2,19},{3,18},{4,21},{5,20},{6,23},{7,22},{8,25},{9,... | collective-permute-start | bytes 774152 | tf_op jit(solution)/shard_map/ppermute | solution.py:191
  10.9 12.4 %collective-permute-start.9 = (f32[72,896]{1,0:T(8,128)S(1)}, f32[72,896]{1,0:T(8,128)S(1)}, u32[]{:S(2)}, u32[]{:S(2)}) collective-permute-start(f32[72,896]{1,0:T(8,128)S(1)} %get-tuple-element.25), channel_id=1, source_target_pairs={{0,24},{1,25},{2,26},{3,27},{4,28},{5,29},{6,30},{7,31},{8,16},{9,... | collective-permute-start | bytes 774152 | tf_op jit(solution)/shard_map/ppermute | solution.py:191
  11.8 3.3 %collective-permute-start.3 = (f32[32,72]{1,0:T(8,128)S(1)}, f32[32,72]{1,0:T(8,128)S(1)}, u32[]{:S(2)}, u32[]{:S(2)}) collective-permute-start(f32[32,72]{1,0:T(8,128)S(1)} %add_add_fusion), channel_id=1, source_target_pairs={{0,3},{1,2},{2,1},{3,0},{4,7},{5,6},{6,5},{7,4},{8,11},{9,10},{10,... | collective-permute-start | bytes 27656 | tf_op jit(solution)/shard_map/ppermute | solution.py:191
  15.1 4.1 %collective-permute-start.4 = (f32[32,72]{1,0:T(8,128)S(1)}, f32[32,72]{1,0:T(8,128)S(1)}, u32[]{:S(2)}, u32[]{:S(2)}) collective-permute-start(f32[32,72]{1,0:T(8,128)S(1)} %add.30), channel_id=1, source_target_pairs={{0,5},{1,4},{2,7},{3,6},{4,1},{5,0},{6,3},{7,2},{8,13},{9,12},{10,... | collective-permute-start | bytes 27656 | tf_op jit(solution)/shard_map/ppermute | solution.py:191
  19.2 1.4 %collective-permute-start.5 = (f32[32,72]{1,0:T(8,128)S(1)}, f32[32,72]{1,0:T(8,128)S(1)}, u32[]{:S(2)}, u32[]{:S(2)}) collective-permute-start(f32[32,72]{1,0:T(8,128)S(1)} %add.31.a), channel_id=1, source_target_pairs={{0,1},{1,0},{2,3},{3,2},{4,5},{5,4},{6,7},{7,6},{8,9},{9,8},{10,11... | collective-permute-start | bytes 27656 | tf_op jit(solution)/shard_map/ppermute | solution.py:194
  23.6 4.0 %collective-permute-start.16 = (f32[16,896]{1,0:T(8,128)S(1)}, f32[16,896]{1,0:T(8,128)S(1)}, u32[]{:S(2)}, u32[]{:S(2)}) collective-permute-start(f32[16,896]{1,0:T(8,128)S(1)} %get-tuple-element.27), channel_id=1, source_target_pairs={{0,3},{1,2},{2,1},{3,0},{4,7},{5,6},{6,5},{7,4},{8,11},{9,10},{10,... | collective-permute-start | bytes 172040 | tf_op jit(solution)/shard_map/ppermute | solution.py:191
  24.8 5.0 %collective-permute-start.10 = (f32[16,896]{1,0:T(8,128)S(1)}, f32[16,896]{1,0:T(8,128)S(1)}, u32[]{:S(2)}, u32[]{:S(2)}) collective-permute-start(f32[16,896]{1,0:T(8,128)S(1)} %get-tuple-element.26), channel_id=1, source_target_pairs={{0,3},{1,2},{2,1},{3,0},{4,7},{5,6},{6,5},{7,4},{8,11},{9,10},{10,... | collective-permute-start | bytes 172040 | tf_op jit(solution)/shard_map/ppermute | solution.py:191
  27.6 4.9 %collective-permute-start.17 = (f32[16,896]{1,0:T(8,128)S(1)}, f32[16,896]{1,0:T(8,128)S(1)}, u32[]{:S(2)}, u32[]{:S(2)}) collective-permute-start(f32[16,896]{1,0:T(8,128)S(1)} %add.34), channel_id=1, source_target_pairs={{0,5},{1,4},{2,7},{3,6},{4,1},{5,0},{6,3},{7,2},{8,13},{9,12},{10,... | collective-permute-start | bytes 172040 | tf_op jit(solution)/shard_map/ppermute | solution.py:191
  29.9 4.9 %collective-permute-start.11 = (f32[16,896]{1,0:T(8,128)S(1)}, f32[16,896]{1,0:T(8,128)S(1)}, u32[]{:S(2)}, u32[]{:S(2)}) collective-permute-start(f32[16,896]{1,0:T(8,128)S(1)} %add.32), channel_id=1, source_target_pairs={{0,5},{1,4},{2,7},{3,6},{4,1},{5,0},{6,3},{7,2},{8,13},{9,12},{10,... | collective-permute-start | bytes 172040 | tf_op jit(solution)/shard_map/ppermute | solution.py:191
  32.5 5.2 %collective-permute-start.19 = (f32[16,896]{1,0:T(8,128)S(1)}, f32[16,896]{1,0:T(8,128)S(1)}, u32[]{:S(2)}, u32[]{:S(2)}) collective-permute-start(f32[16,896]{1,0:T(8,128)S(1)} %add.35.refs_0_), channel_id=1, source_target_pairs={{0,17},{1,16},{2,19},{3,18},{4,21},{5,20},{6,23},{7,22},{8,25},{9,... | collective-permute-start | bytes 172040 | tf_op jit(solution)/shard_map/ppermute | solution.py:191
  34.8 5.1 %collective-permute-start.12 = (f32[16,896]{1,0:T(8,128)S(1)}, f32[16,896]{1,0:T(8,128)S(1)}, u32[]{:S(2)}, u32[]{:S(2)}) collective-permute-start(f32[16,896]{1,0:T(8,128)S(1)} %add.33.refs_0_), channel_id=1, source_target_pairs={{0,9},{1,8},{2,11},{3,10},{4,13},{5,12},{6,15},{7,14},{8,1},{9,0},... | collective-permute-start | bytes 172040 | tf_op jit(solution)/shard_map/ppermute | solution.py:191
  37.6 3.7 %collective-permute-start.18 = (f32[16,896]{1,0:T(8,128)S(1)}, f32[16,896]{1,0:T(8,128)S(1)}, u32[]{:S(2)}, u32[]{:S(2)}) collective-permute-start(f32[16,896]{1,0:T(8,128)S(1)} %add.35.refs_0_), channel_id=1, source_target_pairs={{0,9},{1,8},{2,11},{3,10},{4,13},{5,12},{6,15},{7,14},{8,1},{9,0},... | collective-permute-start | bytes 172040 | tf_op jit(solution)/shard_map/ppermute | solution.py:191
  37.7 4.9 %collective-permute-start.20 = (f32[16,896]{1,0:T(8,128)S(1)}, f32[16,896]{1,0:T(8,128)S(1)}, u32[]{:S(2)}, u32[]{:S(2)}) collective-permute-start(f32[16,896]{1,0:T(8,128)S(1)} %collective-permute-done.19.refs_2_), channel_id=1, source_target_pairs={{0,9},{1,8},{2,11},{3,10},{4,13},{5,12},{6,15},{7,14},{8,1},{9,0},... | collective-permute-start | bytes 172040 | tf_op jit(solution)/shard_map/ppermute | solution.py:191
  39.4 3.9 %collective-permute-start.13 = (f32[16,896]{1,0:T(8,128)S(1)}, f32[16,896]{1,0:T(8,128)S(1)}, u32[]{:S(2)}, u32[]{:S(2)}) collective-permute-start(f32[16,896]{1,0:T(8,128)S(1)} %add.33.refs_0_), channel_id=1, source_target_pairs={{0,17},{1,16},{2,19},{3,18},{4,21},{5,20},{6,23},{7,22},{8,25},{9,... | collective-permute-start | bytes 172040 | tf_op jit(solution)/shard_map/ppermute | solution.py:191
  39.9 4.4 %collective-permute-start.14 = (f32[16,896]{1,0:T(8,128)S(1)}, f32[16,896]{1,0:T(8,128)S(1)}, u32[]{:S(2)}, u32[]{:S(2)}) collective-permute-start(f32[16,896]{1,0:T(8,128)S(1)} %collective-permute-done.12.refs_1_), channel_id=1, source_target_pairs={{0,17},{1,16},{2,19},{3,18},{4,21},{5,20},{6,23},{7,22},{8,25},{9,... | collective-permute-start | bytes 172040 | tf_op jit(solution)/shard_map/ppermute | solution.py:191
  42.6 3.3 %collective-permute-start.21 = (f32[64,896]{1,0:T(8,128)S(1)}, f32[64,896]{1,0:T(8,128)S(1)}, u32[]{:S(2)}, u32[]{:S(2)}) collective-permute-start(f32[64,896]{1,0:T(8,128)S(1)} %shard_map.56.refs_1_), channel_id=1, source_target_pairs={{0,1},{1,0},{2,3},{3,2},{4,5},{5,4},{6,7},{7,6},{8,9},{9,8},{10,11... | collective-permute-start | bytes 688136 | tf_op jit(solution)/shard_map/ppermute | solution.py:194
  44.3 1.6 %collective-permute-start.15 = (f32[64,896]{1,0:T(8,128)S(1)}, f32[64,896]{1,0:T(8,128)S(1)}, u32[]{:S(2)}, u32[]{:S(2)}) collective-permute-start(f32[64,896]{1,0:T(8,128)S(1)} %shard_map.55.refs_0_), channel_id=1, source_target_pairs={{0,1},{1,0},{2,3},{3,2},{4,5},{5,4},{6,7},{7,6},{8,9},{9,8},{10,11... | collective-permute-start | bytes 688136 | tf_op jit(solution)/shard_map/ppermute | solution.py:194

commit v6 on v5

--- a/solution.py
+++ b/solution.py
@@ -93,28 +93,39 @@
         out[...] = g[:, span].astype(F32) + f[:, span].astype(F32) + got[:, pl.ds(inner, width)]
 
 
-def gram_schmidt_kernel(block, a, b, basis, basis_t):
+def column_sum(value):
+    rows = value.shape[0]
+    if rows % 8:
+        return jnp.sum(value, axis=0, keepdims=True)
+    terms = [value[i : i + 8] for i in range(0, rows, 8)]
+    while len(terms) > 1:
+        terms = [sum(terms[i + 1 : i + 2], terms[i]) for i in range(0, len(terms), 2)]
+    return jnp.sum(terms[0], axis=0, keepdims=True)
+
+
+def gram_schmidt_kernel(window, a, b, basis, basis_t):
     rank, rows = a.shape
     lanes = 128
     total = jnp.concatenate([a[...] + b[...], jnp.zeros((lanes - rank, rows), F32)], axis=0)
     work = total.T
-    lane = lax.broadcasted_iota(jnp.int32, (rows, lanes), 1)
-    done = jnp.zeros((rows, lanes), F32)
-    for start in range(0, rank, block):
-        count = min(block, rank - start)
-        columns = [jnp.broadcast_to(work[:, start + i : start + i + 1], (rows, lanes)) for i in range(count)]
-        for i in range(count):
-            column = columns[i]
-            scale = lax.rsqrt(jnp.sum(column * column, axis=0, keepdims=True) + epsilon)
-            unit = column * scale
-            for k in range(i + 1, count):
-                dot = jnp.sum(column * columns[k], axis=0, keepdims=True) * scale
-                columns[k] = columns[k] - unit * dot
-            dots = jnp.sum(column * work, axis=0, keepdims=True) * scale
-            work = work - unit * dots
-            done = jnp.where(lane == start + i, unit, done)
-    basis[...] = done[:, :rank]
-    basis_t[...] = done.T[:rank]
+    lane = lax.broadcasted_iota(jnp.int32, (1, lanes), 1)
+
+    def spread(index):
+        return jnp.broadcast_to(work[:, index : index + 1], (rows, lanes))
+
+    columns = {index: spread(index) for index in range(min(window, rank))}
+    for index in range(rank):
+        column = columns.pop(index)
+        scale = lax.rsqrt(column_sum(column * column) + epsilon)
+        unit = column * scale
+        for later in columns:
+            columns[later] = columns[later] - unit * (column_sum(column * columns[later]) * scale)
+        dots = jnp.where(lane > index, column_sum(column * work) * scale, 0.0)
+        work = jnp.where(lane == index, unit, work - unit * dots)
+        if index + window < rank:
+            columns[index + window] = spread(index + window)
+    basis[...] = work[:, :rank]
+    basis_t[...] = work.T[:rank]
 
 
 def right_kernel(basis_t, *refs):
@@ -178,12 +189,12 @@
     half = columns // 2
     width = half // local
 
-    def permute(value, along_local, step):
+    def permute(value, along_local, step, cross=None):
         pairs = []
         for x in range(local):
             for z in range(groups):
                 to = (partner(x, step, local), z) if along_local else (x, partner(z, step, groups))
-                flip = odd_bits(step, local if along_local else groups)
+                flip = odd_bits(step, local if along_local else groups) if cross is None else cross
                 for core in range(2):
                     pairs.append((x * dp + 2 * z + core, to[0] * dp + 2 * to[1] + (core ^ flip)))
         if partner(0, step, local if along_local else groups) != step:
@@ -193,15 +204,14 @@
     def swap(value):
         return lax.ppermute(value, AXES, [(i, i ^ 1) for i in range(local * dp)])
 
-    def total_over(value, along_local, direct=False):
+    def total_over(value, along_local, direct=False, cross=None, turn=0):
         size = local if along_local else groups
         double = not direct and not size & (size - 1)
         first = value
-        step = 1
-        while step < size:
-            other = permute(value if double else first, along_local, step)
+        steps = [1 << i for i in range(size.bit_length() - 1)] if double else range(1, size)
+        for step in steps[::-1] if turn else steps:
+            other = permute(value if double else first, along_local, step, cross)
             value = value + other
-            step = 2 * step if double else step + 1
         return value
 
     def gather(own, turn):
@@ -224,10 +234,10 @@
     )
     left = call(left_kernel, ((rank, rows), F32), g, f, b, flops=1 << 27)
     got = swap(send)
-    left = total_over(left, True, direct=True)
+    left = total_over(left, True, direct=True, cross=1)
     chunks = call(pair_kernel, [((rows, width), F32)] * local, g, f, got)
     terms = [chunks[0]] + [permute(chunks[s], True, s) for s in range(1, local)]
-    left = total_over(left, False)
+    left = total_over(left, False, cross=1)
     basis, basis_t = call(
         functools.partial(gram_schmidt_kernel, 4),
         [((rows, rank), F32), ((rank, rows), F32)],
@@ -236,7 +246,7 @@
     rights = call(right_kernel, [((rank // PARTS, width), F32)] * PARTS, basis_t, *terms, flops=1 << 25)
     blocks, others = [], []
     for part, right in enumerate(rights):
-        own = total_over(right, False)
+        own = total_over(right, False, turn=part % 2)
         gathered = gather(own, part % 2)
         blocks.append(call(pack_kernel, ((local * own.shape[0], width), F32), *gathered))
         others.append(swap(blocks[-1]))

time: 47.2 us -> 48.3 us (1.023)
  starting transfers between devices: 25.2 us -> 28.1 us
  waiting for transfers between devices: 14 us -> 12.5 us
    ppermute x18, starting transfers between devices: 23.1 us -> 25.9 us  [permute(): return lax.ppermute(value, AXES, pairs)]
    ppermute x18, waiting for transfers between devices: 13.2 us -> 11.7 us  [permute(): return lax.ppermute(value, AXES, pairs)]
  transfers between devices with their start and end apart: 22 -> 22, of which waited for: 12 -> 12; matrix products, arithmetic and copies ran while one was open for 0% -> 0% of each run, Pallas kernels for 8% -> 7%
where the time goes in v6:
time: 48.3 us; the launch traced here: 48.2 us
  starting transfers between devices  28.1 us (58%)
  waiting for transfers between devices  12.5 us (26%)
  Pallas kernels  6.74 us (14%)
  between operations  0.71 us (1%)
    ppermute x18, starting transfers between devices, permute(): return lax.ppermute(value, AXES, pairs)  25.9 us
    ppermute x18, waiting for transfers between devices, permute(): return lax.ppermute(value, AXES, pairs)  11.7 us
    pallas_call x9, Pallas kernels, call(): pl.pallas_call(kernel, out_shape=shapes, in_specs=[pl.BlockSpec(memory_sp...  6.74 us
    ppermute x4, starting transfers between devices, swap(): return lax.ppermute(value, AXES, [(i, i ^ 1) for i in range(local * dp)])  2.2 us
  transfers between devices with their start and end apart: 22, of which 12 were waited for; matrix products, arithmetic and copies ran while one was open for 0% of the time, Pallas kernels for 7%

profile of v6, /device:TPU:0, one launch (start us, length us, event | category | flops | bytes accessed | tf_op | source)
XLA Modules:
  0.0 48.2 jit_solution(9926160159341981368)
XLA Ops:
  0.6 1.7 %shard_map.50 = (bf16[72,7168]{1,0:T(8,128)(2,1)S(1)}, bf16[72,7168]{1,0:T(8,128)(2,1)S(1)}, f32[72,3584]{1,0:T(8,128)S(1)}) custom-call(bf16[72,7168]{1,0:T(8,128)(2,1)} %bitcast.7, bf16[72,7168]{1,0:T(8,128)(2,1)} %bitcast.8), custom_call_target="tpu_custom_call" | custom-call | flops 1048576 | bytes 2064384 | tf_op jit(solution)/shard_map/pallas_call | solution.py:23
  2.4 0.6 %collective-permute-start.6 = (f32[72,3584]{1,0:T(8,128)S(1)}, f32[72,3584]{1,0:T(8,128)S(1)}, u32[]{:S(2)}, u32[]{:S(2)}) collective-permute-start(f32[72,3584]{1,0:T(8,128)S(1)} %get-tuple-element.21), channel_id=1, source_target_pairs={{0,1},{1,0},{2,3},{3,2},{4,5},{5,4},{6,7},{7,6},{8,9},{9,8},{10,11... | collective-permute-start | bytes 3096584 | tf_op jit(solution)/shard_map/ppermute | solution.py:205
  2.9 0.7 %shard_map.51 = f32[32,72]{1,0:T(8,128)S(1)} custom-call(bf16[72,7168]{1,0:T(8,128)(2,1)S(1)} %get-tuple-element.17.g, bf16[72,7168]{1,0:T(8,128)(2,1)S(1)} %get-tuple-element.18.f, f32[32,7168]{1,0:T(8,128)S(1)} %bitcast.5), custom_call_target="tpu_custom_call" | custom-call | flops 134217728 | bytes 2981888 | tf_op jit(solution)/shard_map/pallas_call | solution.py:23
  3.7 3.6 %collective-permute-start.2 = (f32[32,72]{1,0:T(8,128)S(1)}, f32[32,72]{1,0:T(8,128)S(1)}, u32[]{:S(2)}, u32[]{:S(2)}) collective-permute-start(f32[32,72]{1,0:T(8,128)S(1)} %shard_map.51), channel_id=1, source_target_pairs={{0,25},{1,24},{2,27},{3,26},{4,29},{5,28},{6,31},{7,30},{8,17},{9,... | collective-permute-start | bytes 27656 | tf_op jit(solution)/shard_map/ppermute | solution.py:202
  7.2 0.1 collective-permute-start.1
  7.4 0.1 collective-permute-start
  7.5 0.0 collective-permute-done.6.got
  7.5 0.2 shard_map.53
  7.7 1.7 %collective-permute-start.7 = (f32[72,896]{1,0:T(8,128)S(1)}, f32[72,896]{1,0:T(8,128)S(1)}, u32[]{:S(2)}, u32[]{:S(2)}) collective-permute-start(f32[72,896]{1,0:T(8,128)S(1)} %get-tuple-element.23), channel_id=1, source_target_pairs={{0,9},{1,8},{2,11},{3,10},{4,13},{5,12},{6,15},{7,14},{8,1},{9,0},... | collective-permute-start | bytes 774152 | tf_op jit(solution)/shard_map/ppermute | solution.py:202
  9.3 1.6 %collective-permute-start.8 = (f32[72,896]{1,0:T(8,128)S(1)}, f32[72,896]{1,0:T(8,128)S(1)}, u32[]{:S(2)}, u32[]{:S(2)}) collective-permute-start(f32[72,896]{1,0:T(8,128)S(1)} %get-tuple-element.24), channel_id=1, source_target_pairs={{0,17},{1,16},{2,19},{3,18},{4,21},{5,20},{6,23},{7,22},{8,25},{9,... | collective-permute-start | bytes 774152 | tf_op jit(solution)/shard_map/ppermute | solution.py:202
  11.0 0.0 collective-permute-done.2
  11.0 0.3 collective-permute-start.9
  11.2 0.0 collective-permute-done.1
  11.2 0.0 collective-permute-done
  11.2 1.5 %collective-permute-start.3 = (f32[32,72]{1,0:T(8,128)S(1)}, f32[32,72]{1,0:T(8,128)S(1)}, u32[]{:S(2)}, u32[]{:S(2)}) collective-permute-start(f32[32,72]{1,0:T(8,128)S(1)} %add_add_fusion), channel_id=1, source_target_pairs={{0,3},{1,2},{2,1},{3,0},{4,7},{5,6},{6,5},{7,4},{8,11},{9,10},{10,... | collective-permute-start | bytes 27656 | tf_op jit(solution)/shard_map/ppermute | solution.py:202
  12.8 1.7 %collective-permute-done.3 = f32[32,72]{1,0:T(8,128)S(1)} collective-permute-done((f32[32,72]{1,0:T(8,128)S(1)}, f32[32,72]{1,0:T(8,128)S(1)}, u32[]{:S(2)}, u32[]{:S(2)}) %collective-permute-start.3) | collective-permute-done | bytes 9248 | tf_op jit(solution)/shard_map/ppermute | solution.py:202
  14.5 2.8 %collective-permute-start.4 = (f32[32,72]{1,0:T(8,128)S(1)}, f32[32,72]{1,0:T(8,128)S(1)}, u32[]{:S(2)}, u32[]{:S(2)}) collective-permute-start(f32[32,72]{1,0:T(8,128)S(1)} %add.30), channel_id=1, source_target_pairs={{0,5},{1,4},{2,7},{3,6},{4,1},{5,0},{6,3},{7,2},{8,13},{9,12},{10,... | collective-permute-start | bytes 27656 | tf_op jit(solution)/shard_map/ppermute | solution.py:202
  17.2 1.4 %collective-permute-done.4 = f32[32,72]{1,0:T(8,128)S(1)} collective-permute-done((f32[32,72]{1,0:T(8,128)S(1)}, f32[32,72]{1,0:T(8,128)S(1)}, u32[]{:S(2)}, u32[]{:S(2)}) %collective-permute-start.4) | collective-permute-done | bytes 9248 | tf_op jit(solution)/shard_map/ppermute | solution.py:202
  18.7 0.8 %collective-permute-start.5 = (f32[32,72]{1,0:T(8,128)S(1)}, f32[32,72]{1,0:T(8,128)S(1)}, u32[]{:S(2)}, u32[]{:S(2)}) collective-permute-start(f32[32,72]{1,0:T(8,128)S(1)} %add.31.a), channel_id=1, source_target_pairs={{0,1},{1,0},{2,3},{3,2},{4,5},{5,4},{6,7},{7,6},{8,9},{9,8},{10,11... | collective-permute-start | bytes 27656 | tf_op jit(solution)/shard_map/ppermute | solution.py:205
  19.4 0.8 %collective-permute-done.5.b = f32[32,72]{1,0:T(8,128)S(1)} collective-permute-done((f32[32,72]{1,0:T(8,128)S(1)}, f32[32,72]{1,0:T(8,128)S(1)}, u32[]{:S(2)}, u32[]{:S(2)}) %collective-permute-start.5) | collective-permute-done | bytes 9248 | tf_op jit(solution)/shard_map/ppermute | solution.py:205
  20.3 1.5 %shard_map.52 = (f32[72,32]{1,0:T(8,128)S(1)}, f32[32,72]{1,0:T(8,128)S(1)}) custom-call(f32[32,72]{1,0:T(8,128)S(1)} %add.31.a, f32[32,72]{1,0:T(8,128)S(1)} %collective-permute-done.5.b), custom_call_target="tpu_custom_call" | custom-call | flops 67108864 | bytes 18432 | tf_op jit(solution)/shard_map/pallas_call | solution.py:23
  21.8 0.0 collective-permute-done.7.refs_1_
  21.8 0.7 %collective-permute-done.8.refs_2_ = f32[72,896]{1,0:T(8,128)S(1)} collective-permute-done((f32[72,896]{1,0:T(8,128)S(1)}, f32[72,896]{1,0:T(8,128)S(1)}, u32[]{:S(2)}, u32[]{:S(2)}) %collective-permute-start.8) | collective-permute-done | bytes 258080 | tf_op jit(solution)/shard_map/ppermute | solution.py:202
  22.5 0.9 %collective-permute-done.9.refs_3_ = f32[72,896]{1,0:T(8,128)S(1)} collective-permute-done((f32[72,896]{1,0:T(8,128)S(1)}, f32[72,896]{1,0:T(8,128)S(1)}, u32[]{:S(2)}, u32[]{:S(2)}) %collective-permute-start.9) | collective-permute-done | bytes 258080 | tf_op jit(solution)/shard_map/ppermute | solution.py:202
  23.4 0.3 shard_map.54
  23.7 2.2 %collective-permute-start.16 = (f32[16,896]{1,0:T(8,128)S(1)}, f32[16,896]{1,0:T(8,128)S(1)}, u32[]{:S(2)}, u32[]{:S(2)}) collective-permute-start(f32[16,896]{1,0:T(8,128)S(1)} %get-tuple-element.27), channel_id=1, source_target_pairs={{0,5},{1,4},{2,7},{3,6},{4,1},{5,0},{6,3},{7,2},{8,13},{9,12},{10,... | collective-permute-start | bytes 172040 | tf_op jit(solution)/shard_map/ppermute | solution.py:202
  25.9 1.7 %collective-permute-start.10 = (f32[16,896]{1,0:T(8,128)S(1)}, f32[16,896]{1,0:T(8,128)S(1)}, u32[]{:S(2)}, u32[]{:S(2)}) collective-permute-start(f32[16,896]{1,0:T(8,128)S(1)} %get-tuple-element.26), channel_id=1, source_target_pairs={{0,3},{1,2},{2,1},{3,0},{4,7},{5,6},{6,5},{7,4},{8,11},{9,10},{10,... | collective-permute-start | bytes 172040 | tf_op jit(solution)/shard_map/ppermute | solution.py:202
  27.6 1.0 %collective-permute-done.16 = f32[16,896]{1,0:T(8,128)S(1)} collective-permute-done((f32[16,896]{1,0:T(8,128)S(1)}, f32[16,896]{1,0:T(8,128)S(1)}, u32[]{:S(2)}, u32[]{:S(2)}) %collective-permute-start.16) | collective-permute-done | bytes 57376 | tf_op jit(solution)/shard_map/ppermute | solution.py:202
  28.6 1.8 %collective-permute-start.17 = (f32[16,896]{1,0:T(8,128)S(1)}, f32[16,896]{1,0:T(8,128)S(1)}, u32[]{:S(2)}, u32[]{:S(2)}) collective-permute-start(f32[16,896]{1,0:T(8,128)S(1)} %add.34), channel_id=1, source_target_pairs={{0,3},{1,2},{2,1},{3,0},{4,7},{5,6},{6,5},{7,4},{8,11},{9,10},{10,... | collective-permute-start | bytes 172040 | tf_op jit(solution)/shard_map/ppermute | solution.py:202
  30.4 0.0 collective-permute-done.10
  30.4 3.5 %collective-permute-start.11 = (f32[16,896]{1,0:T(8,128)S(1)}, f32[16,896]{1,0:T(8,128)S(1)}, u32[]{:S(2)}, u32[]{:S(2)}) collective-permute-start(f32[16,896]{1,0:T(8,128)S(1)} %add.32), channel_id=1, source_target_pairs={{0,5},{1,4},{2,7},{3,6},{4,1},{5,0},{6,3},{7,2},{8,13},{9,12},{10,... | collective-permute-start | bytes 172040 | tf_op jit(solution)/shard_map/ppermute | solution.py:202
  33.9 0.0 collective-permute-done.17
  33.9 0.6 %collective-permute-start.19 = (f32[16,896]{1,0:T(8,128)S(1)}, f32[16,896]{1,0:T(8,128)S(1)}, u32[]{:S(2)}, u32[]{:S(2)}) collective-permute-start(f32[16,896]{1,0:T(8,128)S(1)} %add.35.refs_0_), channel_id=1, source_target_pairs={{0,17},{1,16},{2,19},{3,18},{4,21},{5,20},{6,23},{7,22},{8,25},{9,... | collective-permute-start | bytes 172040 | tf_op jit(solution)/shard_map/ppermute | solution.py:202
  34.5 2.9 %collective-permute-done.11 = f32[16,896]{1,0:T(8,128)S(1)} collective-permute-done((f32[16,896]{1,0:T(8,128)S(1)}, f32[16,896]{1,0:T(8,128)S(1)}, u32[]{:S(2)}, u32[]{:S(2)}) %collective-permute-start.11) | collective-permute-done | bytes 57376 | tf_op jit(solution)/shard_map/ppermute | solution.py:202
  37.5 1.2 %collective-permute-start.12 = (f32[16,896]{1,0:T(8,128)S(1)}, f32[16,896]{1,0:T(8,128)S(1)}, u32[]{:S(2)}, u32[]{:S(2)}) collective-permute-start(f32[16,896]{1,0:T(8,128)S(1)} %add.33.refs_0_), channel_id=1, source_target_pairs={{0,9},{1,8},{2,11},{3,10},{4,13},{5,12},{6,15},{7,14},{8,1},{9,0},... | collective-permute-start | bytes 172040 | tf_op jit(solution)/shard_map/ppermute | solution.py:202
  38.7 0.6 %collective-permute-start.18 = (f32[16,896]{1,0:T(8,128)S(1)}, f32[16,896]{1,0:T(8,128)S(1)}, u32[]{:S(2)}, u32[]{:S(2)}) collective-permute-start(f32[16,896]{1,0:T(8,128)S(1)} %add.35.refs_0_), channel_id=1, source_target_pairs={{0,9},{1,8},{2,11},{3,10},{4,13},{5,12},{6,15},{7,14},{8,1},{9,0},... | collective-permute-start | bytes 172040 | tf_op jit(solution)/shard_map/ppermute | solution.py:202
  39.3 1.2 %collective-permute-start.20 = (f32[16,896]{1,0:T(8,128)S(1)}, f32[16,896]{1,0:T(8,128)S(1)}, u32[]{:S(2)}, u32[]{:S(2)}) collective-permute-start(f32[16,896]{1,0:T(8,128)S(1)} %collective-permute-done.19.refs_2_), channel_id=1, source_target_pairs={{0,9},{1,8},{2,11},{3,10},{4,13},{5,12},{6,15},{7,14},{8,1},{9,0},... | collective-permute-start | bytes 172040 | tf_op jit(solution)/shard_map/ppermute | solution.py:202
  40.4 0.6 %collective-permute-start.13 = (f32[16,896]{1,0:T(8,128)S(1)}, f32[16,896]{1,0:T(8,128)S(1)}, u32[]{:S(2)}, u32[]{:S(2)}) collective-permute-start(f32[16,896]{1,0:T(8,128)S(1)} %add.33.refs_0_), channel_id=1, source_target_pairs={{0,17},{1,16},{2,19},{3,18},{4,21},{5,20},{6,23},{7,22},{8,25},{9,... | collective-permute-start | bytes 172040 | tf_op jit(solution)/shard_map/ppermute | solution.py:202
  41.0 0.4 collective-permute-done.12.refs_1_
  41.5 0.9 %collective-permute-start.14 = (f32[16,896]{1,0:T(8,128)S(1)}, f32[16,896]{1,0:T(8,128)S(1)}, u32[]{:S(2)}, u32[]{:S(2)}) collective-permute-start(f32[16,896]{1,0:T(8,128)S(1)} %collective-permute-done.12.refs_1_), channel_id=1, source_target_pairs={{0,17},{1,16},{2,19},{3,18},{4,21},{5,20},{6,23},{7,22},{8,25},{9,... | collective-permute-start | bytes 172040 | tf_op jit(solution)/shard_map/ppermute | solution.py:202
  42.3 0.1 collective-permute-done.18.refs_1_
  42.5 1.2 %collective-permute-done.20.refs_3_ = f32[16,896]{1,0:T(8,128)S(1)} collective-permute-done((f32[16,896]{1,0:T(8,128)S(1)}, f32[16,896]{1,0:T(8,128)S(1)}, u32[]{:S(2)}, u32[]{:S(2)}) %collective-permute-start.20) | collective-permute-done | bytes 57376 | tf_op jit(solution)/shard_map/ppermute | solution.py:202
  43.7 0.6 %collective-permute-start.21 = (f32[64,896]{1,0:T(8,128)S(1)}, f32[64,896]{1,0:T(8,128)S(1)}, u32[]{:S(2)}, u32[]{:S(2)}) collective-permute-start(f32[64,896]{1,0:T(8,128)S(1)} %shard_map.56.refs_1_), channel_id=1, source_target_pairs={{0,1},{1,0},{2,3},{3,2},{4,5},{5,4},{6,7},{7,6},{8,9},{9,8},{10,11... | collective-permute-start | bytes 688136 | tf_op jit(solution)/shard_map/ppermute | solution.py:205
  44.3 1.1 %collective-permute-done.14.refs_3_ = f32[16,896]{1,0:T(8,128)S(1)} collective-permute-done((f32[16,896]{1,0:T(8,128)S(1)}, f32[16,896]{1,0:T(8,128)S(1)}, u32[]{:S(2)}, u32[]{:S(2)}) %collective-permute-start.14) | collective-permute-done | bytes 57376 | tf_op jit(solution)/shard_map/ppermute | solution.py:202
  45.5 0.3 collective-permute-start.15
  45.8 1.1 %shard_map.57 = (bf16[72,7168]{1,0:T(8,128)(2,1)}, f32[32,7168]{1,0:T(8,128)}) custom-call(bf16[72,7168]{1,0:T(8,128)(2,1)S(1)} %get-tuple-element.17.g, bf16[72,7168]{1,0:T(8,128)(2,1)S(1)} %get-tuple-element.18.f, f32[72,32]{1,0:T(8,128)S(1)} %get-tuple-element.19.basis, f32[64,896]{1,0:T(8,128)S(1)} %shard_map.55.refs_0_, f32[64,896]{1,0:T(8,128)S(1)} %shard_map.56.refs_1_), custom_call_target="tpu_custom_call" | custom-call | flops 134217728 | bytes 2532352 | tf_op jit(solution)/shard_map/pallas_call | solution.py:23
  47.0 0.1 collective-permute-done.15.refs_0_
  47.0 1.1 %shard_map.58 = (bf16[72,7168]{1,0:T(8,128)(2,1)}, f32[32,7168]{1,0:T(8,128)}) custom-call(bf16[72,7168]{1,0:T(8,128)(2,1)S(1)} %get-tuple-element.17.g, bf16[72,7168]{1,0:T(8,128)(2,1)S(1)} %get-tuple-element.18.f, f32[72,32]{1,0:T(8,128)S(1)} %get-tuple-element.19.basis, ...), custom_call_target="tpu_custom_call", output_to_operand_aliasing={{0}: (5, {}), {1}: (6, {})} | custom-call | flops 134217728 | bytes 4482048 | tf_op jit(solution)/shard_map/pallas_call | solution.py:23
  (14 shorter events, 0.1 us)
Async XLA Ops:
  0.6 2.3 %copy-start = (f32[7168,32]{0,1:T(8,128)S(1)}, f32[7168,32]{0,1:T(8,128)}, u32[]{:S(2)}) copy-start(f32[7168,32]{0,1:T(8,128)} %param.5) | copy-start | bytes 2752516
  2.4 5.1 %collective-permute-start.6 = (f32[72,3584]{1,0:T(8,128)S(1)}, f32[72,3584]{1,0:T(8,128)S(1)}, u32[]{:S(2)}, u32[]{:S(2)}) collective-permute-start(f32[72,3584]{1,0:T(8,128)S(1)} %get-tuple-element.21), channel_id=1, source_target_pairs={{0,1},{1,0},{2,3},{3,2},{4,5},{5,4},{6,7},{7,6},{8,9},{9,8},{10,11... | collective-permute-start | bytes 3096584 | tf_op jit(solution)/shard_map/ppermute | solution.py:205
  3.7 7.3 %collective-permute-start.2 = (f32[32,72]{1,0:T(8,128)S(1)}, f32[32,72]{1,0:T(8,128)S(1)}, u32[]{:S(2)}, u32[]{:S(2)}) collective-permute-start(f32[32,72]{1,0:T(8,128)S(1)} %shard_map.51), channel_id=1, source_target_pairs={{0,25},{1,24},{2,27},{3,26},{4,29},{5,28},{6,31},{7,30},{8,17},{9,... | collective-permute-start | bytes 27656 | tf_op jit(solution)/shard_map/ppermute | solution.py:202
  7.2 4.0 %collective-permute-start.1 = (f32[32,72]{1,0:T(8,128)S(1)}, f32[32,72]{1,0:T(8,128)S(1)}, u32[]{:S(2)}, u32[]{:S(2)}) collective-permute-start(f32[32,72]{1,0:T(8,128)S(1)} %shard_map.51), channel_id=1, source_target_pairs={{0,17},{1,16},{2,19},{3,18},{4,21},{5,20},{6,23},{7,22},{8,25},{9,... | collective-permute-start | bytes 27656 | tf_op jit(solution)/shard_map/ppermute | solution.py:202
  7.4 3.9 %collective-permute-start = (f32[32,72]{1,0:T(8,128)S(1)}, f32[32,72]{1,0:T(8,128)S(1)}, u32[]{:S(2)}, u32[]{:S(2)}) collective-permute-start(f32[32,72]{1,0:T(8,128)S(1)} %shard_map.51), channel_id=1, source_target_pairs={{0,9},{1,8},{2,11},{3,10},{4,13},{5,12},{6,15},{7,14},{8,1},{9,0},... | collective-permute-start | bytes 27656 | tf_op jit(solution)/shard_map/ppermute | solution.py:202
  7.7 14.1 %collective-permute-start.7 = (f32[72,896]{1,0:T(8,128)S(1)}, f32[72,896]{1,0:T(8,128)S(1)}, u32[]{:S(2)}, u32[]{:S(2)}) collective-permute-start(f32[72,896]{1,0:T(8,128)S(1)} %get-tuple-element.23), channel_id=1, source_target_pairs={{0,9},{1,8},{2,11},{3,10},{4,13},{5,12},{6,15},{7,14},{8,1},{9,0},... | collective-permute-start | bytes 774152 | tf_op jit(solution)/shard_map/ppermute | solution.py:202
  9.3 13.1 %collective-permute-start.8 = (f32[72,896]{1,0:T(8,128)S(1)}, f32[72,896]{1,0:T(8,128)S(1)}, u32[]{:S(2)}, u32[]{:S(2)}) collective-permute-start(f32[72,896]{1,0:T(8,128)S(1)} %get-tuple-element.24), channel_id=1, source_target_pairs={{0,17},{1,16},{2,19},{3,18},{4,21},{5,20},{6,23},{7,22},{8,25},{9,... | collective-permute-start | bytes 774152 | tf_op jit(solution)/shard_map/ppermute | solution.py:202
  11.0 12.4 %collective-permute-start.9 = (f32[72,896]{1,0:T(8,128)S(1)}, f32[72,896]{1,0:T(8,128)S(1)}, u32[]{:S(2)}, u32[]{:S(2)}) collective-permute-start(f32[72,896]{1,0:T(8,128)S(1)} %get-tuple-element.25), channel_id=1, source_target_pairs={{0,24},{1,25},{2,26},{3,27},{4,28},{5,29},{6,30},{7,31},{8,16},{9,... | collective-permute-start | bytes 774152 | tf_op jit(solution)/shard_map/ppermute | solution.py:202
  11.2 3.2 %collective-permute-start.3 = (f32[32,72]{1,0:T(8,128)S(1)}, f32[32,72]{1,0:T(8,128)S(1)}, u32[]{:S(2)}, u32[]{:S(2)}) collective-permute-start(f32[32,72]{1,0:T(8,128)S(1)} %add_add_fusion), channel_id=1, source_target_pairs={{0,3},{1,2},{2,1},{3,0},{4,7},{5,6},{6,5},{7,4},{8,11},{9,10},{10,... | collective-permute-start | bytes 27656 | tf_op jit(solution)/shard_map/ppermute | solution.py:202
  14.5 4.2 %collective-permute-start.4 = (f32[32,72]{1,0:T(8,128)S(1)}, f32[32,72]{1,0:T(8,128)S(1)}, u32[]{:S(2)}, u32[]{:S(2)}) collective-permute-start(f32[32,72]{1,0:T(8,128)S(1)} %add.30), channel_id=1, source_target_pairs={{0,5},{1,4},{2,7},{3,6},{4,1},{5,0},{6,3},{7,2},{8,13},{9,12},{10,... | collective-permute-start | bytes 27656 | tf_op jit(solution)/shard_map/ppermute | solution.py:202
  18.7 1.6 %collective-permute-start.5 = (f32[32,72]{1,0:T(8,128)S(1)}, f32[32,72]{1,0:T(8,128)S(1)}, u32[]{:S(2)}, u32[]{:S(2)}) collective-permute-start(f32[32,72]{1,0:T(8,128)S(1)} %add.31.a), channel_id=1, source_target_pairs={{0,1},{1,0},{2,3},{3,2},{4,5},{5,4},{6,7},{7,6},{8,9},{9,8},{10,11... | collective-permute-start | bytes 27656 | tf_op jit(solution)/shard_map/ppermute | solution.py:205
  23.7 4.9 %collective-permute-start.16 = (f32[16,896]{1,0:T(8,128)S(1)}, f32[16,896]{1,0:T(8,128)S(1)}, u32[]{:S(2)}, u32[]{:S(2)}) collective-permute-start(f32[16,896]{1,0:T(8,128)S(1)} %get-tuple-element.27), channel_id=1, source_target_pairs={{0,5},{1,4},{2,7},{3,6},{4,1},{5,0},{6,3},{7,2},{8,13},{9,12},{10,... | collective-permute-start | bytes 172040 | tf_op jit(solution)/shard_map/ppermute | solution.py:202
  25.9 4.5 %collective-permute-start.10 = (f32[16,896]{1,0:T(8,128)S(1)}, f32[16,896]{1,0:T(8,128)S(1)}, u32[]{:S(2)}, u32[]{:S(2)}) collective-permute-start(f32[16,896]{1,0:T(8,128)S(1)} %get-tuple-element.26), channel_id=1, source_target_pairs={{0,3},{1,2},{2,1},{3,0},{4,7},{5,6},{6,5},{7,4},{8,11},{9,10},{10,... | collective-permute-start | bytes 172040 | tf_op jit(solution)/shard_map/ppermute | solution.py:202
  28.6 5.3 %collective-permute-start.17 = (f32[16,896]{1,0:T(8,128)S(1)}, f32[16,896]{1,0:T(8,128)S(1)}, u32[]{:S(2)}, u32[]{:S(2)}) collective-permute-start(f32[16,896]{1,0:T(8,128)S(1)} %add.34), channel_id=1, source_target_pairs={{0,3},{1,2},{2,1},{3,0},{4,7},{5,6},{6,5},{7,4},{8,11},{9,10},{10,... | collective-permute-start | bytes 172040 | tf_op jit(solution)/shard_map/ppermute | solution.py:202
  30.4 7.1 %collective-permute-start.11 = (f32[16,896]{1,0:T(8,128)S(1)}, f32[16,896]{1,0:T(8,128)S(1)}, u32[]{:S(2)}, u32[]{:S(2)}) collective-permute-start(f32[16,896]{1,0:T(8,128)S(1)} %add.32), channel_id=1, source_target_pairs={{0,5},{1,4},{2,7},{3,6},{4,1},{5,0},{6,3},{7,2},{8,13},{9,12},{10,... | collective-permute-start | bytes 172040 | tf_op jit(solution)/shard_map/ppermute | solution.py:202
  33.9 5.4 %collective-permute-start.19 = (f32[16,896]{1,0:T(8,128)S(1)}, f32[16,896]{1,0:T(8,128)S(1)}, u32[]{:S(2)}, u32[]{:S(2)}) collective-permute-start(f32[16,896]{1,0:T(8,128)S(1)} %add.35.refs_0_), channel_id=1, source_target_pairs={{0,17},{1,16},{2,19},{3,18},{4,21},{5,20},{6,23},{7,22},{8,25},{9,... | collective-permute-start | bytes 172040 | tf_op jit(solution)/shard_map/ppermute | solution.py:202
  37.5 4.0 %collective-permute-start.12 = (f32[16,896]{1,0:T(8,128)S(1)}, f32[16,896]{1,0:T(8,128)S(1)}, u32[]{:S(2)}, u32[]{:S(2)}) collective-permute-start(f32[16,896]{1,0:T(8,128)S(1)} %add.33.refs_0_), channel_id=1, source_target_pairs={{0,9},{1,8},{2,11},{3,10},{4,13},{5,12},{6,15},{7,14},{8,1},{9,0},... | collective-permute-start | bytes 172040 | tf_op jit(solution)/shard_map/ppermute | solution.py:202
  38.7 3.8 %collective-permute-start.18 = (f32[16,896]{1,0:T(8,128)S(1)}, f32[16,896]{1,0:T(8,128)S(1)}, u32[]{:S(2)}, u32[]{:S(2)}) collective-permute-start(f32[16,896]{1,0:T(8,128)S(1)} %add.35.refs_0_), channel_id=1, source_target_pairs={{0,9},{1,8},{2,11},{3,10},{4,13},{5,12},{6,15},{7,14},{8,1},{9,0},... | collective-permute-start | bytes 172040 | tf_op jit(solution)/shard_map/ppermute | solution.py:202
  39.3 4.4 %collective-permute-start.20 = (f32[16,896]{1,0:T(8,128)S(1)}, f32[16,896]{1,0:T(8,128)S(1)}, u32[]{:S(2)}, u32[]{:S(2)}) collective-permute-start(f32[16,896]{1,0:T(8,128)S(1)} %collective-permute-done.19.refs_2_), channel_id=1, source_target_pairs={{0,9},{1,8},{2,11},{3,10},{4,13},{5,12},{6,15},{7,14},{8,1},{9,0},... | collective-permute-start | bytes 172040 | tf_op jit(solution)/shard_map/ppermute | solution.py:202
  40.4 3.8 %collective-permute-start.13 = (f32[16,896]{1,0:T(8,128)S(1)}, f32[16,896]{1,0:T(8,128)S(1)}, u32[]{:S(2)}, u32[]{:S(2)}) collective-permute-start(f32[16,896]{1,0:T(8,128)S(1)} %add.33.refs_0_), channel_id=1, source_target_pairs={{0,17},{1,16},{2,19},{3,18},{4,21},{5,20},{6,23},{7,22},{8,25},{9,... | collective-permute-start | bytes 172040 | tf_op jit(solution)/shard_map/ppermute | solution.py:202
  41.5 4.0 %collective-permute-start.14 = (f32[16,896]{1,0:T(8,128)S(1)}, f32[16,896]{1,0:T(8,128)S(1)}, u32[]{:S(2)}, u32[]{:S(2)}) collective-permute-start(f32[16,896]{1,0:T(8,128)S(1)} %collective-permute-done.12.refs_1_), channel_id=1, source_target_pairs={{0,17},{1,16},{2,19},{3,18},{4,21},{5,20},{6,23},{7,22},{8,25},{9,... | collective-permute-start | bytes 172040 | tf_op jit(solution)/shard_map/ppermute | solution.py:202
  43.7 3.2 %collective-permute-start.21 = (f32[64,896]{1,0:T(8,128)S(1)}, f32[64,896]{1,0:T(8,128)S(1)}, u32[]{:S(2)}, u32[]{:S(2)}) collective-permute-start(f32[64,896]{1,0:T(8,128)S(1)} %shard_map.56.refs_1_), channel_id=1, source_target_pairs={{0,1},{1,0},{2,3},{3,2},{4,5},{5,4},{6,7},{7,6},{8,9},{9,8},{10,11... | collective-permute-start | bytes 688136 | tf_op jit(solution)/shard_map/ppermute | solution.py:205
  45.5 1.6 %collective-permute-start.15 = (f32[64,896]{1,0:T(8,128)S(1)}, f32[64,896]{1,0:T(8,128)S(1)}, u32[]{:S(2)}, u32[]{:S(2)}) collective-permute-start(f32[64,896]{1,0:T(8,128)S(1)} %shard_map.55.refs_0_), channel_id=1, source_target_pairs={{0,1},{1,0},{2,3},{3,2},{4,5},{5,4},{6,7},{7,6},{8,9},{9,8},{10,11... | collective-permute-start | bytes 688136 | tf_op jit(solution)/shard_map/ppermute | solution.py:205

commit v7 on v6

--- a/solution.py
+++ b/solution.py
@@ -146,35 +146,35 @@
         out[i * size : (i + 1) * size] = block[...]
 
 
-def final_kernel(workers, other, g, f, basis, *refs):
-    parts = refs[:PARTS]
+def final_kernel(workers, plan, g, f, basis, *refs):
     feedback, new_basis_t, staged, sems = refs[-4:]
-    chunks = sems.shape[0]
-    size, width = parts[0].shape[0] // chunks, parts[0].shape[1]
+    rank = basis.shape[1]
+    width = refs[0].shape[1]
+    local = lax.axis_size("local")
     mine = lax.axis_index("local")
-    side = (own_half() + other) % 2
     high, low = split(basis[...] * (1.0 / workers))
     left = jnp.concatenate([high, low, high], axis=1)
-    copies = []
+    work, copies = [], []
 
     def put(source, target, i, j):
         copies.append(pltpu.make_async_copy(source, target, sems.at[i, j]))
         copies[-1].start()
 
-    spans = []
-    for i in range(chunks):
-        start = (side * chunks + partner(mine, i, chunks)) * width
-        spans.append(pl.ds(pl.multiple_of(start, 128), width))
-        for j, part in enumerate(parts):
-            put(part.at[pl.ds(i * size, size)], new_basis_t.at[pl.ds(j * size, size), spans[i]], i, j)
-    for i, span in enumerate(spans):
-        piece = jnp.concatenate([part[i * size : (i + 1) * size] for part in parts], axis=0)
-        upper, lower = split(piece)
+    for (other, chunks), packed in zip(plan, refs):
+        side = (own_half() + other) % 2
+        for place, chunk in enumerate(chunks):
+            start = (side * local + partner(mine, chunk, local)) * width
+            span = pl.ds(pl.multiple_of(start, 128), width)
+            piece = packed.at[pl.ds(place * rank, rank)]
+            put(piece, new_basis_t.at[:, span], len(work), 0)
+            work.append((piece, span))
+    for i, (piece, span) in enumerate(work):
+        upper, lower = split(piece[...])
         right = jnp.concatenate([upper, upper, lower], axis=0)
         approx = jnp.dot(left, right, preferred_element_type=F32)
         merged = g[:, span].astype(F32) + f[:, span].astype(F32)
-        staged[:, i * width : (i + 1) * width] = (merged - approx).astype(BF16)
-        put(staged.at[:, i * width : (i + 1) * width], feedback.at[:, span], i, PARTS)
+        staged[i] = (merged - approx).astype(BF16)
+        put(staged.at[i], feedback.at[:, span], i, 1)
     for copy in copies:
         copy.wait()
 
@@ -244,19 +244,29 @@
         left, swap(left), flops=1 << 26,
     )
     rights = call(right_kernel, [((rank // PARTS, width), F32)] * PARTS, basis_t, *terms, flops=1 << 25)
-    blocks, others = [], []
+    gathered = []
     for part, right in enumerate(rights):
-        own = total_over(right, False, turn=part % 2)
-        gathered = gather(own, part % 2)
-        blocks.append(call(pack_kernel, ((local * own.shape[0], width), F32), *gathered))
-        others.append(swap(blocks[-1]))
+        total = total_over(right, False, turn=part % 2)
+        gathered.append(gather(total, part % 2))
+    groups_of = [chunks for chunks in (tuple(range(local - 1)), (local - 1,)) if chunks]
+    own, others = [], []
+    for chunks in groups_of:
+        pieces = [blocks[chunk] for chunk in chunks for blocks in gathered]
+        own.append(call(pack_kernel, ((len(chunks) * rank, width), F32), *pieces))
+        others.append(swap(own[-1]))
+    early, late = groups_of[0], groups_of[-1]
+    stages = [((0, early, own[0]),), ((1, late, others[-1]),)]
+    if len(groups_of) > 1:
+        stages.insert(1, ((1, early, others[0]), (0, late, own[-1])))
     outs = ()
-    for other, arrays in enumerate((blocks, others)):
+    for stage in stages:
+        count = sum(len(chunks) for _, chunks, _ in stage)
         outs = call(
-            functools.partial(final_kernel, local * dp, other),
+            functools.partial(final_kernel, local * dp, [(other, chunks) for other, chunks, _ in stage]),
             [((rows, columns), BF16), ((rank, columns), F32)],
-            g, f, basis, *arrays, *outs, flops=1 << 27, aliased=len(outs), target=pltpu.HBM,
-            scratch=[VMEM((rows, half), BF16), pltpu.SemaphoreType.DMA((local, PARTS + 1))],
+            g, f, basis, *[packed for _, _, packed in stage], *outs,
+            flops=1 << 27, aliased=len(outs), target=pltpu.HBM,
+            scratch=[VMEM((count, rows, width), BF16), pltpu.SemaphoreType.DMA((count, 2))],
         )
     return (outs[0][None], outs[1].T)
 

time: 48.3 us -> 50.5 us (1.046)
  waiting for transfers between devices: 12.5 us -> 14.3 us
  Pallas kernels: 6.74 us -> 7.53 us
    ppermute x18, waiting for transfers between devices: 11.7 us -> 13.4 us  [permute(): return lax.ppermute(value, AXES, pairs)]
    pallas_call x9 -> x10, Pallas kernels: 6.74 us -> 7.53 us  [call(): pl.pallas_call(kernel, out_shape=shapes, in_specs=[pl.BlockSpec(memory_sp...]
  transfers between devices with their start and end apart: 22 -> 22, of which waited for: 12 -> 11; matrix products, arithmetic and copies ran while one was open for 0% -> 0% of each run, Pallas kernels for 7% -> 9%
where the time goes in v7:
time: 50.5 us; the launch traced here: 50.4 us
  starting transfers between devices  27.8 us (55%)
  waiting for transfers between devices  14.3 us (28%)
  Pallas kernels  7.53 us (15%)
  between operations  0.73 us (1%)
    ppermute x18, starting transfers between devices, permute(): return lax.ppermute(value, AXES, pairs)  25.6 us
    ppermute x18, waiting for transfers between devices, permute(): return lax.ppermute(value, AXES, pairs)  13.4 us
    pallas_call x10, Pallas kernels, call(): pl.pallas_call(kernel, out_shape=shapes, in_specs=[pl.BlockSpec(memory_sp...  7.53 us
    ppermute x4, starting transfers between devices, swap(): return lax.ppermute(value, AXES, [(i, i ^ 1) for i in range(local * dp)])  2.21 us
  transfers between devices with their start and end apart: 22, of which 11 were waited for; matrix products, arithmetic and copies ran while one was open for 0% of the time, Pallas kernels for 9%

profile of v7, /device:TPU:0, one launch (start us, length us, event | category | flops | bytes accessed | tf_op | source)
XLA Modules:
  0.0 50.4 jit_solution(4698795843793256719)
XLA Ops:
  0.6 1.7 %shard_map.50 = (bf16[72,7168]{1,0:T(8,128)(2,1)S(1)}, bf16[72,7168]{1,0:T(8,128)(2,1)S(1)}, f32[72,3584]{1,0:T(8,128)S(1)}) custom-call(bf16[72,7168]{1,0:T(8,128)(2,1)} %bitcast.8, bf16[72,7168]{1,0:T(8,128)(2,1)} %bitcast.9), custom_call_target="tpu_custom_call" | custom-call | flops 1048576 | bytes 2064384 | tf_op jit(solution)/shard_map/pallas_call | solution.py:23
  2.4 0.6 %collective-permute-start.6 = (f32[72,3584]{1,0:T(8,128)S(1)}, f32[72,3584]{1,0:T(8,128)S(1)}, u32[]{:S(2)}, u32[]{:S(2)}) collective-permute-start(f32[72,3584]{1,0:T(8,128)S(1)} %get-tuple-element.23), channel_id=1, source_target_pairs={{0,1},{1,0},{2,3},{3,2},{4,5},{5,4},{6,7},{7,6},{8,9},{9,8},{10,11... | collective-permute-start | bytes 3096584 | tf_op jit(solution)/shard_map/ppermute | solution.py:205
  2.9 0.7 %shard_map.51 = f32[32,72]{1,0:T(8,128)S(1)} custom-call(bf16[72,7168]{1,0:T(8,128)(2,1)S(1)} %get-tuple-element.19.g, bf16[72,7168]{1,0:T(8,128)(2,1)S(1)} %get-tuple-element.20.f, f32[32,7168]{1,0:T(8,128)S(1)} %bitcast.5), custom_call_target="tpu_custom_call" | custom-call | flops 134217728 | bytes 2981888 | tf_op jit(solution)/shard_map/pallas_call | solution.py:23
  3.7 2.6 %collective-permute-start = (f32[32,72]{1,0:T(8,128)S(1)}, f32[32,72]{1,0:T(8,128)S(1)}, u32[]{:S(2)}, u32[]{:S(2)}) collective-permute-start(f32[32,72]{1,0:T(8,128)S(1)} %shard_map.51), channel_id=1, source_target_pairs={{0,9},{1,8},{2,11},{3,10},{4,13},{5,12},{6,15},{7,14},{8,1},{9,0},... | collective-permute-start | bytes 27656 | tf_op jit(solution)/shard_map/ppermute | solution.py:202
  6.3 1.1 %collective-permute-start.1 = (f32[32,72]{1,0:T(8,128)S(1)}, f32[32,72]{1,0:T(8,128)S(1)}, u32[]{:S(2)}, u32[]{:S(2)}) collective-permute-start(f32[32,72]{1,0:T(8,128)S(1)} %shard_map.51), channel_id=1, source_target_pairs={{0,17},{1,16},{2,19},{3,18},{4,21},{5,20},{6,23},{7,22},{8,25},{9,... | collective-permute-start | bytes 27656 | tf_op jit(solution)/shard_map/ppermute | solution.py:202
  7.4 0.0 collective-permute-start.2
  7.4 0.0 collective-permute-done.6.got
  7.4 0.2 shard_map.53
  7.6 1.7 %collective-permute-start.7 = (f32[72,896]{1,0:T(8,128)S(1)}, f32[72,896]{1,0:T(8,128)S(1)}, u32[]{:S(2)}, u32[]{:S(2)}) collective-permute-start(f32[72,896]{1,0:T(8,128)S(1)} %get-tuple-element.25), channel_id=1, source_target_pairs={{0,9},{1,8},{2,11},{3,10},{4,13},{5,12},{6,15},{7,14},{8,1},{9,0},... | collective-permute-start | bytes 774152 | tf_op jit(solution)/shard_map/ppermute | solution.py:202
  9.3 1.6 %collective-permute-start.8 = (f32[72,896]{1,0:T(8,128)S(1)}, f32[72,896]{1,0:T(8,128)S(1)}, u32[]{:S(2)}, u32[]{:S(2)}) collective-permute-start(f32[72,896]{1,0:T(8,128)S(1)} %get-tuple-element.26), channel_id=1, source_target_pairs={{0,17},{1,16},{2,19},{3,18},{4,21},{5,20},{6,23},{7,22},{8,25},{9,... | collective-permute-start | bytes 774152 | tf_op jit(solution)/shard_map/ppermute | solution.py:202
  11.0 0.0 collective-permute-start.9
  11.0 0.0 collective-permute-done.1
  11.0 0.5 %collective-permute-done.2 = f32[32,72]{1,0:T(8,128)S(1)} collective-permute-done((f32[32,72]{1,0:T(8,128)S(1)}, f32[32,72]{1,0:T(8,128)S(1)}, u32[]{:S(2)}, u32[]{:S(2)}) %collective-permute-start.2) | collective-permute-done | bytes 9248 | tf_op jit(solution)/shard_map/ppermute | solution.py:202
  11.5 1.7 %collective-permute-start.3 = (f32[32,72]{1,0:T(8,128)S(1)}, f32[32,72]{1,0:T(8,128)S(1)}, u32[]{:S(2)}, u32[]{:S(2)}) collective-permute-start(f32[32,72]{1,0:T(8,128)S(1)} %add_add_fusion), channel_id=1, source_target_pairs={{0,3},{1,2},{2,1},{3,0},{4,7},{5,6},{6,5},{7,4},{8,11},{9,10},{10,... | collective-permute-start | bytes 27656 | tf_op jit(solution)/shard_map/ppermute | solution.py:202
  13.2 1.5 %collective-permute-done.3 = f32[32,72]{1,0:T(8,128)S(1)} collective-permute-done((f32[32,72]{1,0:T(8,128)S(1)}, f32[32,72]{1,0:T(8,128)S(1)}, u32[]{:S(2)}, u32[]{:S(2)}) %collective-permute-start.3) | collective-permute-done | bytes 9248 | tf_op jit(solution)/shard_map/ppermute | solution.py:202
  14.7 3.0 %collective-permute-start.4 = (f32[32,72]{1,0:T(8,128)S(1)}, f32[32,72]{1,0:T(8,128)S(1)}, u32[]{:S(2)}, u32[]{:S(2)}) collective-permute-start(f32[32,72]{1,0:T(8,128)S(1)} %add.30), channel_id=1, source_target_pairs={{0,5},{1,4},{2,7},{3,6},{4,1},{5,0},{6,3},{7,2},{8,13},{9,12},{10,... | collective-permute-start | bytes 27656 | tf_op jit(solution)/shard_map/ppermute | solution.py:202
  17.6 1.4 %collective-permute-done.4 = f32[32,72]{1,0:T(8,128)S(1)} collective-permute-done((f32[32,72]{1,0:T(8,128)S(1)}, f32[32,72]{1,0:T(8,128)S(1)}, u32[]{:S(2)}, u32[]{:S(2)}) %collective-permute-start.4) | collective-permute-done | bytes 9248 | tf_op jit(solution)/shard_map/ppermute | solution.py:202
  19.1 0.7 %collective-permute-start.5 = (f32[32,72]{1,0:T(8,128)S(1)}, f32[32,72]{1,0:T(8,128)S(1)}, u32[]{:S(2)}, u32[]{:S(2)}) collective-permute-start(f32[32,72]{1,0:T(8,128)S(1)} %add.31.a), channel_id=1, source_target_pairs={{0,1},{1,0},{2,3},{3,2},{4,5},{5,4},{6,7},{7,6},{8,9},{9,8},{10,11... | collective-permute-start | bytes 27656 | tf_op jit(solution)/shard_map/ppermute | solution.py:205
  19.8 0.8 %collective-permute-done.5.b = f32[32,72]{1,0:T(8,128)S(1)} collective-permute-done((f32[32,72]{1,0:T(8,128)S(1)}, f32[32,72]{1,0:T(8,128)S(1)}, u32[]{:S(2)}, u32[]{:S(2)}) %collective-permute-start.5) | collective-permute-done | bytes 9248 | tf_op jit(solution)/shard_map/ppermute | solution.py:205
  20.7 1.5 %shard_map.52 = (f32[72,32]{1,0:T(8,128)S(1)}, f32[32,72]{1,0:T(8,128)S(1)}) custom-call(f32[32,72]{1,0:T(8,128)S(1)} %add.31.a, f32[32,72]{1,0:T(8,128)S(1)} %collective-permute-done.5.b), custom_call_target="tpu_custom_call" | custom-call | flops 67108864 | bytes 18432 | tf_op jit(solution)/shard_map/pallas_call | solution.py:23
  22.2 0.3 collective-permute-done.8.refs_2_
  22.5 0.9 %collective-permute-done.9.refs_3_ = f32[72,896]{1,0:T(8,128)S(1)} collective-permute-done((f32[72,896]{1,0:T(8,128)S(1)}, f32[72,896]{1,0:T(8,128)S(1)}, u32[]{:S(2)}, u32[]{:S(2)}) %collective-permute-start.9) | collective-permute-done | bytes 258080 | tf_op jit(solution)/shard_map/ppermute | solution.py:202
  23.4 0.3 shard_map.54
  23.7 2.2 %collective-permute-start.14 = (f32[16,896]{1,0:T(8,128)S(1)}, f32[16,896]{1,0:T(8,128)S(1)}, u32[]{:S(2)}, u32[]{:S(2)}) collective-permute-start(f32[16,896]{1,0:T(8,128)S(1)} %get-tuple-element.29), channel_id=1, source_target_pairs={{0,5},{1,4},{2,7},{3,6},{4,1},{5,0},{6,3},{7,2},{8,13},{9,12},{10,... | collective-permute-start | bytes 172040 | tf_op jit(solution)/shard_map/ppermute | solution.py:202
  25.9 1.7 %collective-permute-start.10 = (f32[16,896]{1,0:T(8,128)S(1)}, f32[16,896]{1,0:T(8,128)S(1)}, u32[]{:S(2)}, u32[]{:S(2)}) collective-permute-start(f32[16,896]{1,0:T(8,128)S(1)} %get-tuple-element.28), channel_id=1, source_target_pairs={{0,3},{1,2},{2,1},{3,0},{4,7},{5,6},{6,5},{7,4},{8,11},{9,10},{10,... | collective-permute-start | bytes 172040 | tf_op jit(solution)/shard_map/ppermute | solution.py:202
  27.6 1.0 %collective-permute-done.14 = f32[16,896]{1,0:T(8,128)S(1)} collective-permute-done((f32[16,896]{1,0:T(8,128)S(1)}, f32[16,896]{1,0:T(8,128)S(1)}, u32[]{:S(2)}, u32[]{:S(2)}) %collective-permute-start.14) | collective-permute-done | bytes 57376 | tf_op jit(solution)/shard_map/ppermute | solution.py:202
  28.6 1.8 %collective-permute-start.15 = (f32[16,896]{1,0:T(8,128)S(1)}, f32[16,896]{1,0:T(8,128)S(1)}, u32[]{:S(2)}, u32[]{:S(2)}) collective-permute-start(f32[16,896]{1,0:T(8,128)S(1)} %add.34), channel_id=1, source_target_pairs={{0,3},{1,2},{2,1},{3,0},{4,7},{5,6},{6,5},{7,4},{8,11},{9,10},{10,... | collective-permute-start | bytes 172040 | tf_op jit(solution)/shard_map/ppermute | solution.py:202
  30.4 0.0 collective-permute-done.10
  30.4 3.5 %collective-permute-start.11 = (f32[16,896]{1,0:T(8,128)S(1)}, f32[16,896]{1,0:T(8,128)S(1)}, u32[]{:S(2)}, u32[]{:S(2)}) collective-permute-start(f32[16,896]{1,0:T(8,128)S(1)} %add.32), channel_id=1, source_target_pairs={{0,5},{1,4},{2,7},{3,6},{4,1},{5,0},{6,3},{7,2},{8,13},{9,12},{10,... | collective-permute-start | bytes 172040 | tf_op jit(solution)/shard_map/ppermute | solution.py:202
  33.9 0.0 collective-permute-done.15
  33.9 0.6 %collective-permute-start.16 = (f32[16,896]{1,0:T(8,128)S(1)}, f32[16,896]{1,0:T(8,128)S(1)}, u32[]{:S(2)}, u32[]{:S(2)}) collective-permute-start(f32[16,896]{1,0:T(8,128)S(1)} %add.35.refs_1_), channel_id=1, source_target_pairs={{0,17},{1,16},{2,19},{3,18},{4,21},{5,20},{6,23},{7,22},{8,25},{9,... | collective-permute-start | bytes 172040 | tf_op jit(solution)/shard_map/ppermute | solution.py:202
  34.5 1.2 %collective-permute-start.19 = (f32[16,896]{1,0:T(8,128)S(1)}, f32[16,896]{1,0:T(8,128)S(1)}, u32[]{:S(2)}, u32[]{:S(2)}) collective-permute-start(f32[16,896]{1,0:T(8,128)S(1)} %add.35.refs_1_), channel_id=1, source_target_pairs={{0,9},{1,8},{2,11},{3,10},{4,13},{5,12},{6,15},{7,14},{8,1},{9,0},... | collective-permute-start | bytes 172040 | tf_op jit(solution)/shard_map/ppermute | solution.py:202
  35.7 1.8 %collective-permute-done.11 = f32[16,896]{1,0:T(8,128)S(1)} collective-permute-done((f32[16,896]{1,0:T(8,128)S(1)}, f32[16,896]{1,0:T(8,128)S(1)}, u32[]{:S(2)}, u32[]{:S(2)}) %collective-permute-start.11) | collective-permute-done | bytes 57376 | tf_op jit(solution)/shard_map/ppermute | solution.py:202
  37.5 1.2 %collective-permute-start.12 = (f32[16,896]{1,0:T(8,128)S(1)}, f32[16,896]{1,0:T(8,128)S(1)}, u32[]{:S(2)}, u32[]{:S(2)}) collective-permute-start(f32[16,896]{1,0:T(8,128)S(1)} %add.33.refs_0_), channel_id=1, source_target_pairs={{0,9},{1,8},{2,11},{3,10},{4,13},{5,12},{6,15},{7,14},{8,1},{9,0},... | collective-permute-start | bytes 172040 | tf_op jit(solution)/shard_map/ppermute | solution.py:202
  38.7 0.6 %collective-permute-start.20 = (f32[16,896]{1,0:T(8,128)S(1)}, f32[16,896]{1,0:T(8,128)S(1)}, u32[]{:S(2)}, u32[]{:S(2)}) collective-permute-start(f32[16,896]{1,0:T(8,128)S(1)} %add.33.refs_0_), channel_id=1, source_target_pairs={{0,17},{1,16},{2,19},{3,18},{4,21},{5,20},{6,23},{7,22},{8,25},{9,... | collective-permute-start | bytes 172040 | tf_op jit(solution)/shard_map/ppermute | solution.py:202
  39.2 0.0 collective-permute-done.16.refs_5_
  39.3 0.0 collective-permute-done.19.refs_3_
  39.3 2.2 %collective-permute-done.12.refs_2_ = f32[16,896]{1,0:T(8,128)S(1)} collective-permute-done((f32[16,896]{1,0:T(8,128)S(1)}, f32[16,896]{1,0:T(8,128)S(1)}, u32[]{:S(2)}, u32[]{:S(2)}) %collective-permute-start.12) | collective-permute-done | bytes 57376 | tf_op jit(solution)/shard_map/ppermute | solution.py:202
  41.5 0.9 %collective-permute-done.20.refs_4_ = f32[16,896]{1,0:T(8,128)S(1)} collective-permute-done((f32[16,896]{1,0:T(8,128)S(1)}, f32[16,896]{1,0:T(8,128)S(1)}, u32[]{:S(2)}, u32[]{:S(2)}) %collective-permute-start.20) | collective-permute-done | bytes 57376 | tf_op jit(solution)/shard_map/ppermute | solution.py:202
  42.4 0.5 collective-permute-start.21
  42.8 0.3 collective-permute-start.17
  43.1 0.7 %collective-permute-start.13 = (f32[16,896]{1,0:T(8,128)S(1)}, f32[16,896]{1,0:T(8,128)S(1)}, u32[]{:S(2)}, u32[]{:S(2)}) collective-permute-start(f32[16,896]{1,0:T(8,128)S(1)} %collective-permute-done.12.refs_2_), channel_id=1, source_target_pairs={{0,17},{1,16},{2,19},{3,18},{4,21},{5,20},{6,23},{7,22},{8,25},{9,... | collective-permute-start | bytes 172040 | tf_op jit(solution)/shard_map/ppermute | solution.py:202
  43.8 2.9 %collective-permute-done.17.refs_1_ = f32[16,896]{1,0:T(8,128)S(1)} collective-permute-done((f32[16,896]{1,0:T(8,128)S(1)}, f32[16,896]{1,0:T(8,128)S(1)}, u32[]{:S(2)}, u32[]{:S(2)}) %collective-permute-start.17) | collective-permute-done | bytes 57376 | tf_op jit(solution)/shard_map/ppermute | solution.py:202
  46.7 0.0 collective-permute-done.13.refs_0_
  46.8 0.5 collective-permute-start.18
  47.2 1.0 %shard_map.57 = (bf16[72,7168]{1,0:T(8,128)(2,1)}, f32[32,7168]{1,0:T(8,128)}) custom-call(bf16[72,7168]{1,0:T(8,128)(2,1)S(1)} %get-tuple-element.19.g, bf16[72,7168]{1,0:T(8,128)(2,1)S(1)} %get-tuple-element.20.f, f32[72,32]{1,0:T(8,128)S(1)} %get-tuple-element.21.basis, f32[96,896]{1,0:T(8,128)S(1)} %shard_map.56.refs_0_), custom_call_target="tpu_custom_call" | custom-call | flops 134217728 | bytes 2417664 | tf_op jit(solution)/shard_map/pallas_call | solution.py:23
  48.3 1.1 %shard_map.58 = (bf16[72,7168]{1,0:T(8,128)(2,1)}, f32[32,7168]{1,0:T(8,128)}) custom-call(bf16[72,7168]{1,0:T(8,128)(2,1)S(1)} %get-tuple-element.19.g, bf16[72,7168]{1,0:T(8,128)(2,1)S(1)} %get-tuple-element.20.f, f32[72,32]{1,0:T(8,128)S(1)} %get-tuple-element.21.basis, ...), custom_call_target="tpu_custom_call", output_to_operand_aliasing={{0}: (5, {}), {1}: (6, {})} | custom-call | flops 134217728 | bytes 4482048 | tf_op jit(solution)/shard_map/pallas_call | solution.py:23
  49.4 0.9 %shard_map.59 = (bf16[72,7168]{1,0:T(8,128)(2,1)}, f32[32,7168]{1,0:T(8,128)}) custom-call(bf16[72,7168]{1,0:T(8,128)(2,1)S(1)} %get-tuple-element.19.g, bf16[72,7168]{1,0:T(8,128)(2,1)S(1)} %get-tuple-element.20.f, f32[72,32]{1,0:T(8,128)S(1)} %get-tuple-element.21.basis, ...), custom_call_target="tpu_custom_call", output_to_operand_aliasing={{0}: (4, {}), {1}: (5, {})} | custom-call | flops 134217728 | bytes 4137984 | tf_op jit(solution)/shard_map/pallas_call | solution.py:23
  (15 shorter events, 0.1 us)
Async XLA Ops:
  0.6 2.3 %copy-start = (f32[7168,32]{0,1:T(8,128)S(1)}, f32[7168,32]{0,1:T(8,128)}, u32[]{:S(2)}) copy-start(f32[7168,32]{0,1:T(8,128)} %param.5) | copy-start | bytes 2752516
  2.4 5.1 %collective-permute-start.6 = (f32[72,3584]{1,0:T(8,128)S(1)}, f32[72,3584]{1,0:T(8,128)S(1)}, u32[]{:S(2)}, u32[]{:S(2)}) collective-permute-start(f32[72,3584]{1,0:T(8,128)S(1)} %get-tuple-element.23), channel_id=1, source_target_pairs={{0,1},{1,0},{2,3},{3,2},{4,5},{5,4},{6,7},{7,6},{8,9},{9,8},{10,11... | collective-permute-start | bytes 3096584 | tf_op jit(solution)/shard_map/ppermute | solution.py:205
  3.7 7.3 %collective-permute-start = (f32[32,72]{1,0:T(8,128)S(1)}, f32[32,72]{1,0:T(8,128)S(1)}, u32[]{:S(2)}, u32[]{:S(2)}) collective-permute-start(f32[32,72]{1,0:T(8,128)S(1)} %shard_map.51), channel_id=1, source_target_pairs={{0,9},{1,8},{2,11},{3,10},{4,13},{5,12},{6,15},{7,14},{8,1},{9,0},... | collective-permute-start | bytes 27656 | tf_op jit(solution)/shard_map/ppermute | solution.py:202
  6.3 4.7 %collective-permute-start.1 = (f32[32,72]{1,0:T(8,128)S(1)}, f32[32,72]{1,0:T(8,128)S(1)}, u32[]{:S(2)}, u32[]{:S(2)}) collective-permute-start(f32[32,72]{1,0:T(8,128)S(1)} %shard_map.51), channel_id=1, source_target_pairs={{0,17},{1,16},{2,19},{3,18},{4,21},{5,20},{6,23},{7,22},{8,25},{9,... | collective-permute-start | bytes 27656 | tf_op jit(solution)/shard_map/ppermute | solution.py:202
  7.4 4.1 %collective-permute-start.2 = (f32[32,72]{1,0:T(8,128)S(1)}, f32[32,72]{1,0:T(8,128)S(1)}, u32[]{:S(2)}, u32[]{:S(2)}) collective-permute-start(f32[32,72]{1,0:T(8,128)S(1)} %shard_map.51), channel_id=1, source_target_pairs={{0,25},{1,24},{2,27},{3,26},{4,29},{5,28},{6,31},{7,30},{8,17},{9,... | collective-permute-start | bytes 27656 | tf_op jit(solution)/shard_map/ppermute | solution.py:202
  7.6 14.6 %collective-permute-start.7 = (f32[72,896]{1,0:T(8,128)S(1)}, f32[72,896]{1,0:T(8,128)S(1)}, u32[]{:S(2)}, u32[]{:S(2)}) collective-permute-start(f32[72,896]{1,0:T(8,128)S(1)} %get-tuple-element.25), channel_id=1, source_target_pairs={{0,9},{1,8},{2,11},{3,10},{4,13},{5,12},{6,15},{7,14},{8,1},{9,0},... | collective-permute-start | bytes 774152 | tf_op jit(solution)/shard_map/ppermute | solution.py:202
  9.3 13.1 %collective-permute-start.8 = (f32[72,896]{1,0:T(8,128)S(1)}, f32[72,896]{1,0:T(8,128)S(1)}, u32[]{:S(2)}, u32[]{:S(2)}) collective-permute-start(f32[72,896]{1,0:T(8,128)S(1)} %get-tuple-element.26), channel_id=1, source_target_pairs={{0,17},{1,16},{2,19},{3,18},{4,21},{5,20},{6,23},{7,22},{8,25},{9,... | collective-permute-start | bytes 774152 | tf_op jit(solution)/shard_map/ppermute | solution.py:202
  11.0 12.4 %collective-permute-start.9 = (f32[72,896]{1,0:T(8,128)S(1)}, f32[72,896]{1,0:T(8,128)S(1)}, u32[]{:S(2)}, u32[]{:S(2)}) collective-permute-start(f32[72,896]{1,0:T(8,128)S(1)} %get-tuple-element.27), channel_id=1, source_target_pairs={{0,24},{1,25},{2,26},{3,27},{4,28},{5,29},{6,30},{7,31},{8,16},{9,... | collective-permute-start | bytes 774152 | tf_op jit(solution)/shard_map/ppermute | solution.py:202
  11.5 3.2 %collective-permute-start.3 = (f32[32,72]{1,0:T(8,128)S(1)}, f32[32,72]{1,0:T(8,128)S(1)}, u32[]{:S(2)}, u32[]{:S(2)}) collective-permute-start(f32[32,72]{1,0:T(8,128)S(1)} %add_add_fusion), channel_id=1, source_target_pairs={{0,3},{1,2},{2,1},{3,0},{4,7},{5,6},{6,5},{7,4},{8,11},{9,10},{10,... | collective-permute-start | bytes 27656 | tf_op jit(solution)/shard_map/ppermute | solution.py:202
  14.7 4.4 %collective-permute-start.4 = (f32[32,72]{1,0:T(8,128)S(1)}, f32[32,72]{1,0:T(8,128)S(1)}, u32[]{:S(2)}, u32[]{:S(2)}) collective-permute-start(f32[32,72]{1,0:T(8,128)S(1)} %add.30), channel_id=1, source_target_pairs={{0,5},{1,4},{2,7},{3,6},{4,1},{5,0},{6,3},{7,2},{8,13},{9,12},{10,... | collective-permute-start | bytes 27656 | tf_op jit(solution)/shard_map/ppermute | solution.py:202
  19.1 1.6 %collective-permute-start.5 = (f32[32,72]{1,0:T(8,128)S(1)}, f32[32,72]{1,0:T(8,128)S(1)}, u32[]{:S(2)}, u32[]{:S(2)}) collective-permute-start(f32[32,72]{1,0:T(8,128)S(1)} %add.31.a), channel_id=1, source_target_pairs={{0,1},{1,0},{2,3},{3,2},{4,5},{5,4},{6,7},{7,6},{8,9},{9,8},{10,11... | collective-permute-start | bytes 27656 | tf_op jit(solution)/shard_map/ppermute | solution.py:205
  23.7 4.9 %collective-permute-start.14 = (f32[16,896]{1,0:T(8,128)S(1)}, f32[16,896]{1,0:T(8,128)S(1)}, u32[]{:S(2)}, u32[]{:S(2)}) collective-permute-start(f32[16,896]{1,0:T(8,128)S(1)} %get-tuple-element.29), channel_id=1, source_target_pairs={{0,5},{1,4},{2,7},{3,6},{4,1},{5,0},{6,3},{7,2},{8,13},{9,12},{10,... | collective-permute-start | bytes 172040 | tf_op jit(solution)/shard_map/ppermute | solution.py:202
  25.9 4.5 %collective-permute-start.10 = (f32[16,896]{1,0:T(8,128)S(1)}, f32[16,896]{1,0:T(8,128)S(1)}, u32[]{:S(2)}, u32[]{:S(2)}) collective-permute-start(f32[16,896]{1,0:T(8,128)S(1)} %get-tuple-element.28), channel_id=1, source_target_pairs={{0,3},{1,2},{2,1},{3,0},{4,7},{5,6},{6,5},{7,4},{8,11},{9,10},{10,... | collective-permute-start | bytes 172040 | tf_op jit(solution)/shard_map/ppermute | solution.py:202
  28.6 5.3 %collective-permute-start.15 = (f32[16,896]{1,0:T(8,128)S(1)}, f32[16,896]{1,0:T(8,128)S(1)}, u32[]{:S(2)}, u32[]{:S(2)}) collective-permute-start(f32[16,896]{1,0:T(8,128)S(1)} %add.34), channel_id=1, source_target_pairs={{0,3},{1,2},{2,1},{3,0},{4,7},{5,6},{6,5},{7,4},{8,11},{9,10},{10,... | collective-permute-start | bytes 172040 | tf_op jit(solution)/shard_map/ppermute | solution.py:202
  30.4 7.1 %collective-permute-start.11 = (f32[16,896]{1,0:T(8,128)S(1)}, f32[16,896]{1,0:T(8,128)S(1)}, u32[]{:S(2)}, u32[]{:S(2)}) collective-permute-start(f32[16,896]{1,0:T(8,128)S(1)} %add.32), channel_id=1, source_target_pairs={{0,5},{1,4},{2,7},{3,6},{4,1},{5,0},{6,3},{7,2},{8,13},{9,12},{10,... | collective-permute-start | bytes 172040 | tf_op jit(solution)/shard_map/ppermute | solution.py:202
  33.9 5.3 %collective-permute-start.16 = (f32[16,896]{1,0:T(8,128)S(1)}, f32[16,896]{1,0:T(8,128)S(1)}, u32[]{:S(2)}, u32[]{:S(2)}) collective-permute-start(f32[16,896]{1,0:T(8,128)S(1)} %add.35.refs_1_), channel_id=1, source_target_pairs={{0,17},{1,16},{2,19},{3,18},{4,21},{5,20},{6,23},{7,22},{8,25},{9,... | collective-permute-start | bytes 172040 | tf_op jit(solution)/shard_map/ppermute | solution.py:202
  34.5 4.7 %collective-permute-start.19 = (f32[16,896]{1,0:T(8,128)S(1)}, f32[16,896]{1,0:T(8,128)S(1)}, u32[]{:S(2)}, u32[]{:S(2)}) collective-permute-start(f32[16,896]{1,0:T(8,128)S(1)} %add.35.refs_1_), channel_id=1, source_target_pairs={{0,9},{1,8},{2,11},{3,10},{4,13},{5,12},{6,15},{7,14},{8,1},{9,0},... | collective-permute-start | bytes 172040 | tf_op jit(solution)/shard_map/ppermute | solution.py:202
  37.5 4.0 %collective-permute-start.12 = (f32[16,896]{1,0:T(8,128)S(1)}, f32[16,896]{1,0:T(8,128)S(1)}, u32[]{:S(2)}, u32[]{:S(2)}) collective-permute-start(f32[16,896]{1,0:T(8,128)S(1)} %add.33.refs_0_), channel_id=1, source_target_pairs={{0,9},{1,8},{2,11},{3,10},{4,13},{5,12},{6,15},{7,14},{8,1},{9,0},... | collective-permute-start | bytes 172040 | tf_op jit(solution)/shard_map/ppermute | solution.py:202
  38.7 3.6 %collective-permute-start.20 = (f32[16,896]{1,0:T(8,128)S(1)}, f32[16,896]{1,0:T(8,128)S(1)}, u32[]{:S(2)}, u32[]{:S(2)}) collective-permute-start(f32[16,896]{1,0:T(8,128)S(1)} %add.33.refs_0_), channel_id=1, source_target_pairs={{0,17},{1,16},{2,19},{3,18},{4,21},{5,20},{6,23},{7,22},{8,25},{9,... | collective-permute-start | bytes 172040 | tf_op jit(solution)/shard_map/ppermute | solution.py:202
  42.4 5.9 %collective-permute-start.21 = (f32[96,896]{1,0:T(8,128)S(1)}, f32[96,896]{1,0:T(8,128)S(1)}, u32[]{:S(2)}, u32[]{:S(2)}) collective-permute-start(f32[96,896]{1,0:T(8,128)S(1)} %shard_map.56.refs_0_), channel_id=1, source_target_pairs={{0,1},{1,0},{2,3},{3,2},{4,5},{5,4},{6,7},{7,6},{8,9},{9,8},{10,11... | collective-permute-start | bytes 1032200 | tf_op jit(solution)/shard_map/ppermute | solution.py:205
  42.8 3.9 %collective-permute-start.17 = (f32[16,896]{1,0:T(8,128)S(1)}, f32[16,896]{1,0:T(8,128)S(1)}, u32[]{:S(2)}, u32[]{:S(2)}) collective-permute-start(f32[16,896]{1,0:T(8,128)S(1)} %collective-permute-done.16.refs_5_), channel_id=1, source_target_pairs={{0,9},{1,8},{2,11},{3,10},{4,13},{5,12},{6,15},{7,14},{8,1},{9,0},... | collective-permute-start | bytes 172040 | tf_op jit(solution)/shard_map/ppermute | solution.py:202
  43.1 3.6 %collective-permute-start.13 = (f32[16,896]{1,0:T(8,128)S(1)}, f32[16,896]{1,0:T(8,128)S(1)}, u32[]{:S(2)}, u32[]{:S(2)}) collective-permute-start(f32[16,896]{1,0:T(8,128)S(1)} %collective-permute-done.12.refs_2_), channel_id=1, source_target_pairs={{0,17},{1,16},{2,19},{3,18},{4,21},{5,20},{6,23},{7,22},{8,25},{9,... | collective-permute-start | bytes 172040 | tf_op jit(solution)/shard_map/ppermute | solution.py:202
  46.8 2.7 %collective-permute-start.18 = (f32[32,896]{1,0:T(8,128)S(1)}, f32[32,896]{1,0:T(8,128)S(1)}, u32[]{:S(2)}, u32[]{:S(2)}) collective-permute-start(f32[32,896]{1,0:T(8,128)S(1)} %shard_map.55.refs_1_), channel_id=1, source_target_pairs={{0,1},{1,0},{2,3},{3,2},{4,5},{5,4},{6,7},{7,6},{8,9},{9,8},{10,11... | collective-permute-start | bytes 344072 | tf_op jit(solution)/shard_map/ppermute | solution.py:205

commit v8 on v7

--- a/solution.py
+++ b/solution.py
@@ -204,15 +204,20 @@
     def swap(value):
         return lax.ppermute(value, AXES, [(i, i ^ 1) for i in range(local * dp)])
 
-    def total_over(value, along_local, direct=False, cross=None, turn=0):
+    def total_over(value, along_local, direct=False, cross=None, turn=0, only=None):
         size = local if along_local else groups
-        double = not direct and not size & (size - 1)
+        double = not (direct and size <= 4) and not size & (size - 1)
         first = value
-        steps = [1 << i for i in range(size.bit_length() - 1)] if double else range(1, size)
+        steps = doubling(size) if double else range(1, size)
+        if only is not None:
+            steps = only
         for step in steps[::-1] if turn else steps:
             other = permute(value if double else first, along_local, step, cross)
             value = value + other
         return value
+
+    def doubling(size):
+        return [] if size & (size - 1) else [1 << i for i in range(size.bit_length() - 1)]
 
     def gather(own, turn):
         if local & (local - 1):
@@ -234,14 +239,20 @@
     )
     left = call(left_kernel, ((rank, rows), F32), g, f, b, flops=1 << 27)
     got = swap(send)
+    near = doubling(groups)[:1] or None
+    left = total_over(left, False, cross=1, only=near)
+    other = swap(left)
+    left = left + other
     left = total_over(left, True, direct=True, cross=1)
     chunks = call(pair_kernel, [((rows, width), F32)] * local, g, f, got)
     terms = [chunks[0]] + [permute(chunks[s], True, s) for s in range(1, local)]
-    left = total_over(left, False, cross=1)
+    far = doubling(groups)[1:]
+    left = total_over(left, False, cross=1, only=far[:-1])
+    other = permute(left, False, far[-1], 1) if far else jnp.zeros_like(left)
     basis, basis_t = call(
         functools.partial(gram_schmidt_kernel, 4),
         [((rows, rank), F32), ((rank, rows), F32)],
-        left, swap(left), flops=1 << 26,
+        left, other, flops=1 << 26,
     )
     rights = call(right_kernel, [((rank // PARTS, width), F32)] * PARTS, basis_t, *terms, flops=1 << 25)
     gathered = []

time: 50.5 us -> 58.6 us (1.16)
  waiting for transfers between devices: 14.3 us -> 21.2 us
  starting transfers between devices: 27.8 us -> 28.9 us
    ppermute x18, waiting for transfers between devices: 13.4 us -> 20.1 us  [permute(): return lax.ppermute(value, AXES, pairs)]
    ppermute x18, starting transfers between devices: 25.6 us -> 27.6 us  [permute(): return lax.ppermute(value, AXES, pairs)]
    ppermute x4, starting transfers between devices: 2.21 us -> 1.3 us  [swap(): return lax.ppermute(value, AXES, [(i, i ^ 1) for i in range(local * dp)])]
  transfers between devices with their start and end apart: 22 -> 22, of which waited for: 11 -> 11; matrix products, arithmetic and copies ran while one was open for 0% -> 0% of each run, Pallas kernels for 9% -> 8%
where the time goes in v8:
time: 58.6 us; the launch traced here: 58.5 us
  starting transfers between devices  28.9 us (49%)
  waiting for transfers between devices  21.2 us (36%)
  Pallas kernels  7.53 us (13%)
  between operations  0.74 us (1%)
    ppermute x18, starting transfers between devices, permute(): return lax.ppermute(value, AXES, pairs)  27.6 us
    ppermute x18, waiting for transfers between devices, permute(): return lax.ppermute(value, AXES, pairs)  20.1 us
    pallas_call x10, Pallas kernels, call(): pl.pallas_call(kernel, out_shape=shapes, in_specs=[pl.BlockSpec(memory_sp...  7.53 us
    ppermute x4, starting transfers between devices, swap(): return lax.ppermute(value, AXES, [(i, i ^ 1) for i in range(local * dp)])  1.3 us
  transfers between devices with their start and end apart: 22, of which 11 were waited for; matrix products, arithmetic and copies ran while one was open for 0% of the time, Pallas kernels for 8%

profile of v8, /device:TPU:0, one launch (start us, length us, event | category | flops | bytes accessed | tf_op | source)
XLA Modules:
  0.0 58.5 jit_solution(8498158493591727789)
XLA Ops:
  0.6 1.7 %shard_map.50 = (bf16[72,7168]{1,0:T(8,128)(2,1)S(1)}, bf16[72,7168]{1,0:T(8,128)(2,1)S(1)}, f32[72,3584]{1,0:T(8,128)S(1)}) custom-call(bf16[72,7168]{1,0:T(8,128)(2,1)} %bitcast.8, bf16[72,7168]{1,0:T(8,128)(2,1)} %bitcast.9), custom_call_target="tpu_custom_call" | custom-call | flops 1048576 | bytes 2064384 | tf_op jit(solution)/shard_map/pallas_call | solution.py:23
  2.4 0.6 collective-permute-start.6
  2.9 0.7 %shard_map.51 = f32[32,72]{1,0:T(8,128)S(1)} custom-call(bf16[72,7168]{1,0:T(8,128)(2,1)S(1)} %get-tuple-element.19.g, bf16[72,7168]{1,0:T(8,128)(2,1)S(1)} %get-tuple-element.20.f, f32[32,7168]{1,0:T(8,128)S(1)} %bitcast.5), custom_call_target="tpu_custom_call" | custom-call | flops 134217728 | bytes 2981888 | tf_op jit(solution)/shard_map/pallas_call | solution.py:23
  3.7 2.7 %collective-permute-start = (f32[32,72]{1,0:T(8,128)S(1)}, f32[32,72]{1,0:T(8,128)S(1)}, u32[]{:S(2)}, u32[]{:S(2)}) collective-permute-start(f32[32,72]{1,0:T(8,128)S(1)} %shard_map.51), channel_id=1, source_target_pairs={{0,3},{1,2},{2,1},{3,0},{4,7},{5,6},{6,5},{7,4},{8,11},{9,10},{10,... | collective-permute-start | bytes 27656 | tf_op jit(solution)/shard_map/ppermute | solution.py:202
  6.4 1.4 %collective-permute-done = f32[32,72]{1,0:T(8,128)S(1)} collective-permute-done((f32[32,72]{1,0:T(8,128)S(1)}, f32[32,72]{1,0:T(8,128)S(1)}, u32[]{:S(2)}, u32[]{:S(2)}) %collective-permute-start) | collective-permute-done | bytes 9248 | tf_op jit(solution)/shard_map/ppermute | solution.py:202
  7.8 0.1 collective-permute-start.1
  7.9 1.1 %collective-permute-done.1 = f32[32,72]{1,0:T(8,128)S(1)} collective-permute-done((f32[32,72]{1,0:T(8,128)S(1)}, f32[32,72]{1,0:T(8,128)S(1)}, u32[]{:S(2)}, u32[]{:S(2)}) %collective-permute-start.1) | collective-permute-done | bytes 9248 | tf_op jit(solution)/shard_map/ppermute | solution.py:205
  9.0 1.6 %collective-permute-start.2 = (f32[32,72]{1,0:T(8,128)S(1)}, f32[32,72]{1,0:T(8,128)S(1)}, u32[]{:S(2)}, u32[]{:S(2)}) collective-permute-start(f32[32,72]{1,0:T(8,128)S(1)} %add.28), channel_id=1, source_target_pairs={{0,9},{1,8},{2,11},{3,10},{4,13},{5,12},{6,15},{7,14},{8,1},{9,0},... | collective-permute-start | bytes 27656 | tf_op jit(solution)/shard_map/ppermute | solution.py:202
  10.6 0.0 collective-permute-done.6.got
  10.6 0.2 shard_map.53
  10.8 0.2 collective-permute-start.7
  11.0 1.7 %collective-permute-start.8 = (f32[72,896]{1,0:T(8,128)S(1)}, f32[72,896]{1,0:T(8,128)S(1)}, u32[]{:S(2)}, u32[]{:S(2)}) collective-permute-start(f32[72,896]{1,0:T(8,128)S(1)} %get-tuple-element.26), channel_id=1, source_target_pairs={{0,17},{1,16},{2,19},{3,18},{4,21},{5,20},{6,23},{7,22},{8,25},{9,... | collective-permute-start | bytes 774152 | tf_op jit(solution)/shard_map/ppermute | solution.py:202
  12.6 1.4 %collective-permute-start.9 = (f32[72,896]{1,0:T(8,128)S(1)}, f32[72,896]{1,0:T(8,128)S(1)}, u32[]{:S(2)}, u32[]{:S(2)}) collective-permute-start(f32[72,896]{1,0:T(8,128)S(1)} %get-tuple-element.27), channel_id=1, source_target_pairs={{0,24},{1,25},{2,26},{3,27},{4,28},{5,29},{6,30},{7,31},{8,16},{9,... | collective-permute-start | bytes 774152 | tf_op jit(solution)/shard_map/ppermute | solution.py:202
  14.1 1.0 %collective-permute-start.3 = (f32[32,72]{1,0:T(8,128)S(1)}, f32[32,72]{1,0:T(8,128)S(1)}, u32[]{:S(2)}, u32[]{:S(2)}) collective-permute-start(f32[32,72]{1,0:T(8,128)S(1)} %add.28), channel_id=1, source_target_pairs={{0,17},{1,16},{2,19},{3,18},{4,21},{5,20},{6,23},{7,22},{8,25},{9,... | collective-permute-start | bytes 27656 | tf_op jit(solution)/shard_map/ppermute | solution.py:202
  15.1 0.0 collective-permute-done.2
  15.1 0.4 collective-permute-start.4
  15.5 9.5 %collective-permute-done.3 = f32[32,72]{1,0:T(8,128)S(1)} collective-permute-done((f32[32,72]{1,0:T(8,128)S(1)}, f32[32,72]{1,0:T(8,128)S(1)}, u32[]{:S(2)}, u32[]{:S(2)}) %collective-permute-start.3) | collective-permute-done | bytes 9248 | tf_op jit(solution)/shard_map/ppermute | solution.py:202
  25.0 0.9 %collective-permute-done.4 = f32[32,72]{1,0:T(8,128)S(1)} collective-permute-done((f32[32,72]{1,0:T(8,128)S(1)}, f32[32,72]{1,0:T(8,128)S(1)}, u32[]{:S(2)}, u32[]{:S(2)}) %collective-permute-start.4) | collective-permute-done | bytes 9248 | tf_op jit(solution)/shard_map/ppermute | solution.py:202
  25.9 2.4 %collective-permute-start.5 = (f32[32,72]{1,0:T(8,128)S(1)}, f32[32,72]{1,0:T(8,128)S(1)}, u32[]{:S(2)}, u32[]{:S(2)}) collective-permute-start(f32[32,72]{1,0:T(8,128)S(1)} %add_add_fusion.a), channel_id=1, source_target_pairs={{0,5},{1,4},{2,7},{3,6},{4,1},{5,0},{6,3},{7,2},{8,13},{9,12},{10,... | collective-permute-start | bytes 27656 | tf_op jit(solution)/shard_map/ppermute | solution.py:202
  28.4 1.6 %collective-permute-done.5.b = f32[32,72]{1,0:T(8,128)S(1)} collective-permute-done((f32[32,72]{1,0:T(8,128)S(1)}, f32[32,72]{1,0:T(8,128)S(1)}, u32[]{:S(2)}, u32[]{:S(2)}) %collective-permute-start.5) | collective-permute-done | bytes 9248 | tf_op jit(solution)/shard_map/ppermute | solution.py:202
  30.0 1.5 %shard_map.52 = (f32[72,32]{1,0:T(8,128)S(1)}, f32[32,72]{1,0:T(8,128)S(1)}) custom-call(f32[32,72]{1,0:T(8,128)S(1)} %add_add_fusion.a, f32[32,72]{1,0:T(8,128)S(1)} %collective-permute-done.5.b), custom_call_target="tpu_custom_call" | custom-call | flops 67108864 | bytes 18432 | tf_op jit(solution)/shard_map/pallas_call | solution.py:23
  31.5 0.0 collective-permute-done.7.refs_1_
  31.5 0.0 collective-permute-done.8.refs_2_
  31.5 0.3 shard_map.54
  31.8 2.5 %collective-permute-start.14 = (f32[16,896]{1,0:T(8,128)S(1)}, f32[16,896]{1,0:T(8,128)S(1)}, u32[]{:S(2)}, u32[]{:S(2)}) collective-permute-start(f32[16,896]{1,0:T(8,128)S(1)} %get-tuple-element.29), channel_id=1, source_target_pairs={{0,5},{1,4},{2,7},{3,6},{4,1},{5,0},{6,3},{7,2},{8,13},{9,12},{10,... | collective-permute-start | bytes 172040 | tf_op jit(solution)/shard_map/ppermute | solution.py:202
  34.3 1.5 %collective-permute-start.10 = (f32[16,896]{1,0:T(8,128)S(1)}, f32[16,896]{1,0:T(8,128)S(1)}, u32[]{:S(2)}, u32[]{:S(2)}) collective-permute-start(f32[16,896]{1,0:T(8,128)S(1)} %get-tuple-element.28), channel_id=1, source_target_pairs={{0,3},{1,2},{2,1},{3,0},{4,7},{5,6},{6,5},{7,4},{8,11},{9,10},{10,... | collective-permute-start | bytes 172040 | tf_op jit(solution)/shard_map/ppermute | solution.py:202
  35.7 0.8 %collective-permute-done.14 = f32[16,896]{1,0:T(8,128)S(1)} collective-permute-done((f32[16,896]{1,0:T(8,128)S(1)}, f32[16,896]{1,0:T(8,128)S(1)}, u32[]{:S(2)}, u32[]{:S(2)}) %collective-permute-start.14) | collective-permute-done | bytes 57376 | tf_op jit(solution)/shard_map/ppermute | solution.py:202
  36.5 2.0 %collective-permute-start.15 = (f32[16,896]{1,0:T(8,128)S(1)}, f32[16,896]{1,0:T(8,128)S(1)}, u32[]{:S(2)}, u32[]{:S(2)}) collective-permute-start(f32[16,896]{1,0:T(8,128)S(1)} %add.34), channel_id=1, source_target_pairs={{0,3},{1,2},{2,1},{3,0},{4,7},{5,6},{6,5},{7,4},{8,11},{9,10},{10,... | collective-permute-start | bytes 172040 | tf_op jit(solution)/shard_map/ppermute | solution.py:202
  38.5 3.5 %collective-permute-start.11 = (f32[16,896]{1,0:T(8,128)S(1)}, f32[16,896]{1,0:T(8,128)S(1)}, u32[]{:S(2)}, u32[]{:S(2)}) collective-permute-start(f32[16,896]{1,0:T(8,128)S(1)} %add.32), channel_id=1, source_target_pairs={{0,5},{1,4},{2,7},{3,6},{4,1},{5,0},{6,3},{7,2},{8,13},{9,12},{10,... | collective-permute-start | bytes 172040 | tf_op jit(solution)/shard_map/ppermute | solution.py:202
  42.0 0.0 collective-permute-done.15
  42.0 0.9 %collective-permute-start.16 = (f32[16,896]{1,0:T(8,128)S(1)}, f32[16,896]{1,0:T(8,128)S(1)}, u32[]{:S(2)}, u32[]{:S(2)}) collective-permute-start(f32[16,896]{1,0:T(8,128)S(1)} %add.35.refs_1_), channel_id=1, source_target_pairs={{0,17},{1,16},{2,19},{3,18},{4,21},{5,20},{6,23},{7,22},{8,25},{9,... | collective-permute-start | bytes 172040 | tf_op jit(solution)/shard_map/ppermute | solution.py:202
  42.9 1.6 %collective-permute-start.19 = (f32[16,896]{1,0:T(8,128)S(1)}, f32[16,896]{1,0:T(8,128)S(1)}, u32[]{:S(2)}, u32[]{:S(2)}) collective-permute-start(f32[16,896]{1,0:T(8,128)S(1)} %add.35.refs_1_), channel_id=1, source_target_pairs={{0,9},{1,8},{2,11},{3,10},{4,13},{5,12},{6,15},{7,14},{8,1},{9,0},... | collective-permute-start | bytes 172040 | tf_op jit(solution)/shard_map/ppermute | solution.py:202
  44.5 1.1 %collective-permute-done.11 = f32[16,896]{1,0:T(8,128)S(1)} collective-permute-done((f32[16,896]{1,0:T(8,128)S(1)}, f32[16,896]{1,0:T(8,128)S(1)}, u32[]{:S(2)}, u32[]{:S(2)}) %collective-permute-start.11) | collective-permute-done | bytes 57376 | tf_op jit(solution)/shard_map/ppermute | solution.py:202
  45.6 0.2 collective-permute-start.12
  45.7 2.3 %collective-permute-start.20 = (f32[16,896]{1,0:T(8,128)S(1)}, f32[16,896]{1,0:T(8,128)S(1)}, u32[]{:S(2)}, u32[]{:S(2)}) collective-permute-start(f32[16,896]{1,0:T(8,128)S(1)} %add.33.refs_0_), channel_id=1, source_target_pairs={{0,17},{1,16},{2,19},{3,18},{4,21},{5,20},{6,23},{7,22},{8,25},{9,... | collective-permute-start | bytes 172040 | tf_op jit(solution)/shard_map/ppermute | solution.py:202
  48.0 0.0 collective-permute-done.16.refs_5_
  48.0 0.0 collective-permute-done.19.refs_3_
  48.0 1.5 %collective-permute-done.12.refs_2_ = f32[16,896]{1,0:T(8,128)S(1)} collective-permute-done((f32[16,896]{1,0:T(8,128)S(1)}, f32[16,896]{1,0:T(8,128)S(1)}, u32[]{:S(2)}, u32[]{:S(2)}) %collective-permute-start.12) | collective-permute-done | bytes 57376 | tf_op jit(solution)/shard_map/ppermute | solution.py:202
  49.6 0.7 %collective-permute-done.20.refs_4_ = f32[16,896]{1,0:T(8,128)S(1)} collective-permute-done((f32[16,896]{1,0:T(8,128)S(1)}, f32[16,896]{1,0:T(8,128)S(1)}, u32[]{:S(2)}, u32[]{:S(2)}) %collective-permute-start.20) | collective-permute-done | bytes 57376 | tf_op jit(solution)/shard_map/ppermute | solution.py:202
  50.2 0.2 collective-permute-start.21
  50.4 0.8 %collective-permute-start.17 = (f32[16,896]{1,0:T(8,128)S(1)}, f32[16,896]{1,0:T(8,128)S(1)}, u32[]{:S(2)}, u32[]{:S(2)}) collective-permute-start(f32[16,896]{1,0:T(8,128)S(1)} %collective-permute-done.16.refs_5_), channel_id=1, source_target_pairs={{0,9},{1,8},{2,11},{3,10},{4,13},{5,12},{6,15},{7,14},{8,1},{9,0},... | collective-permute-start | bytes 172040 | tf_op jit(solution)/shard_map/ppermute | solution.py:202
  51.2 1.1 %collective-permute-start.13 = (f32[16,896]{1,0:T(8,128)S(1)}, f32[16,896]{1,0:T(8,128)S(1)}, u32[]{:S(2)}, u32[]{:S(2)}) collective-permute-start(f32[16,896]{1,0:T(8,128)S(1)} %collective-permute-done.12.refs_2_), channel_id=1, source_target_pairs={{0,17},{1,16},{2,19},{3,18},{4,21},{5,20},{6,23},{7,22},{8,25},{9,... | collective-permute-start | bytes 172040 | tf_op jit(solution)/shard_map/ppermute | solution.py:202
  52.3 1.7 %collective-permute-done.17.refs_1_ = f32[16,896]{1,0:T(8,128)S(1)} collective-permute-done((f32[16,896]{1,0:T(8,128)S(1)}, f32[16,896]{1,0:T(8,128)S(1)}, u32[]{:S(2)}, u32[]{:S(2)}) %collective-permute-start.17) | collective-permute-done | bytes 57376 | tf_op jit(solution)/shard_map/ppermute | solution.py:202
  54.1 0.8 %collective-permute-done.13.refs_0_ = f32[16,896]{1,0:T(8,128)S(1)} collective-permute-done((f32[16,896]{1,0:T(8,128)S(1)}, f32[16,896]{1,0:T(8,128)S(1)}, u32[]{:S(2)}, u32[]{:S(2)}) %collective-permute-start.13) | collective-permute-done | bytes 57376 | tf_op jit(solution)/shard_map/ppermute | solution.py:202
  54.9 0.5 collective-permute-start.18
  55.3 1.0 %shard_map.57 = (bf16[72,7168]{1,0:T(8,128)(2,1)}, f32[32,7168]{1,0:T(8,128)}) custom-call(bf16[72,7168]{1,0:T(8,128)(2,1)S(1)} %get-tuple-element.19.g, bf16[72,7168]{1,0:T(8,128)(2,1)S(1)} %get-tuple-element.20.f, f32[72,32]{1,0:T(8,128)S(1)} %get-tuple-element.21.basis, f32[96,896]{1,0:T(8,128)S(1)} %shard_map.56.refs_0_), custom_call_target="tpu_custom_call" | custom-call | flops 134217728 | bytes 2417664 | tf_op jit(solution)/shard_map/pallas_call | solution.py:23
  56.4 1.1 %shard_map.58 = (bf16[72,7168]{1,0:T(8,128)(2,1)}, f32[32,7168]{1,0:T(8,128)}) custom-call(bf16[72,7168]{1,0:T(8,128)(2,1)S(1)} %get-tuple-element.19.g, bf16[72,7168]{1,0:T(8,128)(2,1)S(1)} %get-tuple-element.20.f, f32[72,32]{1,0:T(8,128)S(1)} %get-tuple-element.21.basis, ...), custom_call_target="tpu_custom_call", output_to_operand_aliasing={{0}: (5, {}), {1}: (6, {})} | custom-call | flops 134217728 | bytes 4482048 | tf_op jit(solution)/shard_map/pallas_call | solution.py:23
  57.5 0.9 %shard_map.59 = (bf16[72,7168]{1,0:T(8,128)(2,1)}, f32[32,7168]{1,0:T(8,128)}) custom-call(bf16[72,7168]{1,0:T(8,128)(2,1)S(1)} %get-tuple-element.19.g, bf16[72,7168]{1,0:T(8,128)(2,1)S(1)} %get-tuple-element.20.f, f32[72,32]{1,0:T(8,128)S(1)} %get-tuple-element.21.basis, ...), custom_call_target="tpu_custom_call", output_to_operand_aliasing={{0}: (4, {}), {1}: (5, {})} | custom-call | flops 134217728 | bytes 4137984 | tf_op jit(solution)/shard_map/pallas_call | solution.py:23
  (15 shorter events, 0.1 us)
Async XLA Ops:
  0.6 2.3 %copy-start = (f32[7168,32]{0,1:T(8,128)S(1)}, f32[7168,32]{0,1:T(8,128)}, u32[]{:S(2)}) copy-start(f32[7168,32]{0,1:T(8,128)} %param.5) | copy-start | bytes 2752516
  2.4 8.3 %collective-permute-start.6 = (f32[72,3584]{1,0:T(8,128)S(1)}, f32[72,3584]{1,0:T(8,128)S(1)}, u32[]{:S(2)}, u32[]{:S(2)}) collective-permute-start(f32[72,3584]{1,0:T(8,128)S(1)} %get-tuple-element.23), channel_id=1, source_target_pairs={{0,1},{1,0},{2,3},{3,2},{4,5},{5,4},{6,7},{7,6},{8,9},{9,8},{10,11... | collective-permute-start | bytes 3096584 | tf_op jit(solution)/shard_map/ppermute | solution.py:205
  3.7 4.1 %collective-permute-start = (f32[32,72]{1,0:T(8,128)S(1)}, f32[32,72]{1,0:T(8,128)S(1)}, u32[]{:S(2)}, u32[]{:S(2)}) collective-permute-start(f32[32,72]{1,0:T(8,128)S(1)} %shard_map.51), channel_id=1, source_target_pairs={{0,3},{1,2},{2,1},{3,0},{4,7},{5,6},{6,5},{7,4},{8,11},{9,10},{10,... | collective-permute-start | bytes 27656 | tf_op jit(solution)/shard_map/ppermute | solution.py:202
  7.8 1.2 %collective-permute-start.1 = (f32[32,72]{1,0:T(8,128)S(1)}, f32[32,72]{1,0:T(8,128)S(1)}, u32[]{:S(2)}, u32[]{:S(2)}) collective-permute-start(f32[32,72]{1,0:T(8,128)S(1)} %add.27), channel_id=1, source_target_pairs={{0,1},{1,0},{2,3},{3,2},{4,5},{5,4},{6,7},{7,6},{8,9},{9,8},{10,11... | collective-permute-start | bytes 27656 | tf_op jit(solution)/shard_map/ppermute | solution.py:205
  9.0 6.1 %collective-permute-start.2 = (f32[32,72]{1,0:T(8,128)S(1)}, f32[32,72]{1,0:T(8,128)S(1)}, u32[]{:S(2)}, u32[]{:S(2)}) collective-permute-start(f32[32,72]{1,0:T(8,128)S(1)} %add.28), channel_id=1, source_target_pairs={{0,9},{1,8},{2,11},{3,10},{4,13},{5,12},{6,15},{7,14},{8,1},{9,0},... | collective-permute-start | bytes 27656 | tf_op jit(solution)/shard_map/ppermute | solution.py:202
  10.8 20.7 %collective-permute-start.7 = (f32[72,896]{1,0:T(8,128)S(1)}, f32[72,896]{1,0:T(8,128)S(1)}, u32[]{:S(2)}, u32[]{:S(2)}) collective-permute-start(f32[72,896]{1,0:T(8,128)S(1)} %get-tuple-element.25), channel_id=1, source_target_pairs={{0,9},{1,8},{2,11},{3,10},{4,13},{5,12},{6,15},{7,14},{8,1},{9,0},... | collective-permute-start | bytes 774152 | tf_op jit(solution)/shard_map/ppermute | solution.py:202
  11.0 20.5 %collective-permute-start.8 = (f32[72,896]{1,0:T(8,128)S(1)}, f32[72,896]{1,0:T(8,128)S(1)}, u32[]{:S(2)}, u32[]{:S(2)}) collective-permute-start(f32[72,896]{1,0:T(8,128)S(1)} %get-tuple-element.26), channel_id=1, source_target_pairs={{0,17},{1,16},{2,19},{3,18},{4,21},{5,20},{6,23},{7,22},{8,25},{9,... | collective-permute-start | bytes 774152 | tf_op jit(solution)/shard_map/ppermute | solution.py:202
  12.6 18.9 %collective-permute-start.9 = (f32[72,896]{1,0:T(8,128)S(1)}, f32[72,896]{1,0:T(8,128)S(1)}, u32[]{:S(2)}, u32[]{:S(2)}) collective-permute-start(f32[72,896]{1,0:T(8,128)S(1)} %get-tuple-element.27), channel_id=1, source_target_pairs={{0,24},{1,25},{2,26},{3,27},{4,28},{5,29},{6,30},{7,31},{8,16},{9,... | collective-permute-start | bytes 774152 | tf_op jit(solution)/shard_map/ppermute | solution.py:202
  14.1 10.9 %collective-permute-start.3 = (f32[32,72]{1,0:T(8,128)S(1)}, f32[32,72]{1,0:T(8,128)S(1)}, u32[]{:S(2)}, u32[]{:S(2)}) collective-permute-start(f32[32,72]{1,0:T(8,128)S(1)} %add.28), channel_id=1, source_target_pairs={{0,17},{1,16},{2,19},{3,18},{4,21},{5,20},{6,23},{7,22},{8,25},{9,... | collective-permute-start | bytes 27656 | tf_op jit(solution)/shard_map/ppermute | solution.py:202
  15.1 10.8 %collective-permute-start.4 = (f32[32,72]{1,0:T(8,128)S(1)}, f32[32,72]{1,0:T(8,128)S(1)}, u32[]{:S(2)}, u32[]{:S(2)}) collective-permute-start(f32[32,72]{1,0:T(8,128)S(1)} %add.28), channel_id=1, source_target_pairs={{0,25},{1,24},{2,27},{3,26},{4,29},{5,28},{6,31},{7,30},{8,17},{9,... | collective-permute-start | bytes 27656 | tf_op jit(solution)/shard_map/ppermute | solution.py:202
  25.9 4.1 %collective-permute-start.5 = (f32[32,72]{1,0:T(8,128)S(1)}, f32[32,72]{1,0:T(8,128)S(1)}, u32[]{:S(2)}, u32[]{:S(2)}) collective-permute-start(f32[32,72]{1,0:T(8,128)S(1)} %add_add_fusion.a), channel_id=1, source_target_pairs={{0,5},{1,4},{2,7},{3,6},{4,1},{5,0},{6,3},{7,2},{8,13},{9,12},{10,... | collective-permute-start | bytes 27656 | tf_op jit(solution)/shard_map/ppermute | solution.py:202
  31.8 4.7 %collective-permute-start.14 = (f32[16,896]{1,0:T(8,128)S(1)}, f32[16,896]{1,0:T(8,128)S(1)}, u32[]{:S(2)}, u32[]{:S(2)}) collective-permute-start(f32[16,896]{1,0:T(8,128)S(1)} %get-tuple-element.29), channel_id=1, source_target_pairs={{0,5},{1,4},{2,7},{3,6},{4,1},{5,0},{6,3},{7,2},{8,13},{9,12},{10,... | collective-permute-start | bytes 172040 | tf_op jit(solution)/shard_map/ppermute | solution.py:202
  34.3 4.2 %collective-permute-start.10 = (f32[16,896]{1,0:T(8,128)S(1)}, f32[16,896]{1,0:T(8,128)S(1)}, u32[]{:S(2)}, u32[]{:S(2)}) collective-permute-start(f32[16,896]{1,0:T(8,128)S(1)} %get-tuple-element.28), channel_id=1, source_target_pairs={{0,3},{1,2},{2,1},{3,0},{4,7},{5,6},{6,5},{7,4},{8,11},{9,10},{10,... | collective-permute-start | bytes 172040 | tf_op jit(solution)/shard_map/ppermute | solution.py:202
  36.5 5.5 %collective-permute-start.15 = (f32[16,896]{1,0:T(8,128)S(1)}, f32[16,896]{1,0:T(8,128)S(1)}, u32[]{:S(2)}, u32[]{:S(2)}) collective-permute-start(f32[16,896]{1,0:T(8,128)S(1)} %add.34), channel_id=1, source_target_pairs={{0,3},{1,2},{2,1},{3,0},{4,7},{5,6},{6,5},{7,4},{8,11},{9,10},{10,... | collective-permute-start | bytes 172040 | tf_op jit(solution)/shard_map/ppermute | solution.py:202
  38.5 7.0 %collective-permute-start.11 = (f32[16,896]{1,0:T(8,128)S(1)}, f32[16,896]{1,0:T(8,128)S(1)}, u32[]{:S(2)}, u32[]{:S(2)}) collective-permute-start(f32[16,896]{1,0:T(8,128)S(1)} %add.32), channel_id=1, source_target_pairs={{0,5},{1,4},{2,7},{3,6},{4,1},{5,0},{6,3},{7,2},{8,13},{9,12},{10,... | collective-permute-start | bytes 172040 | tf_op jit(solution)/shard_map/ppermute | solution.py:202
  42.0 6.0 %collective-permute-start.16 = (f32[16,896]{1,0:T(8,128)S(1)}, f32[16,896]{1,0:T(8,128)S(1)}, u32[]{:S(2)}, u32[]{:S(2)}) collective-permute-start(f32[16,896]{1,0:T(8,128)S(1)} %add.35.refs_1_), channel_id=1, source_target_pairs={{0,17},{1,16},{2,19},{3,18},{4,21},{5,20},{6,23},{7,22},{8,25},{9,... | collective-permute-start | bytes 172040 | tf_op jit(solution)/shard_map/ppermute | solution.py:202
  42.9 5.1 %collective-permute-start.19 = (f32[16,896]{1,0:T(8,128)S(1)}, f32[16,896]{1,0:T(8,128)S(1)}, u32[]{:S(2)}, u32[]{:S(2)}) collective-permute-start(f32[16,896]{1,0:T(8,128)S(1)} %add.35.refs_1_), channel_id=1, source_target_pairs={{0,9},{1,8},{2,11},{3,10},{4,13},{5,12},{6,15},{7,14},{8,1},{9,0},... | collective-permute-start | bytes 172040 | tf_op jit(solution)/shard_map/ppermute | solution.py:202
  45.6 4.0 %collective-permute-start.12 = (f32[16,896]{1,0:T(8,128)S(1)}, f32[16,896]{1,0:T(8,128)S(1)}, u32[]{:S(2)}, u32[]{:S(2)}) collective-permute-start(f32[16,896]{1,0:T(8,128)S(1)} %add.33.refs_0_), channel_id=1, source_target_pairs={{0,9},{1,8},{2,11},{3,10},{4,13},{5,12},{6,15},{7,14},{8,1},{9,0},... | collective-permute-start | bytes 172040 | tf_op jit(solution)/shard_map/ppermute | solution.py:202
  45.7 4.5 %collective-permute-start.20 = (f32[16,896]{1,0:T(8,128)S(1)}, f32[16,896]{1,0:T(8,128)S(1)}, u32[]{:S(2)}, u32[]{:S(2)}) collective-permute-start(f32[16,896]{1,0:T(8,128)S(1)} %add.33.refs_0_), channel_id=1, source_target_pairs={{0,17},{1,16},{2,19},{3,18},{4,21},{5,20},{6,23},{7,22},{8,25},{9,... | collective-permute-start | bytes 172040 | tf_op jit(solution)/shard_map/ppermute | solution.py:202
  50.2 6.2 %collective-permute-start.21 = (f32[96,896]{1,0:T(8,128)S(1)}, f32[96,896]{1,0:T(8,128)S(1)}, u32[]{:S(2)}, u32[]{:S(2)}) collective-permute-start(f32[96,896]{1,0:T(8,128)S(1)} %shard_map.56.refs_0_), channel_id=1, source_target_pairs={{0,1},{1,0},{2,3},{3,2},{4,5},{5,4},{6,7},{7,6},{8,9},{9,8},{10,11... | collective-permute-start | bytes 1032200 | tf_op jit(solution)/shard_map/ppermute | solution.py:205
  50.4 3.6 %collective-permute-start.17 = (f32[16,896]{1,0:T(8,128)S(1)}, f32[16,896]{1,0:T(8,128)S(1)}, u32[]{:S(2)}, u32[]{:S(2)}) collective-permute-start(f32[16,896]{1,0:T(8,128)S(1)} %collective-permute-done.16.refs_5_), channel_id=1, source_target_pairs={{0,9},{1,8},{2,11},{3,10},{4,13},{5,12},{6,15},{7,14},{8,1},{9,0},... | collective-permute-start | bytes 172040 | tf_op jit(solution)/shard_map/ppermute | solution.py:202
  51.2 3.6 %collective-permute-start.13 = (f32[16,896]{1,0:T(8,128)S(1)}, f32[16,896]{1,0:T(8,128)S(1)}, u32[]{:S(2)}, u32[]{:S(2)}) collective-permute-start(f32[16,896]{1,0:T(8,128)S(1)} %collective-permute-done.12.refs_2_), channel_id=1, source_target_pairs={{0,17},{1,16},{2,19},{3,18},{4,21},{5,20},{6,23},{7,22},{8,25},{9,... | collective-permute-start | bytes 172040 | tf_op jit(solution)/shard_map/ppermute | solution.py:202
  54.9 2.7 %collective-permute-start.18 = (f32[32,896]{1,0:T(8,128)S(1)}, f32[32,896]{1,0:T(8,128)S(1)}, u32[]{:S(2)}, u32[]{:S(2)}) collective-permute-start(f32[32,896]{1,0:T(8,128)S(1)} %shard_map.55.refs_1_), channel_id=1, source_target_pairs={{0,1},{1,0},{2,3},{3,2},{4,5},{5,4},{6,7},{7,6},{8,9},{9,8},{10,11... | collective-permute-start | bytes 344072 | tf_op jit(solution)/shard_map/ppermute | solution.py:205

commit v9 on v8

--- a/solution.py
+++ b/solution.py
@@ -58,19 +58,25 @@
 
 
 def load_kernel(g, f, gv, fv, send, sems):
-    copies = [pltpu.make_async_copy(x, y, sems.at[i]) for i, (x, y) in enumerate(((g, gv), (f, fv)))]
-    for copy in copies:
-        copy.start()
-    for copy in copies:
-        copy.wait()
     width = send.shape[1]
     half = own_half()
+    copies = []
+    for side in range(2):
+        span = pl.ds(pl.multiple_of((half + 1 + side) % 2 * width, 128), width)
+        for i, (x, y) in enumerate(((g, gv), (f, fv))):
+            copies.append(pltpu.make_async_copy(x.at[:, span], y.at[:, span], sems.at[side, i]))
+            copies[-1].start()
+    for copy in copies[:2]:
+        copy.wait()
     for side in range(2):
 
         @pl.when(half == 1 - side)
         def _():
             span = slice(side * width, (side + 1) * width)
             send[...] = gv[:, span].astype(F32) + fv[:, span].astype(F32)
+
+    for copy in copies[2:]:
+        copy.wait()
 
 
 def left_kernel(g, f, b, left):
@@ -133,7 +139,11 @@
     total = terms[0][...]
     for term in terms[1:]:
         total = total + term[...]
-    both = jnp.dot(basis_t[...], total, precision=lax.Precision.HIGHEST, preferred_element_type=F32)
+    high, low = split(basis_t[...])
+    upper, lower = split(total)
+    left = jnp.concatenate([high, low, high], axis=1)
+    right = jnp.concatenate([upper, upper, lower], axis=0)
+    both = jnp.dot(left, right, preferred_element_type=F32)
     size = outs[0].shape[0]
     for i, out in enumerate(outs):
         out[...] = both[i * size : (i + 1) * size]
@@ -235,7 +245,7 @@
         load_kernel,
         [(g.shape, g.dtype), (f.shape, f.dtype), ((rows, half), F32)],
         *(pltpu.with_memory_space_constraint(x, pltpu.HBM) for x in (g, f)),
-        scratch=[pltpu.SemaphoreType.DMA((2,))], space=pltpu.HBM,
+        scratch=[pltpu.SemaphoreType.DMA((2, 2))], space=pltpu.HBM,
     )
     left = call(left_kernel, ((rank, rows), F32), g, f, b, flops=1 << 27)
     got = swap(send)

time: 58.6 us -> 58.5 us (level)
  no operation moved by 1% of the time
where the time goes in v9:
time: 58.5 us; the launch traced here: 58.4 us
  starting transfers between devices  29 us (50%)
  waiting for transfers between devices  21.2 us (36%)
  Pallas kernels  7.4 us (13%)
  between operations  0.74 us (1%)
    ppermute x18, starting transfers between devices, permute(): return lax.ppermute(value, AXES, pairs)  27.7 us
    ppermute x18, waiting for transfers between devices, permute(): return lax.ppermute(value, AXES, pairs)  20.1 us
    pallas_call x10, Pallas kernels, call(): pl.pallas_call(kernel, out_shape=shapes, in_specs=[pl.BlockSpec(memory_sp...  7.4 us
    ppermute x4, starting transfers between devices, swap(): return lax.ppermute(value, AXES, [(i, i ^ 1) for i in range(local * dp)])  1.3 us
  transfers between devices with their start and end apart: 22, of which 11 were waited for; matrix products, arithmetic and copies ran while one was open for 0% of the time, Pallas kernels for 8%

profile of v9, /device:TPU:0, one launch (start us, length us, event | category | flops | bytes accessed | tf_op | source)
XLA Modules:
  0.0 58.4 jit_solution(11818332480854201014)
XLA Ops:
  0.6 1.7 %shard_map.50 = (bf16[72,7168]{1,0:T(8,128)(2,1)S(1)}, bf16[72,7168]{1,0:T(8,128)(2,1)S(1)}, f32[72,3584]{1,0:T(8,128)S(1)}) custom-call(bf16[72,7168]{1,0:T(8,128)(2,1)} %bitcast.8, bf16[72,7168]{1,0:T(8,128)(2,1)} %bitcast.9), custom_call_target="tpu_custom_call" | custom-call | flops 1048576 | bytes 2064384 | tf_op jit(solution)/shard_map/pallas_call | solution.py:23
  2.3 0.6 collective-permute-start.6
  2.9 0.7 %shard_map.51 = f32[32,72]{1,0:T(8,128)S(1)} custom-call(bf16[72,7168]{1,0:T(8,128)(2,1)S(1)} %get-tuple-element.19.g, bf16[72,7168]{1,0:T(8,128)(2,1)S(1)} %get-tuple-element.20.f, f32[32,7168]{1,0:T(8,128)S(1)} %bitcast.5), custom_call_target="tpu_custom_call" | custom-call | flops 134217728 | bytes 2981888 | tf_op jit(solution)/shard_map/pallas_call | solution.py:23
  3.6 2.7 %collective-permute-start = (f32[32,72]{1,0:T(8,128)S(1)}, f32[32,72]{1,0:T(8,128)S(1)}, u32[]{:S(2)}, u32[]{:S(2)}) collective-permute-start(f32[32,72]{1,0:T(8,128)S(1)} %shard_map.51), channel_id=1, source_target_pairs={{0,3},{1,2},{2,1},{3,0},{4,7},{5,6},{6,5},{7,4},{8,11},{9,10},{10,... | collective-permute-start | bytes 27656 | tf_op jit(solution)/shard_map/ppermute | solution.py:212
  6.3 1.4 %collective-permute-done = f32[32,72]{1,0:T(8,128)S(1)} collective-permute-done((f32[32,72]{1,0:T(8,128)S(1)}, f32[32,72]{1,0:T(8,128)S(1)}, u32[]{:S(2)}, u32[]{:S(2)}) %collective-permute-start) | collective-permute-done | bytes 9248 | tf_op jit(solution)/shard_map/ppermute | solution.py:212
  7.7 0.1 collective-permute-start.1
  7.8 1.1 %collective-permute-done.1 = f32[32,72]{1,0:T(8,128)S(1)} collective-permute-done((f32[32,72]{1,0:T(8,128)S(1)}, f32[32,72]{1,0:T(8,128)S(1)}, u32[]{:S(2)}, u32[]{:S(2)}) %collective-permute-start.1) | collective-permute-done | bytes 9248 | tf_op jit(solution)/shard_map/ppermute | solution.py:215
  8.9 1.6 %collective-permute-start.2 = (f32[32,72]{1,0:T(8,128)S(1)}, f32[32,72]{1,0:T(8,128)S(1)}, u32[]{:S(2)}, u32[]{:S(2)}) collective-permute-start(f32[32,72]{1,0:T(8,128)S(1)} %add.28), channel_id=1, source_target_pairs={{0,9},{1,8},{2,11},{3,10},{4,13},{5,12},{6,15},{7,14},{8,1},{9,0},... | collective-permute-start | bytes 27656 | tf_op jit(solution)/shard_map/ppermute | solution.py:212
  10.6 0.0 collective-permute-done.6.got
  10.6 0.2 shard_map.53
  10.7 0.2 collective-permute-start.7
  10.9 1.7 %collective-permute-start.8 = (f32[72,896]{1,0:T(8,128)S(1)}, f32[72,896]{1,0:T(8,128)S(1)}, u32[]{:S(2)}, u32[]{:S(2)}) collective-permute-start(f32[72,896]{1,0:T(8,128)S(1)} %get-tuple-element.26), channel_id=1, source_target_pairs={{0,17},{1,16},{2,19},{3,18},{4,21},{5,20},{6,23},{7,22},{8,25},{9,... | collective-permute-start | bytes 774152 | tf_op jit(solution)/shard_map/ppermute | solution.py:212
  12.6 1.4 %collective-permute-start.9 = (f32[72,896]{1,0:T(8,128)S(1)}, f32[72,896]{1,0:T(8,128)S(1)}, u32[]{:S(2)}, u32[]{:S(2)}) collective-permute-start(f32[72,896]{1,0:T(8,128)S(1)} %get-tuple-element.27), channel_id=1, source_target_pairs={{0,24},{1,25},{2,26},{3,27},{4,28},{5,29},{6,30},{7,31},{8,16},{9,... | collective-permute-start | bytes 774152 | tf_op jit(solution)/shard_map/ppermute | solution.py:212
  14.0 1.0 %collective-permute-start.3 = (f32[32,72]{1,0:T(8,128)S(1)}, f32[32,72]{1,0:T(8,128)S(1)}, u32[]{:S(2)}, u32[]{:S(2)}) collective-permute-start(f32[32,72]{1,0:T(8,128)S(1)} %add.28), channel_id=1, source_target_pairs={{0,17},{1,16},{2,19},{3,18},{4,21},{5,20},{6,23},{7,22},{8,25},{9,... | collective-permute-start | bytes 27656 | tf_op jit(solution)/shard_map/ppermute | solution.py:212
  15.0 0.0 collective-permute-done.2
  15.0 0.4 collective-permute-start.4
  15.4 9.5 %collective-permute-done.3 = f32[32,72]{1,0:T(8,128)S(1)} collective-permute-done((f32[32,72]{1,0:T(8,128)S(1)}, f32[32,72]{1,0:T(8,128)S(1)}, u32[]{:S(2)}, u32[]{:S(2)}) %collective-permute-start.3) | collective-permute-done | bytes 9248 | tf_op jit(solution)/shard_map/ppermute | solution.py:212
  24.9 0.9 %collective-permute-done.4 = f32[32,72]{1,0:T(8,128)S(1)} collective-permute-done((f32[32,72]{1,0:T(8,128)S(1)}, f32[32,72]{1,0:T(8,128)S(1)}, u32[]{:S(2)}, u32[]{:S(2)}) %collective-permute-start.4) | collective-permute-done | bytes 9248 | tf_op jit(solution)/shard_map/ppermute | solution.py:212
  25.9 2.4 %collective-permute-start.5 = (f32[32,72]{1,0:T(8,128)S(1)}, f32[32,72]{1,0:T(8,128)S(1)}, u32[]{:S(2)}, u32[]{:S(2)}) collective-permute-start(f32[32,72]{1,0:T(8,128)S(1)} %add_add_fusion.a), channel_id=1, source_target_pairs={{0,5},{1,4},{2,7},{3,6},{4,1},{5,0},{6,3},{7,2},{8,13},{9,12},{10,... | collective-permute-start | bytes 27656 | tf_op jit(solution)/shard_map/ppermute | solution.py:212
  28.3 1.6 %collective-permute-done.5.b = f32[32,72]{1,0:T(8,128)S(1)} collective-permute-done((f32[32,72]{1,0:T(8,128)S(1)}, f32[32,72]{1,0:T(8,128)S(1)}, u32[]{:S(2)}, u32[]{:S(2)}) %collective-permute-start.5) | collective-permute-done | bytes 9248 | tf_op jit(solution)/shard_map/ppermute | solution.py:212
  29.9 1.5 %shard_map.52 = (f32[72,32]{1,0:T(8,128)S(1)}, f32[32,72]{1,0:T(8,128)S(1)}) custom-call(f32[32,72]{1,0:T(8,128)S(1)} %add_add_fusion.a, f32[32,72]{1,0:T(8,128)S(1)} %collective-permute-done.5.b), custom_call_target="tpu_custom_call" | custom-call | flops 67108864 | bytes 18432 | tf_op jit(solution)/shard_map/pallas_call | solution.py:23
  31.4 0.0 collective-permute-done.7.refs_1_
  31.4 0.0 collective-permute-done.8.refs_2_
  31.5 0.2 shard_map.54
  31.7 2.5 %collective-permute-start.14 = (f32[16,896]{1,0:T(8,128)S(1)}, f32[16,896]{1,0:T(8,128)S(1)}, u32[]{:S(2)}, u32[]{:S(2)}) collective-permute-start(f32[16,896]{1,0:T(8,128)S(1)} %get-tuple-element.29), channel_id=1, source_target_pairs={{0,5},{1,4},{2,7},{3,6},{4,1},{5,0},{6,3},{7,2},{8,13},{9,12},{10,... | collective-permute-start | bytes 172040 | tf_op jit(solution)/shard_map/ppermute | solution.py:212
  34.2 1.5 %collective-permute-start.10 = (f32[16,896]{1,0:T(8,128)S(1)}, f32[16,896]{1,0:T(8,128)S(1)}, u32[]{:S(2)}, u32[]{:S(2)}) collective-permute-start(f32[16,896]{1,0:T(8,128)S(1)} %get-tuple-element.28), channel_id=1, source_target_pairs={{0,3},{1,2},{2,1},{3,0},{4,7},{5,6},{6,5},{7,4},{8,11},{9,10},{10,... | collective-permute-start | bytes 172040 | tf_op jit(solution)/shard_map/ppermute | solution.py:212
  35.6 0.8 %collective-permute-done.14 = f32[16,896]{1,0:T(8,128)S(1)} collective-permute-done((f32[16,896]{1,0:T(8,128)S(1)}, f32[16,896]{1,0:T(8,128)S(1)}, u32[]{:S(2)}, u32[]{:S(2)}) %collective-permute-start.14) | collective-permute-done | bytes 57376 | tf_op jit(solution)/shard_map/ppermute | solution.py:212
  36.4 2.0 %collective-permute-start.15 = (f32[16,896]{1,0:T(8,128)S(1)}, f32[16,896]{1,0:T(8,128)S(1)}, u32[]{:S(2)}, u32[]{:S(2)}) collective-permute-start(f32[16,896]{1,0:T(8,128)S(1)} %add.34), channel_id=1, source_target_pairs={{0,3},{1,2},{2,1},{3,0},{4,7},{5,6},{6,5},{7,4},{8,11},{9,10},{10,... | collective-permute-start | bytes 172040 | tf_op jit(solution)/shard_map/ppermute | solution.py:212
  38.4 0.0 collective-permute-done.10
  38.4 3.5 %collective-permute-start.11 = (f32[16,896]{1,0:T(8,128)S(1)}, f32[16,896]{1,0:T(8,128)S(1)}, u32[]{:S(2)}, u32[]{:S(2)}) collective-permute-start(f32[16,896]{1,0:T(8,128)S(1)} %add.32), channel_id=1, source_target_pairs={{0,5},{1,4},{2,7},{3,6},{4,1},{5,0},{6,3},{7,2},{8,13},{9,12},{10,... | collective-permute-start | bytes 172040 | tf_op jit(solution)/shard_map/ppermute | solution.py:212
  41.9 0.0 collective-permute-done.15
  41.9 0.9 %collective-permute-start.16 = (f32[16,896]{1,0:T(8,128)S(1)}, f32[16,896]{1,0:T(8,128)S(1)}, u32[]{:S(2)}, u32[]{:S(2)}) collective-permute-start(f32[16,896]{1,0:T(8,128)S(1)} %add.35.refs_1_), channel_id=1, source_target_pairs={{0,17},{1,16},{2,19},{3,18},{4,21},{5,20},{6,23},{7,22},{8,25},{9,... | collective-permute-start | bytes 172040 | tf_op jit(solution)/shard_map/ppermute | solution.py:212
  42.8 1.6 %collective-permute-start.19 = (f32[16,896]{1,0:T(8,128)S(1)}, f32[16,896]{1,0:T(8,128)S(1)}, u32[]{:S(2)}, u32[]{:S(2)}) collective-permute-start(f32[16,896]{1,0:T(8,128)S(1)} %add.35.refs_1_), channel_id=1, source_target_pairs={{0,9},{1,8},{2,11},{3,10},{4,13},{5,12},{6,15},{7,14},{8,1},{9,0},... | collective-permute-start | bytes 172040 | tf_op jit(solution)/shard_map/ppermute | solution.py:212
  44.4 1.1 %collective-permute-done.11 = f32[16,896]{1,0:T(8,128)S(1)} collective-permute-done((f32[16,896]{1,0:T(8,128)S(1)}, f32[16,896]{1,0:T(8,128)S(1)}, u32[]{:S(2)}, u32[]{:S(2)}) %collective-permute-start.11) | collective-permute-done | bytes 57376 | tf_op jit(solution)/shard_map/ppermute | solution.py:212
  45.5 0.2 collective-permute-start.12
  45.6 2.3 %collective-permute-start.20 = (f32[16,896]{1,0:T(8,128)S(1)}, f32[16,896]{1,0:T(8,128)S(1)}, u32[]{:S(2)}, u32[]{:S(2)}) collective-permute-start(f32[16,896]{1,0:T(8,128)S(1)} %add.33.refs_0_), channel_id=1, source_target_pairs={{0,17},{1,16},{2,19},{3,18},{4,21},{5,20},{6,23},{7,22},{8,25},{9,... | collective-permute-start | bytes 172040 | tf_op jit(solution)/shard_map/ppermute | solution.py:212
  47.9 0.0 collective-permute-done.16.refs_5_
  47.9 1.5 %collective-permute-done.12.refs_2_ = f32[16,896]{1,0:T(8,128)S(1)} collective-permute-done((f32[16,896]{1,0:T(8,128)S(1)}, f32[16,896]{1,0:T(8,128)S(1)}, u32[]{:S(2)}, u32[]{:S(2)}) %collective-permute-start.12) | collective-permute-done | bytes 57376 | tf_op jit(solution)/shard_map/ppermute | solution.py:212
  49.4 0.7 %collective-permute-done.20.refs_4_ = f32[16,896]{1,0:T(8,128)S(1)} collective-permute-done((f32[16,896]{1,0:T(8,128)S(1)}, f32[16,896]{1,0:T(8,128)S(1)}, u32[]{:S(2)}, u32[]{:S(2)}) %collective-permute-start.20) | collective-permute-done | bytes 57376 | tf_op jit(solution)/shard_map/ppermute | solution.py:212
  50.1 0.2 collective-permute-start.21
  50.3 0.8 %collective-permute-start.17 = (f32[16,896]{1,0:T(8,128)S(1)}, f32[16,896]{1,0:T(8,128)S(1)}, u32[]{:S(2)}, u32[]{:S(2)}) collective-permute-start(f32[16,896]{1,0:T(8,128)S(1)} %collective-permute-done.16.refs_5_), channel_id=1, source_target_pairs={{0,9},{1,8},{2,11},{3,10},{4,13},{5,12},{6,15},{7,14},{8,1},{9,0},... | collective-permute-start | bytes 172040 | tf_op jit(solution)/shard_map/ppermute | solution.py:212
  51.1 1.1 %collective-permute-start.13 = (f32[16,896]{1,0:T(8,128)S(1)}, f32[16,896]{1,0:T(8,128)S(1)}, u32[]{:S(2)}, u32[]{:S(2)}) collective-permute-start(f32[16,896]{1,0:T(8,128)S(1)} %collective-permute-done.12.refs_2_), channel_id=1, source_target_pairs={{0,17},{1,16},{2,19},{3,18},{4,21},{5,20},{6,23},{7,22},{8,25},{9,... | collective-permute-start | bytes 172040 | tf_op jit(solution)/shard_map/ppermute | solution.py:212
  52.2 1.7 %collective-permute-done.17.refs_1_ = f32[16,896]{1,0:T(8,128)S(1)} collective-permute-done((f32[16,896]{1,0:T(8,128)S(1)}, f32[16,896]{1,0:T(8,128)S(1)}, u32[]{:S(2)}, u32[]{:S(2)}) %collective-permute-start.17) | collective-permute-done | bytes 57376 | tf_op jit(solution)/shard_map/ppermute | solution.py:212
  54.0 0.8 %collective-permute-done.13.refs_0_ = f32[16,896]{1,0:T(8,128)S(1)} collective-permute-done((f32[16,896]{1,0:T(8,128)S(1)}, f32[16,896]{1,0:T(8,128)S(1)}, u32[]{:S(2)}, u32[]{:S(2)}) %collective-permute-start.13) | collective-permute-done | bytes 57376 | tf_op jit(solution)/shard_map/ppermute | solution.py:212
  54.8 0.5 collective-permute-start.18
  55.2 1.0 %shard_map.57 = (bf16[72,7168]{1,0:T(8,128)(2,1)}, f32[32,7168]{1,0:T(8,128)}) custom-call(bf16[72,7168]{1,0:T(8,128)(2,1)S(1)} %get-tuple-element.19.g, bf16[72,7168]{1,0:T(8,128)(2,1)S(1)} %get-tuple-element.20.f, f32[72,32]{1,0:T(8,128)S(1)} %get-tuple-element.21.basis, f32[96,896]{1,0:T(8,128)S(1)} %shard_map.56.refs_0_), custom_call_target="tpu_custom_call" | custom-call | flops 134217728 | bytes 2417664 | tf_op jit(solution)/shard_map/pallas_call | solution.py:23
  56.3 1.1 %shard_map.58 = (bf16[72,7168]{1,0:T(8,128)(2,1)}, f32[32,7168]{1,0:T(8,128)}) custom-call(bf16[72,7168]{1,0:T(8,128)(2,1)S(1)} %get-tuple-element.19.g, bf16[72,7168]{1,0:T(8,128)(2,1)S(1)} %get-tuple-element.20.f, f32[72,32]{1,0:T(8,128)S(1)} %get-tuple-element.21.basis, ...), custom_call_target="tpu_custom_call", output_to_operand_aliasing={{0}: (5, {}), {1}: (6, {})} | custom-call | flops 134217728 | bytes 4482048 | tf_op jit(solution)/shard_map/pallas_call | solution.py:23
  57.4 0.9 %shard_map.59 = (bf16[72,7168]{1,0:T(8,128)(2,1)}, f32[32,7168]{1,0:T(8,128)}) custom-call(bf16[72,7168]{1,0:T(8,128)(2,1)S(1)} %get-tuple-element.19.g, bf16[72,7168]{1,0:T(8,128)(2,1)S(1)} %get-tuple-element.20.f, f32[72,32]{1,0:T(8,128)S(1)} %get-tuple-element.21.basis, ...), custom_call_target="tpu_custom_call", output_to_operand_aliasing={{0}: (4, {}), {1}: (5, {})} | custom-call | flops 134217728 | bytes 4137984 | tf_op jit(solution)/shard_map/pallas_call | solution.py:23
  (15 shorter events, 0.1 us)
Async XLA Ops:
  0.6 2.2 %copy-start = (f32[7168,32]{0,1:T(8,128)S(1)}, f32[7168,32]{0,1:T(8,128)}, u32[]{:S(2)}) copy-start(f32[7168,32]{0,1:T(8,128)} %param.5) | copy-start | bytes 2752516
  2.3 8.3 %collective-permute-start.6 = (f32[72,3584]{1,0:T(8,128)S(1)}, f32[72,3584]{1,0:T(8,128)S(1)}, u32[]{:S(2)}, u32[]{:S(2)}) collective-permute-start(f32[72,3584]{1,0:T(8,128)S(1)} %get-tuple-element.23), channel_id=1, source_target_pairs={{0,1},{1,0},{2,3},{3,2},{4,5},{5,4},{6,7},{7,6},{8,9},{9,8},{10,11... | collective-permute-start | bytes 3096584 | tf_op jit(solution)/shard_map/ppermute | solution.py:215
  3.6 4.1 %collective-permute-start = (f32[32,72]{1,0:T(8,128)S(1)}, f32[32,72]{1,0:T(8,128)S(1)}, u32[]{:S(2)}, u32[]{:S(2)}) collective-permute-start(f32[32,72]{1,0:T(8,128)S(1)} %shard_map.51), channel_id=1, source_target_pairs={{0,3},{1,2},{2,1},{3,0},{4,7},{5,6},{6,5},{7,4},{8,11},{9,10},{10,... | collective-permute-start | bytes 27656 | tf_op jit(solution)/shard_map/ppermute | solution.py:212
  7.7 1.2 %collective-permute-start.1 = (f32[32,72]{1,0:T(8,128)S(1)}, f32[32,72]{1,0:T(8,128)S(1)}, u32[]{:S(2)}, u32[]{:S(2)}) collective-permute-start(f32[32,72]{1,0:T(8,128)S(1)} %add.27), channel_id=1, source_target_pairs={{0,1},{1,0},{2,3},{3,2},{4,5},{5,4},{6,7},{7,6},{8,9},{9,8},{10,11... | collective-permute-start | bytes 27656 | tf_op jit(solution)/shard_map/ppermute | solution.py:215
  8.9 6.1 %collective-permute-start.2 = (f32[32,72]{1,0:T(8,128)S(1)}, f32[32,72]{1,0:T(8,128)S(1)}, u32[]{:S(2)}, u32[]{:S(2)}) collective-permute-start(f32[32,72]{1,0:T(8,128)S(1)} %add.28), channel_id=1, source_target_pairs={{0,9},{1,8},{2,11},{3,10},{4,13},{5,12},{6,15},{7,14},{8,1},{9,0},... | collective-permute-start | bytes 27656 | tf_op jit(solution)/shard_map/ppermute | solution.py:212
  10.7 20.7 %collective-permute-start.7 = (f32[72,896]{1,0:T(8,128)S(1)}, f32[72,896]{1,0:T(8,128)S(1)}, u32[]{:S(2)}, u32[]{:S(2)}) collective-permute-start(f32[72,896]{1,0:T(8,128)S(1)} %get-tuple-element.25), channel_id=1, source_target_pairs={{0,9},{1,8},{2,11},{3,10},{4,13},{5,12},{6,15},{7,14},{8,1},{9,0},... | collective-permute-start | bytes 774152 | tf_op jit(solution)/shard_map/ppermute | solution.py:212
  10.9 20.5 %collective-permute-start.8 = (f32[72,896]{1,0:T(8,128)S(1)}, f32[72,896]{1,0:T(8,128)S(1)}, u32[]{:S(2)}, u32[]{:S(2)}) collective-permute-start(f32[72,896]{1,0:T(8,128)S(1)} %get-tuple-element.26), channel_id=1, source_target_pairs={{0,17},{1,16},{2,19},{3,18},{4,21},{5,20},{6,23},{7,22},{8,25},{9,... | collective-permute-start | bytes 774152 | tf_op jit(solution)/shard_map/ppermute | solution.py:212
  12.6 18.9 %collective-permute-start.9 = (f32[72,896]{1,0:T(8,128)S(1)}, f32[72,896]{1,0:T(8,128)S(1)}, u32[]{:S(2)}, u32[]{:S(2)}) collective-permute-start(f32[72,896]{1,0:T(8,128)S(1)} %get-tuple-element.27), channel_id=1, source_target_pairs={{0,24},{1,25},{2,26},{3,27},{4,28},{5,29},{6,30},{7,31},{8,16},{9,... | collective-permute-start | bytes 774152 | tf_op jit(solution)/shard_map/ppermute | solution.py:212
  14.0 10.9 %collective-permute-start.3 = (f32[32,72]{1,0:T(8,128)S(1)}, f32[32,72]{1,0:T(8,128)S(1)}, u32[]{:S(2)}, u32[]{:S(2)}) collective-permute-start(f32[32,72]{1,0:T(8,128)S(1)} %add.28), channel_id=1, source_target_pairs={{0,17},{1,16},{2,19},{3,18},{4,21},{5,20},{6,23},{7,22},{8,25},{9,... | collective-permute-start | bytes 27656 | tf_op jit(solution)/shard_map/ppermute | solution.py:212
  15.0 10.8 %collective-permute-start.4 = (f32[32,72]{1,0:T(8,128)S(1)}, f32[32,72]{1,0:T(8,128)S(1)}, u32[]{:S(2)}, u32[]{:S(2)}) collective-permute-start(f32[32,72]{1,0:T(8,128)S(1)} %add.28), channel_id=1, source_target_pairs={{0,25},{1,24},{2,27},{3,26},{4,29},{5,28},{6,31},{7,30},{8,17},{9,... | collective-permute-start | bytes 27656 | tf_op jit(solution)/shard_map/ppermute | solution.py:212
  25.9 4.1 %collective-permute-start.5 = (f32[32,72]{1,0:T(8,128)S(1)}, f32[32,72]{1,0:T(8,128)S(1)}, u32[]{:S(2)}, u32[]{:S(2)}) collective-permute-start(f32[32,72]{1,0:T(8,128)S(1)} %add_add_fusion.a), channel_id=1, source_target_pairs={{0,5},{1,4},{2,7},{3,6},{4,1},{5,0},{6,3},{7,2},{8,13},{9,12},{10,... | collective-permute-start | bytes 27656 | tf_op jit(solution)/shard_map/ppermute | solution.py:212
  31.7 4.7 %collective-permute-start.14 = (f32[16,896]{1,0:T(8,128)S(1)}, f32[16,896]{1,0:T(8,128)S(1)}, u32[]{:S(2)}, u32[]{:S(2)}) collective-permute-start(f32[16,896]{1,0:T(8,128)S(1)} %get-tuple-element.29), channel_id=1, source_target_pairs={{0,5},{1,4},{2,7},{3,6},{4,1},{5,0},{6,3},{7,2},{8,13},{9,12},{10,... | collective-permute-start | bytes 172040 | tf_op jit(solution)/shard_map/ppermute | solution.py:212
  34.2 4.2 %collective-permute-start.10 = (f32[16,896]{1,0:T(8,128)S(1)}, f32[16,896]{1,0:T(8,128)S(1)}, u32[]{:S(2)}, u32[]{:S(2)}) collective-permute-start(f32[16,896]{1,0:T(8,128)S(1)} %get-tuple-element.28), channel_id=1, source_target_pairs={{0,3},{1,2},{2,1},{3,0},{4,7},{5,6},{6,5},{7,4},{8,11},{9,10},{10,... | collective-permute-start | bytes 172040 | tf_op jit(solution)/shard_map/ppermute | solution.py:212
  36.4 5.5 %collective-permute-start.15 = (f32[16,896]{1,0:T(8,128)S(1)}, f32[16,896]{1,0:T(8,128)S(1)}, u32[]{:S(2)}, u32[]{:S(2)}) collective-permute-start(f32[16,896]{1,0:T(8,128)S(1)} %add.34), channel_id=1, source_target_pairs={{0,3},{1,2},{2,1},{3,0},{4,7},{5,6},{6,5},{7,4},{8,11},{9,10},{10,... | collective-permute-start | bytes 172040 | tf_op jit(solution)/shard_map/ppermute | solution.py:212
  38.4 7.0 %collective-permute-start.11 = (f32[16,896]{1,0:T(8,128)S(1)}, f32[16,896]{1,0:T(8,128)S(1)}, u32[]{:S(2)}, u32[]{:S(2)}) collective-permute-start(f32[16,896]{1,0:T(8,128)S(1)} %add.32), channel_id=1, source_target_pairs={{0,5},{1,4},{2,7},{3,6},{4,1},{5,0},{6,3},{7,2},{8,13},{9,12},{10,... | collective-permute-start | bytes 172040 | tf_op jit(solution)/shard_map/ppermute | solution.py:212
  41.9 6.0 %collective-permute-start.16 = (f32[16,896]{1,0:T(8,128)S(1)}, f32[16,896]{1,0:T(8,128)S(1)}, u32[]{:S(2)}, u32[]{:S(2)}) collective-permute-start(f32[16,896]{1,0:T(8,128)S(1)} %add.35.refs_1_), channel_id=1, source_target_pairs={{0,17},{1,16},{2,19},{3,18},{4,21},{5,20},{6,23},{7,22},{8,25},{9,... | collective-permute-start | bytes 172040 | tf_op jit(solution)/shard_map/ppermute | solution.py:212
  42.8 5.1 %collective-permute-start.19 = (f32[16,896]{1,0:T(8,128)S(1)}, f32[16,896]{1,0:T(8,128)S(1)}, u32[]{:S(2)}, u32[]{:S(2)}) collective-permute-start(f32[16,896]{1,0:T(8,128)S(1)} %add.35.refs_1_), channel_id=1, source_target_pairs={{0,9},{1,8},{2,11},{3,10},{4,13},{5,12},{6,15},{7,14},{8,1},{9,0},... | collective-permute-start | bytes 172040 | tf_op jit(solution)/shard_map/ppermute | solution.py:212
  45.5 4.0 %collective-permute-start.12 = (f32[16,896]{1,0:T(8,128)S(1)}, f32[16,896]{1,0:T(8,128)S(1)}, u32[]{:S(2)}, u32[]{:S(2)}) collective-permute-start(f32[16,896]{1,0:T(8,128)S(1)} %add.33.refs_0_), channel_id=1, source_target_pairs={{0,9},{1,8},{2,11},{3,10},{4,13},{5,12},{6,15},{7,14},{8,1},{9,0},... | collective-permute-start | bytes 172040 | tf_op jit(solution)/shard_map/ppermute | solution.py:212
  45.6 4.5 %collective-permute-start.20 = (f32[16,896]{1,0:T(8,128)S(1)}, f32[16,896]{1,0:T(8,128)S(1)}, u32[]{:S(2)}, u32[]{:S(2)}) collective-permute-start(f32[16,896]{1,0:T(8,128)S(1)} %add.33.refs_0_), channel_id=1, source_target_pairs={{0,17},{1,16},{2,19},{3,18},{4,21},{5,20},{6,23},{7,22},{8,25},{9,... | collective-permute-start | bytes 172040 | tf_op jit(solution)/shard_map/ppermute | solution.py:212
  50.1 6.1 %collective-permute-start.21 = (f32[96,896]{1,0:T(8,128)S(1)}, f32[96,896]{1,0:T(8,128)S(1)}, u32[]{:S(2)}, u32[]{:S(2)}) collective-permute-start(f32[96,896]{1,0:T(8,128)S(1)} %shard_map.56.refs_0_), channel_id=1, source_target_pairs={{0,1},{1,0},{2,3},{3,2},{4,5},{5,4},{6,7},{7,6},{8,9},{9,8},{10,11... | collective-permute-start | bytes 1032200 | tf_op jit(solution)/shard_map/ppermute | solution.py:215
  50.3 3.6 %collective-permute-start.17 = (f32[16,896]{1,0:T(8,128)S(1)}, f32[16,896]{1,0:T(8,128)S(1)}, u32[]{:S(2)}, u32[]{:S(2)}) collective-permute-start(f32[16,896]{1,0:T(8,128)S(1)} %collective-permute-done.16.refs_5_), channel_id=1, source_target_pairs={{0,9},{1,8},{2,11},{3,10},{4,13},{5,12},{6,15},{7,14},{8,1},{9,0},... | collective-permute-start | bytes 172040 | tf_op jit(solution)/shard_map/ppermute | solution.py:212
  51.1 3.6 %collective-permute-start.13 = (f32[16,896]{1,0:T(8,128)S(1)}, f32[16,896]{1,0:T(8,128)S(1)}, u32[]{:S(2)}, u32[]{:S(2)}) collective-permute-start(f32[16,896]{1,0:T(8,128)S(1)} %collective-permute-done.12.refs_2_), channel_id=1, source_target_pairs={{0,17},{1,16},{2,19},{3,18},{4,21},{5,20},{6,23},{7,22},{8,25},{9,... | collective-permute-start | bytes 172040 | tf_op jit(solution)/shard_map/ppermute | solution.py:212
  54.8 2.7 %collective-permute-start.18 = (f32[32,896]{1,0:T(8,128)S(1)}, f32[32,896]{1,0:T(8,128)S(1)}, u32[]{:S(2)}, u32[]{:S(2)}) collective-permute-start(f32[32,896]{1,0:T(8,128)S(1)} %shard_map.55.refs_1_), channel_id=1, source_target_pairs={{0,1},{1,0},{2,3},{3,2},{4,5},{5,4},{6,7},{7,6},{8,9},{9,8},{10,11... | collective-permute-start | bytes 344072 | tf_op jit(solution)/shard_map/ppermute | solution.py:215
